TPU v7x, 32 devices: a whole 2x2x4 slice. The times are simulated.
32 devices in a mesh: ty: 4 (over y, x), tx: 8 (over z, core).
Axes of the slice: x: 2, y: 2, z: 4, core: 2. Of those that a mesh axis runs over, the one named last changes fastest.
Arguments:
- sky: bfloat16 [2048, 4096], P('ty', 'tx'), may hold values from -6 to 6
- point_count: int32 [4, 8], P('ty', 'tx'), may hold values from 0 to 4, as said below
- point_offset: int32 [4, 8, 4, 2], P('ty', 'tx'), may hold values from 0 to 511
- beam_width: bfloat16 [4, 8, 4], P('ty', 'tx'), may hold values from 128 to 340
- uv_bins: int32 [4, 8, 4, 2, 2], P('ty', 'tx'), may hold values from 0 to 7
- uv_count: int32 [4, 8, 4], P('ty', 'tx'), may hold values from 1 to 2
- uv_weight: bfloat16 [4, 8, 4, 2, 128, 128], P('ty', 'tx'), may hold values from 1 to 8
Outputs:
- curvature: float32 [2048, 4096], P('ty', 'tx')
Inputs may be any that keep to these rules, and one draw needn't show every extreme that they name: `point_count`: each tile holds at most 4 pointings, and the tiles of columns 2i and 2i + 1 of one row hold at most 4 together; in every draw some such pair holds exactly 4, all on one of its tiles. `point_offset`: entries of slots at or beyond a tile's count are ignored. `uv_bins`: entries of uv slots at or beyond a pointing's uv_count are ignored.
All inputs are finite; a program needn't handle non-finite values.
Results may differ from a plain program's by a relative error of at most 0.0085.
Values may be sent and summed in bfloat16 or wider, within the bound.
A program may use at most 128 MiB of HBM per device.

v0:
```python
import functools
import math

import jax
import jax.numpy as jnp
from jax import lax
from jax.experimental import pallas as pl
from jax.experimental.pallas import tpu as pltpu
from jax.sharding import PartitionSpec as P

F32 = jnp.float32
BF16 = jnp.bfloat16
CHUNK = 256
BANDS = 2
FINE = 32
MESH = pl.DeviceIdType.MESH


def small_tables(length, fine):
    pixels = jnp.arange(length, dtype=jnp.int32)
    rows = jnp.concatenate(
        [jnp.arange(fine, dtype=jnp.int32), fine * jnp.arange(length // fine, dtype=jnp.int32)]
    )
    phase = rows[:, None] * pixels[None, :] % length
    angle = phase.astype(F32) * (2.0 * math.pi / length)
    scale = jnp.where(jnp.arange(rows.shape[0]) < fine, 1.0 / math.sqrt(length), 1.0)[:, None]
    return jnp.cos(angle) * scale, jnp.sin(angle) * scale


def gaussians(start, decay, size, axis):
    shape = (size, 128) if axis == 0 else (8, size)
    index = lax.broadcasted_iota(jnp.int32, shape, axis)

    def value(pixel):
        away = (pixel - start - size).astype(F32)
        return jnp.exp(-(away * away) * decay)

    zero = jnp.zeros(shape, F32)
    low = jnp.where(index >= start, value(index), zero)
    high = jnp.where(index < start, value(index + 2 * size), zero)
    return low, value(index + size), high


def wide(column, width):
    return jnp.concatenate([column] * (width // 128), axis=1)


def beams(p, off_ref, decay_ref, gy_ref, gx_ref, size):
    decay = decay_ref[p]
    for part, values in enumerate(gaussians(off_ref[p, 0], decay, size, 0)):
        gy_ref[part] = values
    for part, values in enumerate(gaussians(off_ref[p, 1], decay, size, 1)):
        gx_ref[part] = values


def row_tables(p, bins_ref, which, cos_ref, sin_ref, rows_ref, block, slots_uv):
    for k in range(slots_uv):
        at = pl.ds(pl.multiple_of(bins_ref[p, 2 * k + which] * block, block), block)
        rows_ref[(2 * k) * block : (2 * k + 1) * block, :] = cos_ref[at, :]
        rows_ref[(2 * k + 1) * block : (2 * k + 2) * block, :] = sin_ref[at, :]


def flipped_tables(p, bins_ref, cos_ref, sin_ref, flip_ref, block, slots_uv):
    for k in range(slots_uv):
        at = pl.ds(pl.multiple_of(bins_ref[p, 2 * k] * block, block), block)
        flip_ref[:, (2 * k) * block : (2 * k + 1) * block] = cos_ref[:, at]
        flip_ref[:, (2 * k + 1) * block : (2 * k + 2) * block] = sin_ref[:, at]


class Around:
    def __init__(self):
        ty, tx = lax.axis_index("ty"), lax.axis_index("tx")
        ny, nx = lax.axis_size("ty"), lax.axis_size("tx")
        self.has = (ty > 0, ty < ny - 1, tx > 0, tx < nx - 1)
        self.to = ({"ty": ty - 1}, {"ty": ty + 1}, {"tx": tx - 1}, {"tx": tx + 1})

    def greet(self):
        barrier = pltpu.get_barrier_semaphore()
        for side in range(4):

            @pl.when(self.has[side])
            def _(side=side):
                pl.semaphore_signal(barrier, inc=1, device_id=self.to[side], device_id_type=MESH)

        pl.semaphore_wait(barrier, sum(has.astype(jnp.int32) for has in self.has))


UP, DOWN, LEFT, RIGHT = 0, 1, 2, 3
BACK = (DOWN, UP, RIGHT, LEFT)


def bands(size):
    step = size // BANDS
    return [slice(i * step, (i + 1) * step) for i in range(BANDS)]


def halo_kernel(
    cosines_ref, sines_ref, own_ref,
    ul_ref, l_ref, dl_ref, ur_ref, r_ref, dr_ref, cos_out, sin_out, up_ref, down_ref,
    zero_ref, cos_ref, sin_ref, y_send, y_recv, x_send, x_recv, out_sems, zero_sem,
):
    size = own_ref.shape[0]
    length = 2 * size
    fine = FINE
    around = Around()
    pieces = bands(size)
    landing = {LEFT: (ur_ref, r_ref, dr_ref), RIGHT: (ul_ref, l_ref, dl_ref)}

    def vertical(side, i):
        target = down_ref if side == UP else up_ref
        return pltpu.make_async_remote_copy(
            src_ref=own_ref.at[pieces[i]],
            dst_ref=target.at[pieces[i]],
            send_sem=y_send.at[side, i],
            recv_sem=y_recv.at[side, i],
            device_id=around.to[side],
            device_id_type=MESH,
        )

    def beside(side):
        return pltpu.make_async_remote_copy(
            src_ref=own_ref,
            dst_ref=landing[side][1],
            send_sem=x_send.at[side - LEFT, 2 * BANDS],
            recv_sem=x_recv.at[side - LEFT, 2 * BANDS],
            device_id=around.to[side],
            device_id_type=MESH,
        )

    def corner(side, which, i):
        source = up_ref if which == 0 else down_ref
        return pltpu.make_async_remote_copy(
            src_ref=source.at[pieces[i]],
            dst_ref=landing[side][2 * which].at[pieces[i]],
            send_sem=x_send.at[side - LEFT, which * BANDS + i],
            recv_sem=x_recv.at[side - LEFT, which * BANDS + i],
            device_id=around.to[side],
            device_id_type=MESH,
        )

    zero_ref[...] = jnp.zeros_like(zero_ref)
    around.greet()
    for i in range(BANDS):
        for side in (UP, DOWN):

            @pl.when(around.has[side])
            def _(side=side, i=i):
                vertical(side, i).start()

    for side in (LEFT, RIGHT):

        @pl.when(around.has[side])
        def _(side=side):
            beside(side).start()

        @pl.when(jnp.logical_not(around.has[side]))
        def _(side=side):
            for target in landing[BACK[side]]:
                fill = pltpu.make_async_copy(zero_ref, target, zero_sem)
                fill.start()
                fill.wait()

    for side, target in ((UP, up_ref), (DOWN, down_ref)):

        @pl.when(jnp.logical_not(around.has[side]))
        def _(target=target):
            target[...] = jnp.zeros_like(target)

    def table(j, carry):
        c, s = cosines_ref[pl.ds(fine + j, 1), :], sines_ref[pl.ds(fine + j, 1), :]
        fc, fs = cosines_ref[:fine, :], sines_ref[:fine, :]
        at = pl.ds(pl.multiple_of(j * fine, fine), fine)
        cos_ref[at, :] = (fc * c - fs * s).astype(BF16)
        sin_ref[at, :] = (fs * c + fc * s).astype(BF16)
        return carry

    lax.fori_loop(0, length // fine, table, 0)

    for i in range(BANDS):
        for which, side in ((0, UP), (1, DOWN)):

            @pl.when(around.has[side])
            def _(side=side, i=i):
                vertical(BACK[side], i).wait_recv()

            for beyond in (LEFT, RIGHT):

                @pl.when(around.has[beyond])
                def _(beyond=beyond, which=which, i=i):
                    corner(beyond, which, i).start()

    cos_copy = pltpu.make_async_copy(cos_ref, cos_out, out_sems.at[0])
    sin_copy = pltpu.make_async_copy(sin_ref, sin_out, out_sems.at[1])
    cos_copy.start()
    sin_copy.start()
    for side in (UP, DOWN):

        @pl.when(around.has[side])
        def _(side=side):
            for i in range(BANDS):
                vertical(side, i).wait_send()

    for side in (LEFT, RIGHT):

        @pl.when(around.has[side])
        def _(side=side):
            beside(side).wait_send()
            beside(BACK[side]).wait_recv()
            for which in range(2):
                for i in range(BANDS):
                    corner(side, which, i).wait_send()
                    corner(BACK[side], which, i).wait_recv()

    cos_copy.wait()
    sin_copy.wait()


def early_kernel(
    count_ref, off_ref, bins_ref, decay_ref, cos_ref, sin_ref, up_ref, own_ref, down_ref,
    first_ref, gy_ref, gx_ref, rows_ref, beamed_ref,
):
    size = own_ref.shape[0]
    block = rows_ref.shape[0] // bins_ref.shape[1]
    slots_uv = bins_ref.shape[1] // 2

    def step(p, carry):
        beams(p, off_ref, decay_ref, gy_ref, gx_ref, size)
        row_tables(p, bins_ref, 0, cos_ref, sin_ref, rows_ref, block, slots_uv)
        for at in range(0, size, CHUNK):
            cols = slice(at, at + CHUNK)
            gx = gx_ref[1, 0:1, cols]
            top = wide(gy_ref[0], CHUNK) * up_ref[:, cols].astype(F32)
            top = top + wide(gy_ref[2], CHUNK) * down_ref[:, cols].astype(F32)
            beamed_ref[:size, cols] = (gx * top).astype(BF16)
            low = wide(gy_ref[1], CHUNK) * own_ref[:, cols].astype(F32)
            beamed_ref[size:, cols] = (gx * low).astype(BF16)
        for at in range(0, size, CHUNK):
            cols = slice(at, at + CHUNK)
            first_ref[p, :, cols] = jnp.dot(
                rows_ref[...], beamed_ref[:, cols], preferred_element_type=F32
            ).astype(BF16)
        return carry

    lax.fori_loop(0, count_ref[0], step, 0)


def middle_kernel(
    count_ref, off_ref, bins_ref, used_ref, decay_ref, cos_ref, sin_ref, weight_ref, early_ref,
    ul_ref, l_ref, dl_ref, ur_ref, r_ref, dr_ref,
    oul_ref, ol_ref, odl_ref, our_ref, or_ref, odr_ref, late_ref,
    gy_ref, gx_ref, rows_ref, cols_ref, flip_ref, beamed_ref, first_ref, spread_ref, acc_ref,
):
    size = l_ref.shape[0]
    block = rows_ref.shape[0] // bins_ref.shape[1]
    slots_uv = bins_ref.shape[1] // 2
    pair = 2 * block
    acc_ref[...] = jnp.zeros_like(acc_ref)

    def step(p, carry):
        beams(p, off_ref, decay_ref, gy_ref, gx_ref, size)
        row_tables(p, bins_ref, 0, cos_ref, sin_ref, rows_ref, block, slots_uv)
        row_tables(p, bins_ref, 1, cos_ref, sin_ref, cols_ref, block, slots_uv)
        flipped_tables(p, bins_ref, cos_ref, sin_ref, flip_ref, block, slots_uv)
        for at in range(0, size, CHUNK):
            cols = slice(at, at + CHUNK)
            gl = gx_ref[0, 0:1, cols]
            gr = gx_ref[2, 0:1, cols]
            gu = wide(gy_ref[0], CHUNK)
            gd = wide(gy_ref[2], CHUNK)
            left = gu * ul_ref[:, cols].astype(F32) + gd * dl_ref[:, cols].astype(F32)
            right = gu * ur_ref[:, cols].astype(F32) + gd * dr_ref[:, cols].astype(F32)
            beamed_ref[:size, cols] = (gl * left + gr * right).astype(BF16)
            low = gl * l_ref[:, cols].astype(F32) + gr * r_ref[:, cols].astype(F32)
            beamed_ref[size:, cols] = (wide(gy_ref[1], CHUNK) * low).astype(BF16)
        first_ref[:, size:] = early_ref[p]
        for at in range(0, size, CHUNK):
            cols = slice(at, at + CHUNK)
            first_ref[:, cols] = jnp.dot(
                rows_ref[...], beamed_ref[:, cols], preferred_element_type=F32
            ).astype(BF16)
        for k in range(slots_uv):
            rows = slice(k * pair, (k + 1) * pair)
            table = cols_ref[rows, :]
            both = lax.dot_general(
                first_ref[rows, :], table, (((1,), (1,)), ((), ())), preferred_element_type=F32
            )
            used = jnp.where(k < used_ref[p], 1.0, 0.0).astype(F32)
            weight = weight_ref[p, k].astype(F32) * used
            real = ((both[:block, :block] - both[block:, block:]) * weight).astype(BF16)
            turned = ((both[:block, block:] + both[block:, :block]) * weight).astype(BF16)
            scaled = jnp.concatenate(
                [
                    jnp.concatenate([real, turned], axis=1),
                    jnp.concatenate([turned, -real], axis=1),
                ],
                axis=0,
            )
            spread_ref[rows, :] = jnp.dot(scaled, table, preferred_element_type=F32).astype(BF16)
        late_ref[p] = spread_ref[:, size:]
        for at in range(0, size, CHUNK):
            cols = slice(at, at + CHUNK)
            gl = gx_ref[0, 0:1, cols]
            gr = gx_ref[2, 0:1, cols]
            top = jnp.dot(flip_ref[:size, :], spread_ref[:, cols], preferred_element_type=F32)
            up = wide(gy_ref[0], CHUNK) * top
            down = wide(gy_ref[2], CHUNK) * top
            acc_ref[0, :, cols] += gl * up
            acc_ref[2, :, cols] += gl * down
            acc_ref[3, :, cols] += gr * up
            acc_ref[5, :, cols] += gr * down
            low = jnp.dot(flip_ref[size:, :], spread_ref[:, cols], preferred_element_type=F32)
            low = wide(gy_ref[1], CHUNK) * low
            acc_ref[1, :, cols] += gl * low
            acc_ref[4, :, cols] += gr * low
        return carry

    def idle(p, carry):
        late_ref[p] = jnp.zeros(late_ref.shape[1:], BF16)
        return carry

    lax.fori_loop(0, count_ref[0], step, 0)
    lax.fori_loop(count_ref[0], late_ref.shape[0], idle, 0)
    for part, out_ref in enumerate((oul_ref, ol_ref, odl_ref, our_ref, or_ref, odr_ref)):
        out_ref[...] = acc_ref[part].astype(BF16)


def late_kernel(
    count_ref, off_ref, bins_ref, decay_ref, cos_ref, sin_ref, late_ref,
    up_ref, own_ref, down_ref, gy_ref, gx_ref, flip_ref,
):
    size = own_ref.shape[0]
    block = flip_ref.shape[1] // bins_ref.shape[1]
    slots_uv = bins_ref.shape[1] // 2
    for out_ref in (up_ref, own_ref, down_ref):
        out_ref[...] = jnp.zeros_like(out_ref)

    def step(p, carry):
        beams(p, off_ref, decay_ref, gy_ref, gx_ref, size)
        flipped_tables(p, bins_ref, cos_ref, sin_ref, flip_ref, block, slots_uv)
        for at in range(0, size, CHUNK):
            cols = slice(at, at + CHUNK)
            gx = gx_ref[1, 0:1, cols]
            part = late_ref[p, :, cols]
            top = gx * jnp.dot(flip_ref[:size, :], part, preferred_element_type=F32)
            up_ref[:, cols] += wide(gy_ref[0], CHUNK) * top
            down_ref[:, cols] += wide(gy_ref[2], CHUNK) * top
            low = gx * jnp.dot(flip_ref[size:, :], part, preferred_element_type=F32)
            own_ref[:, cols] += wide(gy_ref[1], CHUNK) * low
        return carry

    lax.fori_loop(0, count_ref[0], step, 0)


def sum_kernel(
    ul_ref, l_ref, dl_ref, ur_ref, r_ref, dr_ref, up_ref, mid_ref, down_ref,
    own_ref, above_ref, below_ref, got_ref, going_ref,
    y_send, y_recv, x_send, x_recv,
):
    size = own_ref.shape[0]
    around = Around()
    pieces = bands(size)
    leaving = {LEFT: (ul_ref, l_ref, dl_ref), RIGHT: (ur_ref, r_ref, dr_ref)}

    def corner(side, which, i):
        return pltpu.make_async_remote_copy(
            src_ref=leaving[side][2 * which].at[pieces[i]],
            dst_ref=got_ref.at[side - LEFT, 2 * which, pieces[i]],
            send_sem=x_send.at[side - LEFT, which * BANDS + i],
            recv_sem=x_recv.at[side - LEFT, which * BANDS + i],
            device_id=around.to[side],
            device_id_type=MESH,
        )

    def beside(side):
        return pltpu.make_async_remote_copy(
            src_ref=leaving[side][1],
            dst_ref=got_ref.at[side - LEFT, 1],
            send_sem=x_send.at[side - LEFT, 2 * BANDS],
            recv_sem=x_recv.at[side - LEFT, 2 * BANDS],
            device_id=around.to[side],
            device_id_type=MESH,
        )

    def vertical(side, i):
        target = below_ref if side == UP else above_ref
        return pltpu.make_async_remote_copy(
            src_ref=going_ref.at[side, pieces[i]],
            dst_ref=target.at[pieces[i]],
            send_sem=y_send.at[side, i],
            recv_sem=y_recv.at[side, i],
            device_id=around.to[side],
            device_id_type=MESH,
        )

    around.greet()
    for i in range(BANDS):
        for which in range(2):
            for side in (LEFT, RIGHT):

                @pl.when(around.has[side])
                def _(side=side, which=which, i=i):
                    corner(side, which, i).start()

    for side in (LEFT, RIGHT):

        @pl.when(around.has[side])
        def _(side=side):
            beside(side).start()

        @pl.when(jnp.logical_not(around.has[side]))
        def _(side=side):
            got_ref[BACK[side] - LEFT] = jnp.zeros(got_ref.shape[1:], BF16)

    for side, target in ((UP, above_ref), (DOWN, below_ref)):

        @pl.when(jnp.logical_not(around.has[side]))
        def _(target=target):
            target[...] = jnp.zeros_like(target)

    for i in range(BANDS):
        for which, part_ref in ((0, up_ref), (1, down_ref)):
            for side in (LEFT, RIGHT):

                @pl.when(around.has[side])
                def _(side=side, which=which, i=i):
                    corner(BACK[side], which, i).wait_recv()

            total = part_ref[pieces[i], :]
            for back in range(2):
                total = total + got_ref[back, 2 * which, pieces[i], :].astype(F32)
            going_ref[which, pieces[i], :] = total.astype(BF16)
        for side in (UP, DOWN):

            @pl.when(around.has[side])
            def _(side=side, i=i):
                vertical(side, i).start()

    for side in (LEFT, RIGHT):

        @pl.when(around.has[side])
        def _(side=side):
            beside(BACK[side]).wait_recv()

    own_ref[...] = mid_ref[...] + got_ref[0, 1].astype(F32) + got_ref[1, 1].astype(F32)
    for side in (LEFT, RIGHT):

        @pl.when(around.has[side])
        def _(side=side):
            beside(side).wait_send()
            for which in range(2):
                for i in range(BANDS):
                    corner(side, which, i).wait_send()

    for side in (UP, DOWN):

        @pl.when(around.has[side])
        def _(side=side):
            for i in range(BANDS):
                vertical(side, i).wait_send()
                vertical(BACK[side], i).wait_recv()


def remote_call(kernel, ident, scalars, anys, vectors, outs, spaces, scratch):
    return pl.pallas_call(
        kernel,
        out_shape=outs,
        in_specs=[pl.BlockSpec(memory_space=pltpu.SMEM)] * len(scalars)
        + [pl.BlockSpec(memory_space=pl.ANY)] * len(anys)
        + [pl.BlockSpec(memory_space=pltpu.VMEM)] * len(vectors),
        out_specs=tuple(pl.BlockSpec(memory_space=space) for space in spaces),
        scratch_shapes=scratch,
        compiler_params=pltpu.CompilerParams(
            vmem_limit_bytes=56 * 1024 * 1024, collective_id=ident, has_side_effects=True
        ),
    )(*scalars, *anys, *vectors)


def local_call(kernel, scalars, vectors, outs, scratch, flops):
    return pl.pallas_call(
        kernel,
        out_shape=outs,
        in_specs=[pl.BlockSpec(memory_space=pltpu.SMEM)] * len(scalars)
        + [pl.BlockSpec(memory_space=pltpu.VMEM)] * len(vectors),
        out_specs=jax.tree.map(lambda _: pl.BlockSpec(memory_space=pltpu.VMEM), outs),
        scratch_shapes=scratch,
        compiler_params=pltpu.CompilerParams(vmem_limit_bytes=56 * 1024 * 1024),
        cost_estimate=pl.CostEstimate(flops=flops, bytes_accessed=8 << 20, transcendentals=0),
    )(*scalars, *vectors)


def shards(sky, point_count, point_offset, beam_width, uv_bins, uv_count, uv_weight):
    size = sky.shape[0]
    length = 2 * size
    slots, slots_uv, block = uv_weight.shape[2], uv_weight.shape[3], uv_weight.shape[4]
    depth = 2 * slots_uv * block
    cosines, sines = small_tables(length, FINE)
    count = point_count.reshape(1)
    offset = point_offset.reshape(slots, 2)
    bins = jnp.clip(uv_bins.reshape(slots, 2 * slots_uv), 0, length // block - 1)
    used = uv_count.reshape(slots)
    width = beam_width.reshape(slots).astype(F32)
    decay = 1.0 / (2.0 * width * width)
    weight = uv_weight.reshape(slots, slots_uv, block, block)

    gy = pltpu.VMEM((3, size, 128), F32)
    gx = pltpu.VMEM((3, 8, size), F32)
    rows = pltpu.VMEM((depth, length), BF16)
    flip = pltpu.VMEM((length, depth), BF16)
    beamed = pltpu.VMEM((length, size), BF16)
    half = jax.ShapeDtypeStruct((slots, depth, size), BF16)
    sent = jax.ShapeDtypeStruct((size, size), BF16)
    kept = jax.ShapeDtypeStruct((size, size), F32)
    flops = 2 * slots * depth * length * size

    dma = pltpu.SemaphoreType.DMA
    tile = pltpu.VMEM((size, size), BF16)
    table = pltpu.VMEM((length, length), BF16)
    sems = [dma((2, BANDS))] * 2 + [dma((2, 2 * BANDS + 1))] * 2
    full = jax.ShapeDtypeStruct((length, length), BF16)
    up_left, left, down_left, up_right, right, down_right, cos, sin, up, down = remote_call(
        halo_kernel,
        0,
        (),
        (),
        (cosines, sines, sky),
        (sent,) * 6 + (full, full, sent, sent),
        (pl.ANY,) * 8 + (pltpu.VMEM,) * 2,
        [tile, table, table] + sems + [dma((2,)), dma],
    )
    early = local_call(
        early_kernel,
        (count, offset, bins, decay),
        (cos, sin, up, sky, down),
        half,
        [gy, gx, rows, beamed],
        flops,
    )
    to_ul, to_l, to_dl, to_ur, to_r, to_dr, late = local_call(
        middle_kernel,
        (count, offset, bins, used, decay),
        (cos, sin, weight, early, up_left, left, down_left, up_right, right, down_right),
        (sent,) * 6 + (half,),
        [
            gy, gx, rows, rows, flip, beamed,
            pltpu.VMEM((depth, length), BF16),
            pltpu.VMEM((depth, length), BF16),
            pltpu.VMEM((6, size, size), F32),
        ],
        3 * flops,
    )
    to_up, own, to_down = local_call(
        late_kernel,
        (count, offset, bins, decay),
        (cos, sin, late),
        (kept,) * 3,
        [gy, gx, flip],
        flops,
    )
    own, above, below = remote_call(
        sum_kernel,
        1,
        (),
        (to_ul, to_l, to_dl, to_ur, to_r, to_dr),
        (to_up, own, to_down),
        (kept, sent, sent),
        (pltpu.VMEM,) * 3,
        [pltpu.VMEM((2, 3, size, size), BF16), pltpu.VMEM((2, size, size), BF16)] + sems,
    )
    return own + above.astype(F32) + below.astype(F32)


def solution(mesh):
    in_specs = (
        P("ty", "tx"),
        P("ty", "tx"),
        P("ty", "tx", None, None),
        P("ty", "tx", None),
        P("ty", "tx", None, None, None),
        P("ty", "tx", None),
        P("ty", "tx", None, None, None, None),
    )
    out_specs = P("ty", "tx")
    return jax.shard_map(shards, mesh=mesh, in_specs=in_specs, out_specs=out_specs, check_vma=False)
```

profile of v0, /device:TPU:13, one launch (start us, length us, event | category | flops | bytes accessed | tf_op | source)
XLA Modules:
  0.0 112.8 jit_solution(16144992812360130883)
XLA Ops:
  0.7 1.2 %fusion.6.decay_ref = f32[4]{0:T(128)} fusion(bf16[1,1,4]{2,1,0:T(2,128)(2,1)} %param.10), kind=kLoop, calls=%fused_computation.15 | loop fusion | flops 16 | bytes 24 | tf_op jit(solution)/shard_map/div | solution.py:502
  1.9 0.1 pad_add_fusion
  1.9 1.3 %copy.10.off_ref = s32[4,2]{1,0:T(4,128)} copy(s32[4,2]{0,1:T(2,128)} %bitcast.12) | data formatting | bytes 64 | tf_op jit(solution)/shard_map/reshape | solution.py:498
  3.3 0.7 broadcast_clamp_fusion
  4.0 0.7 copy.11.bins_ref
  4.6 1.9 %sine_multiply_fusion = (f32[64,1024]{1,0:T(8,128)}, f32[64,1024]{1,0:T(8,128)}) fusion(f32[64]{0:T(128)S(1)} %compare_select_fusion, s32[64]{0:T(128)S(1)} %pad_add_fusion), kind=kLoop, calls=%fused_computation.7 | loop fusion | flops 1048576 | bytes 524800 | tf_op jit(solution)/shard_map/mul | solution.py:27
  6.6 37.8 %shard_map.73 = (bf16[512,512]{1,0:T(8,128)(2,1)}, bf16[512,512]{1,0:T(8,128)(2,1)}, bf16[512,512]{1,0:T(8,128)(2,1)}, bf16[512,512]{1,0:T(8,128)(2,1)}, bf16[51...) custom-call(f32[64,1024]{1,0:T(8,128)} %get-tuple-element.52.cosines, ...), custom_call_target="tpu_custom_call" | custom-call | tf_op jit(solution)/shard_map/pallas_call | solution.py:464
  44.3 6.2 %shard_map.74.early_ref = bf16[4,512,512]{2,1,0:T(8,128)(2,1)} custom-call(s32[1]{0:T(128)} %bitcast.8.count_ref, s32[4,2]{1,0:T(4,128)} %copy.10.off_ref, s32[4,4]{1,0:T(4,128)} %copy.11.bins_ref, f32[4]{0:T(128)} %fusion.6.decay_ref, bf16[1024,1024]{1,0:T(8,128)(2,1)} %get-tuple-element.28.cos_ref, bf16[1024,1024]{1,0:T(8,128)(2,1)} %get-tuple-element.29.sin_ref, ...), custom_call_target="tpu_custom_call" | custom-call | flops 2147483648 | bytes 8388608 | tf_op jit(solution)/shard_map/pallas_call | solution.py:479
  50.5 13.1 %shard_map.75 = (bf16[512,512]{1,0:T(8,128)(2,1)}, bf16[512,512]{1,0:T(8,128)(2,1)}, bf16[512,512]{1,0:T(8,128)(2,1)}, bf16[512,512]{1,0:T(8,128)(2,1)}, bf16[51...) custom-call(s32[1]{0:T(128)} %bitcast.9.count_ref, s32[4,2]{1,0:T(4,128)} %copy.10.off_ref, ...), custom_call_target="tpu_custom_call" | custom-call | flops 6442450944 | bytes 8388608 | tf_op jit(solution)/shard_map/pallas_call | solution.py:479
  63.6 6.9 %shard_map.76 = (f32[512,512]{1,0:T(8,128)}, f32[512,512]{1,0:T(8,128)}, f32[512,512]{1,0:T(8,128)}) custom-call(s32[1]{0:T(128)} %bitcast.10.count_ref, s32[4,2]{1,0:T(4,128)} %copy.10.off_ref, s32[4,4]{1,0:T(4,128)} %copy.11.bins_ref, f32[4]{0:T(128)} %fusion.6.decay_ref, bf16[1024,1024]{1,0:T(8,128)(2,1)} %get-tuple-element.28.cos_ref, ...), custom_call_target="tpu_custom_call" | custom-call | flops 2147483648 | bytes 8388608 | tf_op jit(solution)/shard_map/pallas_call | solution.py:479
  70.5 39.6 %shard_map.77 = (f32[512,512]{1,0:T(8,128)}, bf16[512,512]{1,0:T(8,128)(2,1)}, bf16[512,512]{1,0:T(8,128)(2,1)}) custom-call(bf16[512,512]{1,0:T(8,128)(2,1)} %get-tuple-element.38.ul_ref, bf16[512,512]{1,0:T(8,128)(2,1)} %get-tuple-element.39.l_ref, bf16[512,512]{1,0:T(8,128)(2,1)} %get-tuple-element.40.dl_ref, bf16[512,512]{1,0:T(8,128)(2,1)} %get-tuple-element.41.ur_ref, ...), custom_call_target="tpu_custom_call" | custom-call | tf_op jit(solution)/shard_map/pallas_call | solution.py:464
  110.1 2.7 %convert_add_fusion = f32[512,512]{1,0:T(8,128)} fusion(bf16[512,512]{1,0:T(8,128)(2,1)} %get-tuple-element.50, f32[512,512]{1,0:T(8,128)} %get-tuple-element.48, bf16[512,512]{1,0:T(8,128)(2,1)} %get-tuple-element.49), kind=kLoop, calls=%fused_computation | loop fusion | flops 1048576 | bytes 3145728 | tf_op jit(solution)/shard_map/add | solution.py:569
  (3 shorter events, 0.0 us)
where the time goes:
time: 115 us; the launch traced here: 113 us
  Pallas kernels  103 us (90%)
  other arithmetic  6.58 us (6%)
  local copies, waits for them, and re-layouts  2.02 us (2%)
    pallas_call x2, Pallas kernels, remote_call(): pl.pallas_call(kernel, out_shape=outs, in_specs=[pl.BlockSpec(memory_spac...  77.4 us
    pallas_call x3, Pallas kernels, local_call(): pl.pallas_call(kernel, out_shape=outs, in_specs=[pl.BlockSpec(memory_spac...  26.1 us
    add x1, other arithmetic, shards(): return own + above.astype(F32) + below.astype(F32)  2.7 us

commit v1 on v0

v1 whole, which is shorter than its diff:
```python
import functools
import math

import jax
import jax.numpy as jnp
import numpy as np
from jax import lax
from jax.experimental import pallas as pl
from jax.experimental.pallas import tpu as pltpu
from jax.sharding import PartitionSpec as P

F32 = jnp.float32
BF16 = jnp.bfloat16
I32 = jnp.int32
FINE = 32
CHUNK = 256
FIELDS = 8
MESH = pl.DeviceIdType.MESH


def seed_tables(length, fine):
    pixels = np.arange(length, dtype=np.int64)
    rows = np.concatenate([np.arange(fine), fine * np.arange(length // fine)])
    angle = (rows[:, None] * pixels[None, :] % length) * (2.0 * math.pi / length)
    scale = np.where(np.arange(rows.shape[0]) < fine, 1.0 / math.sqrt(length), 1.0)[:, None]
    return (np.cos(angle) * scale).astype(np.float32), (np.sin(angle) * scale).astype(np.float32)


def wide(column, width):
    return jnp.concatenate([column] * (width // column.shape[1]), axis=1)


def kernel(
    meta_ref, cosines_ref, sines_ref, sky_ref, weight_ref, out_ref,
    meta_got, meta_all, outer_ref, inner_ref, weight_got, row_tab, flip_tab, col_tab,
    rows_ref, flip_ref, cols_ref, beamed_ref, first_ref, spread_ref, gx_ref, gy_ref,
    part_send, part_mine, part_got, vis_own, vis_send, vis_got,
    scaled_own, scaled_par, acc_outer, acc_inner, edge_send, edge_got, inner_got,
    meta_sems, sky_sems, weight_sems, part_sems, vis_sems, scaled_sems, par_sems, last_sems,
):
    size = sky_ref.shape[0]
    length = 2 * size
    slots, slots_uv, block = weight_ref.shape[0], weight_ref.shape[1], weight_ref.shape[2]
    half_slots = slots // 2
    ty, tx = lax.axis_index("ty"), lax.axis_index("tx")
    ny, nx = lax.axis_size("ty"), lax.axis_size("tx")
    core = tx % 2
    partner = tx + 1 - 2 * core
    beyond = tx - 1 + 2 * core
    has_up, has_down = ty > 0, ty < ny - 1
    has_beyond = jnp.logical_and(beyond >= 0, beyond < nx)
    has_row = (has_up, has_down)
    row_half = pl.multiple_of((ty % 2) * size, size)
    col_half = pl.multiple_of((1 - core) * size, size)
    to_partner = {"tx": partner}
    to_beyond = {"tx": beyond}
    to_row = ({"ty": ty - 1}, {"ty": ty + 1})
    to_cross = ({"ty": ty - 1, "tx": partner}, {"ty": ty + 1, "tx": partner})

    def remote(src, dst, sems, at, target):
        return pltpu.make_async_remote_copy(
            src_ref=src,
            dst_ref=dst,
            send_sem=sems.at[(0,) + at],
            recv_sem=sems.at[(1,) + at],
            device_id=target,
            device_id_type=MESH,
        )

    def meta_copy(slot, target):
        return remote(meta_ref, meta_got[slot], meta_sems, (slot,), target)

    def meta_partner():
        return meta_copy(0, to_partner)

    def meta_send(side):
        return meta_copy(2 - side, to_row[side]), meta_copy(4 - side, to_cross[side])

    def meta_take(side):
        return meta_copy(1 + side, to_row[side]), meta_copy(3 + side, to_cross[side])

    def sky_partner():
        return remote(sky_ref, inner_ref, sky_sems, (0,), to_partner)

    def sky_beyond():
        return remote(sky_ref, outer_ref, sky_sems, (1,), to_beyond)

    def weight_copy():
        return remote(weight_ref, weight_got, weight_sems, (0,), to_partner)

    def part_copy(d, jj):
        return remote(part_send.at[d, jj], part_got.at[d, jj], part_sems, (d, jj), to_partner)

    def vis_copy(side, slot, jj):
        return remote(vis_send.at[side, jj], vis_got.at[slot, jj], vis_sems, (slot, jj), to_row[side])

    def scaled_copy(side, slot, jj):
        return remote(
            scaled_own.at[1, jj], scaled_own.at[2 * slot, jj], scaled_sems, (slot, jj), to_row[side]
        )

    def par_copy(d, jj):
        return remote(scaled_own.at[d, jj], scaled_par.at[d, jj], par_sems, (d, jj), to_partner)

    def last_edge():
        return remote(edge_send, edge_got, last_sems, (0,), to_beyond)

    def last_inner():
        return remote(acc_inner, inner_got, last_sems, (1,), to_partner)

    for side in range(2):

        @pl.when(jnp.logical_not(has_row[side]))
        def _(side=side):
            vis_got[side] = jnp.zeros(vis_got.shape[1:], BF16)

    @pl.when(jnp.logical_not(has_beyond))
    def _():
        outer_ref[...] = jnp.zeros_like(outer_ref)
        edge_got[...] = jnp.zeros_like(edge_got)

    barrier = pltpu.get_barrier_semaphore()
    pl.semaphore_signal(barrier, inc=1, device_id=to_partner, device_id_type=MESH)

    @pl.when(has_beyond)
    def _():
        pl.semaphore_signal(barrier, inc=1, device_id=to_beyond, device_id_type=MESH)

    for side in range(2):

        @pl.when(has_row[side])
        def _(side=side):
            pl.semaphore_signal(barrier, inc=1, device_id=to_row[side], device_id_type=MESH)
            pl.semaphore_signal(barrier, inc=1, device_id=to_cross[side], device_id_type=MESH)

    pl.semaphore_wait(
        barrier,
        1 + has_beyond.astype(I32) + 2 * has_up.astype(I32) + 2 * has_down.astype(I32),
    )

    @pl.when(has_beyond)
    def _():
        sky_beyond().start()

    meta_partner().start()
    for side in range(2):

        @pl.when(has_row[side])
        def _(side=side):
            for copy in meta_send(side):
                copy.start()

    sky_partner().start()
    weight_copy().start()

    per_block = block // FINE

    def table(j, carry):
        blk, at = j // per_block, pl.ds(pl.multiple_of((j % per_block) * FINE, FINE), FINE)
        for tab, half in ((row_tab, row_half), (col_tab, col_half)):
            lanes = pl.ds(half, size)
            c, s = cosines_ref[pl.ds(FINE + j, 1), lanes], sines_ref[pl.ds(FINE + j, 1), lanes]
            fc, fs = cosines_ref[:FINE, lanes], sines_ref[:FINE, lanes]
            tab[blk, 0, at, :] = (fc * c - fs * s).astype(BF16)
            tab[blk, 1, at, :] = (fs * c + fc * s).astype(BF16)
        return carry

    lax.fori_loop(0, length // FINE, table, 0)

    def flipped(j, carry):
        row = (ty % 2) * (size // FINE) + j
        c, s = cosines_ref[pl.ds(FINE + row, 1), :], sines_ref[pl.ds(FINE + row, 1), :]
        fc, fs = cosines_ref[:FINE, :], sines_ref[:FINE, :]
        at = pl.ds(pl.multiple_of(j * FINE, FINE), FINE)
        cos, sin = (fc * c - fs * s).astype(BF16), (fs * c + fc * s).astype(BF16)
        for blk in range(length // block):
            flip_tab[blk, 0, at, :] = cos[:, blk * block : (blk + 1) * block]
            flip_tab[blk, 1, at, :] = sin[:, blk * block : (blk + 1) * block]
        return carry

    lax.fori_loop(0, size // FINE, flipped, 0)

    meta_partner().wait()
    for side in range(2):

        @pl.when(has_row[side])
        def _(side=side):
            for copy in meta_take(side):
                copy.wait_recv()

        @pl.when(jnp.logical_not(has_row[side]))
        def _(side=side):
            for slot in (1 + side, 3 + side):
                for s in range(slots + 1):
                    for f in range(FIELDS):
                        meta_got[slot][s, f] = 0

    sources = ((meta_got[1], meta_got[3]), (meta_ref, meta_got[0]), (meta_got[2], meta_got[4]))
    even_here = core == 0

    def gather(s, carry):
        for d, (same, other) in enumerate(sources):
            for f in range(FIELDS):
                a, b = same[s, f], other[s, f]
                meta_all[d, 0, s, f] = jnp.where(even_here, a, b)
                meta_all[d, 1, s, f] = jnp.where(even_here, b, a)
        return carry

    lax.fori_loop(0, slots + 1, gather, 0)

    def pointing(d, j):
        even, odd = meta_all[d, 0, slots, 0], meta_all[d, 1, slots, 0]
        from_odd = (j >= even).astype(I32)
        slot = jnp.clip(j - from_odd * even, 0, slots - 1)
        live = j < even + odd
        return from_odd, slot, live

    def bins(d, from_odd, slot, k, which):
        b = meta_all[d, from_odd, slot, 3 + 2 * k + which]
        return jnp.clip(b, 0, length // block - 1)

    def gaussian(shape, axis, shift, decay, live):
        away = lax.broadcasted_iota(I32, shape, axis) + shift
        inside = jnp.logical_and(away >= -size, away < size)
        inside = jnp.logical_and(inside, live)
        away = away.astype(F32)
        if axis == 0:
            fold = away.reshape(shape[0] // 8, 8, shape[1])
            value = jnp.exp(-(fold * fold) * decay[None]).reshape(shape)
        else:
            value = jnp.exp(-(away * away) * wide(decay, shape[1]))
        return jnp.where(inside, value, jnp.zeros(shape, F32))

    def beams(d, from_odd, slot, live):
        oy, ox = meta_all[d, from_odd, slot, 0], meta_all[d, from_odd, slot, 1]
        width = jnp.full((8, 128), meta_all[d, from_odd, slot, 2], I32).astype(F32)
        decay = 1.0 / (2.0 * width * width)
        gy_ref[...] = gaussian((size, 128), 0, (1 - d) * size - oy, decay, live)
        outer_at, inner_at = 3 * core - 1, 1 - core
        gx_ref[0] = gaussian((8, size), 1, (outer_at - from_odd) * size - ox, decay, live)
        gx_ref[1] = gaussian((8, size), 1, (inner_at - from_odd) * size - ox, decay, live)

    def column_tables(d, from_odd, slot):
        for k in range(slots_uv):
            at = bins(d, from_odd, slot, k, 1)
            cols_ref[(2 * k) * block : (2 * k + 1) * block, :] = col_tab[at, 0]
            cols_ref[(2 * k + 1) * block : (2 * k + 2) * block, :] = col_tab[at, 1]

    def forward(d, j, result_ref):
        from_odd, slot, live = pointing(d, j)
        beams(d, from_odd, slot, live)
        column_tables(d, from_odd, slot)
        for k in range(slots_uv):
            at = bins(d, from_odd, slot, k, 0)
            rows_ref[(2 * k) * block : (2 * k + 1) * block, :] = row_tab[at, 0]
            rows_ref[(2 * k + 1) * block : (2 * k + 2) * block, :] = row_tab[at, 1]
        for at in range(0, size, CHUNK):
            cols = slice(at, at + CHUNK)
            value = gx_ref[0, 0:1, cols] * outer_ref[:, cols].astype(F32)
            value = value + gx_ref[1, 0:1, cols] * inner_ref[:, cols].astype(F32)
            beamed_ref[:, cols] = (wide(gy_ref[...], CHUNK) * value).astype(BF16)
        for at in range(0, size, CHUNK):
            cols = slice(at, at + CHUNK)
            first_ref[:, cols] = jnp.dot(
                rows_ref[...], beamed_ref[:, cols], preferred_element_type=F32
            ).astype(BF16)
        for k in range(slots_uv):
            rows = slice(2 * k * block, (2 * k + 2) * block)
            both = lax.dot_general(
                first_ref[rows, :], cols_ref[rows, :], (((1,), (1,)), ((), ())),
                preferred_element_type=F32,
            )
            result_ref[k, :, :block] = both[:block, :block] - both[block:, block:]
            result_ref[k, :, block:] = both[:block, block:] + both[block:, :block]

    def adjoint(d, j, scaled_ref):
        from_odd, slot, live = pointing(d, j)
        beams(d, from_odd, slot, live)
        column_tables(d, from_odd, slot)
        for k in range(slots_uv):
            at = bins(d, from_odd, slot, k, 0)
            flip_ref[:, (2 * k) * block : (2 * k + 1) * block] = flip_tab[at, 0]
            flip_ref[:, (2 * k + 1) * block : (2 * k + 2) * block] = flip_tab[at, 1]
        for k in range(slots_uv):
            rows = slice(2 * k * block, (2 * k + 2) * block)
            value = scaled_ref[k]
            real, turned = value[:, :block], value[:, block:]
            square = jnp.concatenate(
                [value, jnp.concatenate([turned, -real], axis=1)], axis=0
            )
            spread_ref[rows, :] = jnp.dot(
                square, cols_ref[rows, :], preferred_element_type=F32
            ).astype(BF16)
        for at in range(0, size, CHUNK):
            cols = slice(at, at + CHUNK)
            back = jnp.dot(flip_ref[...], spread_ref[:, cols], preferred_element_type=F32)
            back = wide(gy_ref[...], CHUNK) * back
            acc_outer[:, cols] += gx_ref[0, 0:1, cols] * back
            acc_inner[:, cols] += gx_ref[1, 0:1, cols] * back

    mine, theirs = half_slots * core, half_slots * (1 - core)

    @pl.when(has_beyond)
    def _():
        sky_beyond().wait_recv()

    sky_partner().wait_recv()

    def forward_step(s, carry):
        inside = s // (2 * half_slots)
        d = 2 * (s % 2) * (1 - inside) + inside
        jj = (s // 2) * (1 - inside) + (s - 2 * half_slots) * inside

        def role(i, carry):
            @pl.when(i == 0)
            def _():
                forward(d, theirs + jj, part_send.at[d, jj])
                part_copy(d, jj).start()

            @pl.when(i == 1)
            def _():
                forward(d, mine + jj, part_mine.at[d, jj])

            return carry

        lax.fori_loop(0, 2, role, 0)
        part_copy(d, jj).wait_recv()
        total = part_mine[d, jj] + part_got[d, jj]
        for side in range(2):

            @pl.when(jnp.logical_and(d == 2 * side, has_row[side]))
            def _(side=side):
                vis_send[side, jj] = total.astype(BF16)
                vis_copy(side, 1 - side, jj).start()

        @pl.when(d == 1)
        def _():
            vis_own[jj] = total

        return carry

    lax.fori_loop(0, 3 * half_slots, forward_step, 0)

    acc_outer[...] = jnp.zeros_like(acc_outer)
    acc_inner[...] = jnp.zeros_like(acc_inner)
    weight_copy().wait_recv()

    def adjoint_mine(d, jj):
        adjoint(d, mine + jj, scaled_own.at[d, jj])

    def adjoint_theirs(d, jj):
        par_copy(d, jj).wait_recv()
        adjoint(d, theirs + jj, scaled_par.at[d, jj])

    def own_step(jj, carry):
        from_odd, slot, live = pointing(1, mine + jj)
        used = meta_all[1, from_odd, slot, 3 + 2 * slots_uv]
        here = from_odd == core
        for side in range(2):

            @pl.when(has_row[side])
            def _(side=side):
                vis_copy(1 - side, side, jj).wait_recv()

        for k in range(slots_uv):
            weight = jnp.where(here, weight_ref[slot, k], weight_got[slot, k]).astype(F32)
            weight = weight * jnp.where(k < used, 1.0, 0.0).astype(F32)
            total = vis_own[jj, k] + vis_got[0, jj, k].astype(F32) + vis_got[1, jj, k].astype(F32)
            scaled_own[1, jj, k] = (total * wide(weight, 2 * block)).astype(BF16)
        for side in range(2):

            @pl.when(has_row[side])
            def _(side=side):
                scaled_copy(side, 1 - side, jj).start()

        par_copy(1, jj).start()
        adjoint_mine(1, jj)
        adjoint_theirs(1, jj)
        return carry

    lax.fori_loop(0, half_slots, own_step, 0)

    def other_step(jj, carry):
        for side in range(2):

            @pl.when(has_row[side])
            def _(side=side):
                scaled_copy(1 - side, side, jj).wait_recv()
                par_copy(2 * side, jj).start()

        for side in range(2):

            @pl.when(has_row[side])
            def _(side=side):
                adjoint_mine(2 * side, jj)

        for side in range(2):

            @pl.when(has_row[side])
            def _(side=side):
                adjoint_theirs(2 * side, jj)

        return carry

    lax.fori_loop(0, half_slots, other_step, 0)

    @pl.when(has_beyond)
    def _():
        edge_send[...] = acc_outer[...].astype(BF16)
        last_edge().start()

    last_inner().start()

    sky_partner().wait_send()
    weight_copy().wait_send()

    @pl.when(has_beyond)
    def _():
        sky_beyond().wait_send()

    for side in range(2):

        @pl.when(has_row[side])
        def _(side=side):
            for copy in meta_send(side):
                copy.wait_send()
            for jj in range(half_slots):
                vis_copy(side, 1 - side, jj).wait_send()
                scaled_copy(side, 1 - side, jj).wait_send()
                par_copy(2 * side, jj).wait_send()

    for jj in range(half_slots):
        par_copy(1, jj).wait_send()
        for d in range(3):
            part_copy(d, jj).wait_send()

    last_inner().wait()

    @pl.when(has_beyond)
    def _():
        last_edge().wait()

    out_ref[...] = inner_got[...] + edge_got[...].astype(F32)


def shards(sky, point_count, point_offset, beam_width, uv_bins, uv_count, uv_weight):
    size = sky.shape[0]
    length = 2 * size
    slots, slots_uv, block = uv_weight.shape[2], uv_weight.shape[3], uv_weight.shape[4]
    half_slots = slots // 2
    depth = 2 * slots_uv * block
    cosines, sines = seed_tables(length, FINE)
    rows = jnp.concatenate(
        [
            point_offset.reshape(slots, 2),
            beam_width.reshape(slots, 1).astype(I32),
            uv_bins.reshape(slots, 2 * slots_uv),
            uv_count.reshape(slots, 1),
        ],
        axis=1,
    )
    count = jnp.broadcast_to(point_count.reshape(1, 1), (1, FIELDS))
    meta = jnp.concatenate([rows, count], axis=0)
    weight = uv_weight.reshape(slots, slots_uv, block, block)

    dma = pltpu.SemaphoreType.DMA
    meta_shape = (slots + 1, FIELDS)
    tile = pltpu.VMEM((size, size), BF16)
    plane = pltpu.VMEM((size, size), F32)
    patch = (slots_uv, block, 2 * block)
    return pl.pallas_call(
        kernel,
        out_shape=jax.ShapeDtypeStruct((size, size), F32),
        in_specs=[pl.BlockSpec(memory_space=pltpu.SMEM)]
        + [pl.BlockSpec(memory_space=pltpu.VMEM)] * 4,
        out_specs=pl.BlockSpec(memory_space=pltpu.VMEM),
        scratch_shapes=[
            tuple([pltpu.SMEM(meta_shape, I32)] * 5),
            pltpu.SMEM((3, 2) + meta_shape, I32),
            tile,
            tile,
            pltpu.VMEM(weight.shape, BF16),
            pltpu.VMEM((length // block, 2, block, size), BF16),
            pltpu.VMEM((length // block, 2, size, block), BF16),
            pltpu.VMEM((length // block, 2, block, size), BF16),
            pltpu.VMEM((depth, size), BF16),
            pltpu.VMEM((size, depth), BF16),
            pltpu.VMEM((depth, size), BF16),
            tile,
            pltpu.VMEM((depth, size), BF16),
            pltpu.VMEM((depth, size), BF16),
            pltpu.VMEM((2, 8, size), F32),
            pltpu.VMEM((size, 128), F32),
            pltpu.VMEM((3, half_slots) + patch, F32),
            pltpu.VMEM((3, half_slots) + patch, F32),
            pltpu.VMEM((3, half_slots) + patch, F32),
            pltpu.VMEM((half_slots,) + patch, F32),
            pltpu.VMEM((2, half_slots) + patch, BF16),
            pltpu.VMEM((2, half_slots) + patch, BF16),
            pltpu.VMEM((3, half_slots) + patch, BF16),
            pltpu.VMEM((3, half_slots) + patch, BF16),
            plane,
            plane,
            tile,
            tile,
            plane,
            dma((2, 5)),
            dma((2, 2)),
            dma((2, 1)),
            dma((2, 3, half_slots)),
            dma((2, 2, half_slots)),
            dma((2, 2, half_slots)),
            dma((2, 3, half_slots)),
            dma((2, 2)),
        ],
        compiler_params=pltpu.CompilerParams(
            vmem_limit_bytes=56 * 1024 * 1024, collective_id=0, has_side_effects=True
        ),
    )(meta, cosines, sines, sky, weight)


def solution(mesh):
    in_specs = (
        P("ty", "tx"),
        P("ty", "tx"),
        P("ty", "tx", None, None),
        P("ty", "tx", None),
        P("ty", "tx", None, None, None),
        P("ty", "tx", None),
        P("ty", "tx", None, None, None, None),
    )
    out_specs = P("ty", "tx")
    return jax.shard_map(shards, mesh=mesh, in_specs=in_specs, out_specs=out_specs, check_vma=False)
```

time: 115 us -> 58.3 us (0.51); the launches traced: 113 us -> 58.1 us
  Pallas kernels: 103 us -> 51.7 us
  other arithmetic: 6.58 us -> 0.08 us
  local copies, waits for them, and re-layouts: 2.02 us -> 5.62 us
    pallas_call x5 -> x1, Pallas kernels: 103 us -> 51.7 us  [shards(): pl.pallas_call(kernel, out_shape=jax.ShapeDtypeStruct((size, size), F32),...]
    unnamed x0 -> x9, local copies, waits for them, and re-layouts: none -> 4.65 us
    add x1 -> x0, other arithmetic: 2.7 us -> none  [shards(): return own + above.astype(F32) + below.astype(F32)]
    mul x2 -> x0, other arithmetic: 1.91 us -> none  [the longest x1 1.91 us: small_tables(): return (jnp.cos(angle) * scale, jnp.sin(angle) * scale)]
    div x1 -> x0, other arithmetic: 1.2 us -> none  [shards(): decay = 1.0 / (2.0 * width * width)]
where the time goes in v1:
time: 58.3 us; the launch traced here: 58.1 us
  Pallas kernels  51.7 us (89%)
  local copies, waits for them, and re-layouts  5.62 us (10%)
  between operations  0.68 us (1%)
    pallas_call x1, Pallas kernels, shards(): pl.pallas_call(kernel, out_shape=jax.ShapeDtypeStruct((size, size), F32),...  51.7 us
    unnamed x9, local copies, waits for them, and re-layouts  4.65 us

profile of v1, /device:TPU:13, one launch (start us, length us, event | category | flops | bytes accessed | tf_op | source)
XLA Modules:
  0.0 58.1 jit_solution(13198279500857746598)
XLA Ops:
  0.7 0.0 copy-start.3
  0.7 0.6 %copy-done.3 = bf16[1,1,4]{2,1,0:T(2,128)(2,1)S(1)} copy-done((bf16[1,1,4]{2,1,0:T(2,128)(2,1)S(1)}, bf16[1,1,4]{2,1,0:T(2,128)(2,1)}, u32[]{:S(2)}) %copy-start.3) | copy-done | bytes 32
  1.3 0.0 copy-start.1
  1.3 0.1 copy.11
  1.4 0.6 %copy-done.1 = s32[1,1,4,2]{2,3,1,0:T(2,128)S(1)} copy-done((s32[1,1,4,2]{2,3,1,0:T(2,128)S(1)}, s32[1,1,4,2]{2,3,1,0:T(2,128)}, u32[]{:S(2)}) %copy-start.1) | copy-done | bytes 56
  2.0 0.0 copy-start
  2.0 0.1 copy.10
  2.1 0.6 %copy-done = s32[1,1,4,2,2]{2,4,3,1,0:T(2,128)S(1)} copy-done((s32[1,1,4,2,2]{2,4,3,1,0:T(2,128)S(1)}, s32[1,1,4,2,2]{2,4,3,1,0:T(2,128)}, u32[]{:S(2)}) %copy-start) | copy-done | bytes 88
  2.7 0.0 copy-start.2
  2.7 0.1 copy.12
  2.8 0.6 copy-done.2
  3.3 0.1 copy.13
  3.4 0.1 pad_add_fusion
  3.5 0.6 %concatenate.7.meta_ref = s32[5,8]{1,0:T(8,128)} pad(s32[4,8]{1,0:T(4,128)S(1)} %pad_add_fusion, s32[]{:T(128)} %bitcast.8), padding=0_1x0_0 | pad | bytes 292 | tf_op jit(solution)/shard_map/concatenate | solution.py:463
  4.1 51.7 %shard_map.91 = f32[512,512]{1,0:T(8,128)} custom-call(s32[5,8]{1,0:T(8,128)} %concatenate.7.meta_ref, f32[64,1024]{1,0:T(8,128)} %constant.4.clone.cosines_ref, f32[64,1024]{1,0:T(8,128)} %constant.5.clone.sines_ref, bf16[512,512]{1,0:T(8,128)(2,1)} %sky_ref.1, bf16[4,2,128,128]{3,2,1,0:T(8,128)(2,1)} %bitcast.9), custom_call_target="tpu_custom_call" | custom-call | tf_op jit(solution)/shard_map/pallas_call | solution.py:471
  55.8 2.3 %copy.16 = f32[512,512]{1,0:T(8,128)} copy(f32[512,512]{1,0:T(8,128)} %shard_map.91) | data formatting | bytes 2097152
  (1 shorter events, 0.0 us)
Async XLA Ops:
  0.7 0.7 %copy-start.3 = (bf16[1,1,4]{2,1,0:T(2,128)(2,1)S(1)}, bf16[1,1,4]{2,1,0:T(2,128)(2,1)}, u32[]{:S(2)}) copy-start(bf16[1,1,4]{2,1,0:T(2,128)(2,1)} %param.12) | copy-start | bytes 28
  1.3 0.7 %copy-start.1 = (s32[1,1,4,2]{2,3,1,0:T(2,128)S(1)}, s32[1,1,4,2]{2,3,1,0:T(2,128)}, u32[]{:S(2)}) copy-start(s32[1,1,4,2]{2,3,1,0:T(2,128)} %param.11) | copy-start | bytes 100
  2.0 0.7 %copy-start = (s32[1,1,4,2,2]{2,4,3,1,0:T(2,128)S(1)}, s32[1,1,4,2,2]{2,4,3,1,0:T(2,128)}, u32[]{:S(2)}) copy-start(s32[1,1,4,2,2]{2,4,3,1,0:T(2,128)} %param.13) | copy-start | bytes 196
  2.7 0.7 %copy-start.2 = (s32[1,1,4]{2,1,0:T(1,128)S(1)}, s32[1,1,4]{2,1,0:T(1,128)}, u32[]{:S(2)}) copy-start(s32[1,1,4]{2,1,0:T(1,128)} %param.14) | copy-start | bytes 52

commit v2 on v1

--- a/solution.py
+++ b/solution.py
@@ -14,6 +14,7 @@
 I32 = jnp.int32
 FINE = 32
 CHUNK = 256
+BANDS = 4
 FIELDS = 8
 MESH = pl.DeviceIdType.MESH
 
@@ -31,12 +32,14 @@
 
 
 def kernel(
-    meta_ref, cosines_ref, sines_ref, sky_ref, weight_ref, out_ref,
-    meta_got, meta_all, outer_ref, inner_ref, weight_got, row_tab, flip_tab, col_tab,
+    count_in, offset_in, width_in, bins_in, used_in, cosines_in, sines_in, sky_in, weight_in,
+    inner_got, edge_got,
+    meta_ref, meta_got, meta_all, sky_ref, outer_ref, inner_ref, weight_ref, weight_got,
+    cosines_ref, sines_ref, row_tab, flip_tab, col_tab,
     rows_ref, flip_ref, cols_ref, beamed_ref, first_ref, spread_ref, gx_ref, gy_ref,
     part_send, part_mine, part_got, vis_own, vis_send, vis_got,
-    scaled_own, scaled_par, acc_outer, acc_inner, edge_send, edge_got, inner_got,
-    meta_sems, sky_sems, weight_sems, part_sems, vis_sems, scaled_sems, par_sems, last_sems,
+    scaled_own, scaled_par, acc_outer, acc_inner, edge_send,
+    local_sems, meta_sems, sky_sems, weight_sems, part_sems, vis_sems, scaled_sems, par_sems, last_sems,
 ):
     size = sky_ref.shape[0]
     length = 2 * size
@@ -57,6 +60,18 @@
     to_row = ({"ty": ty - 1}, {"ty": ty + 1})
     to_cross = ({"ty": ty - 1, "tx": partner}, {"ty": ty + 1, "tx": partner})
 
+    local = [
+        pltpu.make_async_copy(source, target, local_sems.at[i])
+        for i, (source, target) in enumerate(
+            (
+                (sky_in, sky_ref),
+                (cosines_in, cosines_ref),
+                (sines_in, sines_ref),
+                (weight_in, weight_ref),
+            )
+        )
+    ]
+
     def remote(src, dst, sems, at, target):
         return pltpu.make_async_remote_copy(
             src_ref=src,
@@ -108,17 +123,6 @@
     def last_inner():
         return remote(acc_inner, inner_got, last_sems, (1,), to_partner)
 
-    for side in range(2):
-
-        @pl.when(jnp.logical_not(has_row[side]))
-        def _(side=side):
-            vis_got[side] = jnp.zeros(vis_got.shape[1:], BF16)
-
-    @pl.when(jnp.logical_not(has_beyond))
-    def _():
-        outer_ref[...] = jnp.zeros_like(outer_ref)
-        edge_got[...] = jnp.zeros_like(edge_got)
-
     barrier = pltpu.get_barrier_semaphore()
     pl.semaphore_signal(barrier, inc=1, device_id=to_partner, device_id_type=MESH)
 
@@ -133,6 +137,34 @@
             pl.semaphore_signal(barrier, inc=1, device_id=to_row[side], device_id_type=MESH)
             pl.semaphore_signal(barrier, inc=1, device_id=to_cross[side], device_id_type=MESH)
 
+    for copy in local:
+        copy.start()
+
+    meta_ref[slots, 0] = count_in[0, 0]
+    for s in range(slots):
+        meta_ref[s, 0] = offset_in[0, s]
+        meta_ref[s, 1] = offset_in[1, s]
+        meta_ref[s, 2] = width_in[0, s]
+        for k in range(slots_uv):
+            for which in range(2):
+                meta_ref[s, 3 + 2 * k + which] = bins_in[k, which, s]
+        meta_ref[s, 3 + 2 * slots_uv] = used_in[0, s]
+
+    for side in range(2):
+
+        @pl.when(jnp.logical_not(has_row[side]))
+        def _(side=side):
+            vis_got[side] = jnp.zeros(vis_got.shape[1:], BF16)
+
+    @pl.when(jnp.logical_not(has_beyond))
+    def _():
+        outer_ref[...] = jnp.zeros_like(outer_ref)
+        edge_got[...] = jnp.zeros_like(edge_got)
+
+    acc_outer[...] = jnp.zeros_like(acc_outer)
+    acc_inner[...] = jnp.zeros_like(acc_inner)
+
+    local[0].wait()
     pl.semaphore_wait(
         barrier,
         1 + has_beyond.astype(I32) + 2 * has_up.astype(I32) + 2 * has_down.astype(I32),
@@ -142,6 +174,7 @@
     def _():
         sky_beyond().start()
 
+    sky_partner().start()
     meta_partner().start()
     for side in range(2):
 
@@ -150,7 +183,8 @@
             for copy in meta_send(side):
                 copy.start()
 
-    sky_partner().start()
+    for copy in local[1:]:
+        copy.wait()
     weight_copy().start()
 
     per_block = block // FINE
@@ -191,22 +225,27 @@
         @pl.when(jnp.logical_not(has_row[side]))
         def _(side=side):
             for slot in (1 + side, 3 + side):
-                for s in range(slots + 1):
+                meta_got[slot][slots, 0] = 0
+                for s in range(slots):
                     for f in range(FIELDS):
                         meta_got[slot][s, f] = 0
 
     sources = ((meta_got[1], meta_got[3]), (meta_ref, meta_got[0]), (meta_got[2], meta_got[4]))
     even_here = core == 0
 
-    def gather(s, carry):
+    def gather(s, f):
         for d, (same, other) in enumerate(sources):
-            for f in range(FIELDS):
-                a, b = same[s, f], other[s, f]
-                meta_all[d, 0, s, f] = jnp.where(even_here, a, b)
-                meta_all[d, 1, s, f] = jnp.where(even_here, b, a)
+            a, b = same[s, f], other[s, f]
+            meta_all[d, 0, s, f] = jnp.where(even_here, a, b)
+            meta_all[d, 1, s, f] = jnp.where(even_here, b, a)
+
+    def gather_slot(s, carry):
+        for f in range(FIELDS):
+            gather(s, f)
         return carry
 
-    lax.fori_loop(0, slots + 1, gather, 0)
+    lax.fori_loop(0, slots, gather_slot, 0)
+    gather(slots, 0)
 
     def pointing(d, j):
         even, odd = meta_all[d, 0, slots, 0], meta_all[d, 1, slots, 0]
@@ -306,43 +345,43 @@
 
     sky_partner().wait_recv()
 
-    def forward_step(s, carry):
-        inside = s // (2 * half_slots)
-        d = 2 * (s % 2) * (1 - inside) + inside
-        jj = (s // 2) * (1 - inside) + (s - 2 * half_slots) * inside
-
-        def role(i, carry):
-            @pl.when(i == 0)
+    def member(g, i):
+        own = g // half_slots
+        d = 2 * i * (1 - own) + own
+        jj = g * (1 - own) + i * own
+        return d, jj
+
+    def forward_group(g, carry):
+        def give(i, carry):
+            d, jj = member(g, i)
+            forward(d, theirs + jj, part_send.at[d, jj])
+            part_copy(d, jj).start()
+            return carry
+
+        def take(i, carry):
+            d, jj = member(g, i)
+            forward(d, mine + jj, part_mine)
+            part_copy(d, jj).wait_recv()
+            total = part_mine[...] + part_got[d, jj]
+            for side in range(2):
+
+                @pl.when(jnp.logical_and(d == 2 * side, has_row[side]))
+                def _(side=side):
+                    vis_send[side, jj] = total.astype(BF16)
+                    vis_copy(side, 1 - side, jj).start()
+
+            @pl.when(d == 1)
             def _():
-                forward(d, theirs + jj, part_send.at[d, jj])
-                part_copy(d, jj).start()
-
-            @pl.when(i == 1)
-            def _():
-                forward(d, mine + jj, part_mine.at[d, jj])
+                vis_own[jj] = total
 
             return carry
 
-        lax.fori_loop(0, 2, role, 0)
-        part_copy(d, jj).wait_recv()
-        total = part_mine[d, jj] + part_got[d, jj]
-        for side in range(2):
-
-            @pl.when(jnp.logical_and(d == 2 * side, has_row[side]))
-            def _(side=side):
-                vis_send[side, jj] = total.astype(BF16)
-                vis_copy(side, 1 - side, jj).start()
-
-        @pl.when(d == 1)
-        def _():
-            vis_own[jj] = total
-
+        lax.fori_loop(0, 2, give, 0)
+        lax.fori_loop(0, 2, take, 0)
         return carry
 
-    lax.fori_loop(0, 3 * half_slots, forward_step, 0)
-
-    acc_outer[...] = jnp.zeros_like(acc_outer)
-    acc_inner[...] = jnp.zeros_like(acc_inner)
+    lax.fori_loop(0, half_slots + 1, forward_group, 0)
+
     weight_copy().wait_recv()
 
     def adjoint_mine(d, jj):
@@ -440,7 +479,17 @@
     def _():
         last_edge().wait()
 
-    out_ref[...] = inner_got[...] + edge_got[...].astype(F32)
+
+def add_kernel(inner_ref, edge_ref, out_hbm, out_ref, sems):
+    band = out_ref.shape[0] // BANDS
+    copies = []
+    for i in range(BANDS):
+        rows = slice(i * band, (i + 1) * band)
+        out_ref[rows, :] = inner_ref[rows, :] + edge_ref[rows, :].astype(F32)
+        copies.append(pltpu.make_async_copy(out_ref.at[rows], out_hbm.at[rows], sems.at[i]))
+        copies[-1].start()
+    for copy in copies:
+        copy.wait()
 
 
 def shards(sky, point_count, point_offset, beam_width, uv_bins, uv_count, uv_weight):
@@ -450,17 +499,11 @@
     half_slots = slots // 2
     depth = 2 * slots_uv * block
     cosines, sines = seed_tables(length, FINE)
-    rows = jnp.concatenate(
-        [
-            point_offset.reshape(slots, 2),
-            beam_width.reshape(slots, 1).astype(I32),
-            uv_bins.reshape(slots, 2 * slots_uv),
-            uv_count.reshape(slots, 1),
-        ],
-        axis=1,
-    )
-    count = jnp.broadcast_to(point_count.reshape(1, 1), (1, FIELDS))
-    meta = jnp.concatenate([rows, count], axis=0)
+    count = point_count.reshape(1, 1)
+    offset = jnp.transpose(point_offset, (0, 1, 3, 2)).reshape(2, slots)
+    width = beam_width.astype(I32).reshape(1, slots)
+    bins = jnp.transpose(uv_bins, (0, 1, 3, 4, 2)).reshape(slots_uv, 2, slots)
+    used = uv_count.reshape(1, slots)
     weight = uv_weight.reshape(slots, slots_uv, block, block)
 
     dma = pltpu.SemaphoreType.DMA
@@ -468,18 +511,24 @@
     tile = pltpu.VMEM((size, size), BF16)
     plane = pltpu.VMEM((size, size), F32)
     patch = (slots_uv, block, 2 * block)
-    return pl.pallas_call(
+    vmem = pl.BlockSpec(memory_space=pltpu.VMEM)
+    inner, edge = pl.pallas_call(
         kernel,
-        out_shape=jax.ShapeDtypeStruct((size, size), F32),
-        in_specs=[pl.BlockSpec(memory_space=pltpu.SMEM)]
-        + [pl.BlockSpec(memory_space=pltpu.VMEM)] * 4,
-        out_specs=pl.BlockSpec(memory_space=pltpu.VMEM),
+        out_shape=(jax.ShapeDtypeStruct((size, size), F32), jax.ShapeDtypeStruct((size, size), BF16)),
+        in_specs=[pl.BlockSpec(memory_space=pltpu.SMEM)] * 5
+        + [pl.BlockSpec(memory_space=pl.ANY)] * 4,
+        out_specs=(vmem, vmem),
         scratch_shapes=[
+            pltpu.SMEM(meta_shape, I32),
             tuple([pltpu.SMEM(meta_shape, I32)] * 5),
             pltpu.SMEM((3, 2) + meta_shape, I32),
             tile,
             tile,
+            tile,
             pltpu.VMEM(weight.shape, BF16),
+            pltpu.VMEM(weight.shape, BF16),
+            pltpu.VMEM(cosines.shape, F32),
+            pltpu.VMEM(sines.shape, F32),
             pltpu.VMEM((length // block, 2, block, size), BF16),
             pltpu.VMEM((length // block, 2, size, block), BF16),
             pltpu.VMEM((length // block, 2, block, size), BF16),
@@ -492,7 +541,7 @@
             pltpu.VMEM((2, 8, size), F32),
             pltpu.VMEM((size, 128), F32),
             pltpu.VMEM((3, half_slots) + patch, F32),
-            pltpu.VMEM((3, half_slots) + patch, F32),
+            pltpu.VMEM(patch, F32),
             pltpu.VMEM((3, half_slots) + patch, F32),
             pltpu.VMEM((half_slots,) + patch, F32),
             pltpu.VMEM((2, half_slots) + patch, BF16),
@@ -502,8 +551,7 @@
             plane,
             plane,
             tile,
-            tile,
-            plane,
+            dma((4,)),
             dma((2, 5)),
             dma((2, 2)),
             dma((2, 1)),
@@ -514,9 +562,18 @@
             dma((2, 2)),
         ],
         compiler_params=pltpu.CompilerParams(
-            vmem_limit_bytes=56 * 1024 * 1024, collective_id=0, has_side_effects=True
+            vmem_limit_bytes=30 * 1024 * 1024, collective_id=0, has_side_effects=True
         ),
-    )(meta, cosines, sines, sky, weight)
+    )(count, offset, width, bins, used, cosines, sines, sky, weight)
+    return pl.pallas_call(
+        add_kernel,
+        out_shape=jax.ShapeDtypeStruct((size, size), F32),
+        in_specs=[vmem, vmem],
+        out_specs=pl.BlockSpec(memory_space=pl.ANY),
+        scratch_shapes=[plane, dma((BANDS,))],
+        compiler_params=pltpu.CompilerParams(vmem_limit_bytes=8 * 1024 * 1024),
+        cost_estimate=pl.CostEstimate(flops=size * size, bytes_accessed=10 * size * size, transcendentals=0),
+    )(inner, edge)
 
 
 def solution(mesh):

time: 58.3 us -> 57.7 us (0.990)
    concatenate x1 -> x0, local copies, waits for them, and re-layouts: 0.6 us -> none  [shards(): meta = jnp.concatenate([rows, count], axis=0)]
    unnamed x9 -> x16, local copies, waits for them, and re-layouts: 4.65 us -> 5.2 us
    pallas_call x1 -> x2, Pallas kernels: 51.7 us -> 51.5 us  [the longest x1 50.5 us: shards(): pl.pallas_call(kernel, out_shape=(jax.ShapeDtypeStruct((size, size), F32)...]
where the time goes in v2:
time: 57.7 us; the launch traced here: 57.4 us
  Pallas kernels  51.5 us (89%)
  local copies, waits for them, and re-layouts  5.2 us (9%)
  between operations  0.68 us (1%)
    pallas_call x1, Pallas kernels, shards(): pl.pallas_call(kernel, out_shape=(jax.ShapeDtypeStruct((size, size), F32)...  50.5 us
    unnamed x16, local copies, waits for them, and re-layouts  5.2 us

profile of v2, /device:TPU:13, one launch (start us, length us, event | category | flops | bytes accessed | tf_op | source)
XLA Modules:
  0.0 57.4 jit_solution(16982955926096088974)
XLA Ops:
  0.7 0.0 copy-start.7
  0.7 0.0 copy-start.4
  0.7 0.6 %copy-done.7 = bf16[1,1,4]{2,1,0:T(2,128)(2,1)S(1)} copy-done((bf16[1,1,4]{2,1,0:T(2,128)(2,1)S(1)}, bf16[1,1,4]{2,1,0:T(2,128)(2,1)}, u32[]{:S(2)}) %copy-start.7) | copy-done | bytes 32
  1.3 0.0 copy-start.5
  1.3 0.0 copy-start.6
  1.3 0.0 copy-done.4
  1.4 0.6 %copy-done.5 = s32[1,1,4,2]{2,3,1,0:T(2,128)S(1)} copy-done((s32[1,1,4,2]{2,3,1,0:T(2,128)S(1)}, s32[1,1,4,2]{2,3,1,0:T(2,128)}, u32[]{:S(2)}) %copy-start.5) | copy-done | bytes 56
  2.0 0.0 copy-done.6
  2.0 0.0 copy-start
  2.0 1.0 %copy-done = bf16[512,512]{1,0:T(8,128)(2,1)S(1)} copy-done((bf16[512,512]{1,0:T(8,128)(2,1)S(1)}, bf16[512,512]{1,0:T(8,128)(2,1)}, u32[]{:S(2)}) %copy-start) | copy-done | bytes 524312
  3.0 0.0 copy-start.1
  3.0 0.9 %copy-done.1 = bf16[1,1,4,2,128,128]{5,4,3,2,1,0:T(8,128)(2,1)S(1)} copy-done((bf16[1,1,4,2,128,128]{5,4,3,2,1,0:T(8,128)(2,1)S(1)}, bf16[1,1,4,2,128,128]{5,4,3,2,1,0:T(8,128)(2,1)}, u32[]{:S(2)}) %copy-start.1) | copy-done | bytes 262168
  4.0 0.0 copy-start.2
  4.0 0.9 %copy-done.2 = f32[64,1024]{1,0:T(8,128)S(1)} copy-done((f32[64,1024]{1,0:T(8,128)S(1)}, f32[64,1024]{1,0:T(8,128)}, u32[]{:S(2)}) %copy-start.2) | copy-done | bytes 262168
  4.9 0.0 copy-start.3
  4.9 0.9 %copy-done.3 = f32[64,1024]{1,0:T(8,128)S(1)} copy-done((f32[64,1024]{1,0:T(8,128)S(1)}, f32[64,1024]{1,0:T(8,128)}, u32[]{:S(2)}) %copy-start.3) | copy-done | bytes 262168
  5.9 50.5 %shard_map.91 = (f32[512,512]{1,0:T(8,128)S(1)}, bf16[512,512]{1,0:T(8,128)(2,1)S(1)}) custom-call(s32[1,1]{1,0:T(1,128)S(6)} %copy.10.count_in, s32[2,4]{1,0:T(2,128)S(1)} %bitcast.13, s32[1,4]{1,0:T(1,128)S(1)} %bitcast_convert_fusion.width_in, s32[2,2,4]{2,1,0:T(2,128)S(1)} %bitcast.12, s32[1,4]{1,0:T(1,128)S(1)} %bitcast.14, f32[64,1024]{1,0:T(8,128)S(1)} %copy-done.3, ...), custom_call_target="tpu_custom_call" | custom-call | tf_op jit(solution)/shard_map/pallas_call | solution.py:515
  56.4 1.0 %shard_map.92 = f32[512,512]{1,0:T(8,128)} custom-call(f32[512,512]{1,0:T(8,128)S(1)} %get-tuple-element.7.inner_ref, bf16[512,512]{1,0:T(8,128)(2,1)S(1)} %get-tuple-element.8.edge_ref), custom_call_target="tpu_custom_call" | custom-call | flops 262144 | bytes 2621440 | tf_op jit(solution)/shard_map/pallas_call | solution.py:568
  (1 shorter events, 0.0 us)
Async XLA Ops:
  0.7 0.7 %copy-start.7 = (bf16[1,1,4]{2,1,0:T(2,128)(2,1)S(1)}, bf16[1,1,4]{2,1,0:T(2,128)(2,1)}, u32[]{:S(2)}) copy-start(bf16[1,1,4]{2,1,0:T(2,128)(2,1)} %param.12) | copy-start | bytes 28
  0.7 0.7 %copy-start.4 = (s32[1,1,4,2,2]{2,4,3,1,0:T(2,128)S(1)}, s32[1,1,4,2,2]{2,4,3,1,0:T(2,128)}, u32[]{:S(2)}) copy-start(s32[1,1,4,2,2]{2,4,3,1,0:T(2,128)} %param.13) | copy-start | bytes 196
  1.3 0.7 %copy-start.5 = (s32[1,1,4,2]{2,3,1,0:T(2,128)S(1)}, s32[1,1,4,2]{2,3,1,0:T(2,128)}, u32[]{:S(2)}) copy-start(s32[1,1,4,2]{2,3,1,0:T(2,128)} %param.11) | copy-start | bytes 100
  1.3 0.7 %copy-start.6 = (s32[1,1,4]{2,1,0:T(1,128)S(1)}, s32[1,1,4]{2,1,0:T(1,128)}, u32[]{:S(2)}) copy-start(s32[1,1,4]{2,1,0:T(1,128)} %param.14) | copy-start | bytes 52
  2.0 1.0 %copy-start = (bf16[512,512]{1,0:T(8,128)(2,1)S(1)}, bf16[512,512]{1,0:T(8,128)(2,1)}, u32[]{:S(2)}) copy-start(bf16[512,512]{1,0:T(8,128)(2,1)} %sky_in.1) | copy-start | bytes 1572868
  3.0 0.9 %copy-start.1 = (bf16[1,1,4,2,128,128]{5,4,3,2,1,0:T(8,128)(2,1)S(1)}, bf16[1,1,4,2,128,128]{5,4,3,2,1,0:T(8,128)(2,1)}, u32[]{:S(2)}) copy-start(bf16[1,1,4,2,128,128]{5,4,3,2,1,0:T(8,128)(2,1)} %param.15) | copy-start | bytes 786436
  4.0 0.9 %copy-start.2 = (f32[64,1024]{1,0:T(8,128)S(1)}, f32[64,1024]{1,0:T(8,128)}, u32[]{:S(2)}) copy-start(f32[64,1024]{1,0:T(8,128)} %constant.5.clone.sines_in) | copy-start | bytes 786436
  4.9 0.9 %copy-start.3 = (f32[64,1024]{1,0:T(8,128)S(1)}, f32[64,1024]{1,0:T(8,128)}, u32[]{:S(2)}) copy-start(f32[64,1024]{1,0:T(8,128)} %constant.4.clone.cosines_in) | copy-start | bytes 786436

commit v3 on v2

--- a/solution.py
+++ b/solution.py
@@ -24,7 +24,7 @@
     rows = np.concatenate([np.arange(fine), fine * np.arange(length // fine)])
     angle = (rows[:, None] * pixels[None, :] % length) * (2.0 * math.pi / length)
     scale = np.where(np.arange(rows.shape[0]) < fine, 1.0 / math.sqrt(length), 1.0)[:, None]
-    return (np.cos(angle) * scale).astype(np.float32), (np.sin(angle) * scale).astype(np.float32)
+    return np.stack([np.cos(angle) * scale, np.sin(angle) * scale]).astype(np.float32)
 
 
 def wide(column, width):
@@ -32,14 +32,15 @@
 
 
 def kernel(
-    count_in, offset_in, width_in, bins_in, used_in, cosines_in, sines_in, sky_in, weight_in,
+    count_in, offset_in, width_in, bins_in, used_in, seeds_in, sky_in, weight_in,
     inner_got, edge_got,
     meta_ref, meta_got, meta_all, sky_ref, outer_ref, inner_ref, weight_ref, weight_got,
-    cosines_ref, sines_ref, row_tab, flip_tab, col_tab,
+    seeds_ref, row_tab, flip_tab, col_tab,
     rows_ref, flip_ref, cols_ref, beamed_ref, first_ref, spread_ref, gx_ref, gy_ref,
-    part_send, part_mine, part_got, vis_own, vis_send, vis_got,
+    part_send, part_got, totals, raw_send, raw_got, sum_send, sum_got,
     scaled_own, scaled_par, acc_outer, acc_inner, edge_send,
-    local_sems, meta_sems, sky_sems, weight_sems, part_sems, vis_sems, scaled_sems, par_sems, last_sems,
+    local_sems, meta_sems, sky_sems, weight_sems, part_sems, raw_sems, sum_sems, scaled_sems,
+    onward_sems, par_sems, last_sems,
 ):
     size = sky_ref.shape[0]
     length = 2 * size
@@ -59,14 +60,19 @@
     to_beyond = {"tx": beyond}
     to_row = ({"ty": ty - 1}, {"ty": ty + 1})
     to_cross = ({"ty": ty - 1, "tx": partner}, {"ty": ty + 1, "tx": partner})
+    odd_row = ty % 2
+    d_far, d_mate = 2 * odd_row, 2 * (1 - odd_row)
+    giving, fed = ty - 2 + 4 * odd_row, ty + 2 - 4 * odd_row
+    has_far = jnp.logical_and(giving >= 0, giving < ny)
+    has_fed = jnp.logical_and(fed >= 0, fed < ny)
+    to_mate, to_giving, to_fed = {"ty": ty + 1 - 2 * odd_row}, {"ty": giving}, {"ty": fed}
 
     local = [
         pltpu.make_async_copy(source, target, local_sems.at[i])
         for i, (source, target) in enumerate(
             (
                 (sky_in, sky_ref),
-                (cosines_in, cosines_ref),
-                (sines_in, sines_ref),
+                (seeds_in, seeds_ref),
                 (weight_in, weight_ref),
             )
         )
@@ -103,19 +109,27 @@
     def weight_copy():
         return remote(weight_ref, weight_got, weight_sems, (0,), to_partner)
 
-    def part_copy(d, jj):
-        return remote(part_send.at[d, jj], part_got.at[d, jj], part_sems, (d, jj), to_partner)
-
-    def vis_copy(side, slot, jj):
-        return remote(vis_send.at[side, jj], vis_got.at[slot, jj], vis_sems, (slot, jj), to_row[side])
-
-    def scaled_copy(side, slot, jj):
+    def part_copy(g, jj):
+        return remote(part_send.at[g, jj], part_got.at[g, jj], part_sems, (g, jj), to_partner)
+
+    def raw_copy(target, jj, k):
+        return remote(raw_send.at[jj, k], raw_got.at[jj, k], raw_sems, (jj, k), target)
+
+    def sum_copy(jj, k):
+        return remote(sum_send.at[jj, k], sum_got.at[jj, k], sum_sems, (jj, k), to_mate)
+
+    def scaled_copy(jj, k):
         return remote(
-            scaled_own.at[1, jj], scaled_own.at[2 * slot, jj], scaled_sems, (slot, jj), to_row[side]
+            scaled_own.at[2, jj, k], scaled_own.at[1, jj, k], scaled_sems, (jj, k), to_mate
         )
 
-    def par_copy(d, jj):
-        return remote(scaled_own.at[d, jj], scaled_par.at[d, jj], par_sems, (d, jj), to_partner)
+    def onward_copy(target, jj, k):
+        return remote(
+            scaled_own.at[1, jj, k], scaled_own.at[0, jj, k], onward_sems, (jj, k), target
+        )
+
+    def par_copy(g, jj):
+        return remote(scaled_own.at[g, jj], scaled_par.at[g, jj], par_sems, (g, jj), to_partner)
 
     def last_edge():
         return remote(edge_send, edge_got, last_sems, (0,), to_beyond)
@@ -136,6 +150,12 @@
         def _(side=side):
             pl.semaphore_signal(barrier, inc=1, device_id=to_row[side], device_id_type=MESH)
             pl.semaphore_signal(barrier, inc=1, device_id=to_cross[side], device_id_type=MESH)
+
+    for has, target in ((has_far, to_giving), (has_fed, to_fed)):
+
+        @pl.when(has)
+        def _(target=target):
+            pl.semaphore_signal(barrier, inc=1, device_id=target, device_id_type=MESH)
 
     for copy in local:
         copy.start()
@@ -150,11 +170,9 @@
                 meta_ref[s, 3 + 2 * k + which] = bins_in[k, which, s]
         meta_ref[s, 3 + 2 * slots_uv] = used_in[0, s]
 
-    for side in range(2):
-
-        @pl.when(jnp.logical_not(has_row[side]))
-        def _(side=side):
-            vis_got[side] = jnp.zeros(vis_got.shape[1:], BF16)
+    @pl.when(jnp.logical_not(has_fed))
+    def _():
+        raw_got[...] = jnp.zeros_like(raw_got)
 
     @pl.when(jnp.logical_not(has_beyond))
     def _():
@@ -167,7 +185,8 @@
     local[0].wait()
     pl.semaphore_wait(
         barrier,
-        1 + has_beyond.astype(I32) + 2 * has_up.astype(I32) + 2 * has_down.astype(I32),
+        1 + has_beyond.astype(I32) + 2 * has_up.astype(I32) + 2 * has_down.astype(I32)
+        + has_far.astype(I32) + has_fed.astype(I32),
     )
 
     @pl.when(has_beyond)
@@ -193,8 +212,8 @@
         blk, at = j // per_block, pl.ds(pl.multiple_of((j % per_block) * FINE, FINE), FINE)
         for tab, half in ((row_tab, row_half), (col_tab, col_half)):
             lanes = pl.ds(half, size)
-            c, s = cosines_ref[pl.ds(FINE + j, 1), lanes], sines_ref[pl.ds(FINE + j, 1), lanes]
-            fc, fs = cosines_ref[:FINE, lanes], sines_ref[:FINE, lanes]
+            c, s = seeds_ref[0, pl.ds(FINE + j, 1), lanes], seeds_ref[1, pl.ds(FINE + j, 1), lanes]
+            fc, fs = seeds_ref[0, :FINE, lanes], seeds_ref[1, :FINE, lanes]
             tab[blk, 0, at, :] = (fc * c - fs * s).astype(BF16)
             tab[blk, 1, at, :] = (fs * c + fc * s).astype(BF16)
         return carry
@@ -203,8 +222,8 @@
 
     def flipped(j, carry):
         row = (ty % 2) * (size // FINE) + j
-        c, s = cosines_ref[pl.ds(FINE + row, 1), :], sines_ref[pl.ds(FINE + row, 1), :]
-        fc, fs = cosines_ref[:FINE, :], sines_ref[:FINE, :]
+        c, s = seeds_ref[0, pl.ds(FINE + row, 1), :], seeds_ref[1, pl.ds(FINE + row, 1), :]
+        fc, fs = seeds_ref[0, :FINE, :], seeds_ref[1, :FINE, :]
         at = pl.ds(pl.multiple_of(j * FINE, FINE), FINE)
         cos, sin = (fc * c - fs * s).astype(BF16), (fs * c + fc * s).astype(BF16)
         for blk in range(length // block):
@@ -345,103 +364,108 @@
 
     sky_partner().wait_recv()
 
-    def member(g, i):
-        own = g // half_slots
-        d = 2 * i * (1 - own) + own
-        jj = g * (1 - own) + i * own
-        return d, jj
-
-    def forward_group(g, carry):
-        def give(i, carry):
-            d, jj = member(g, i)
-            forward(d, theirs + jj, part_send.at[d, jj])
-            part_copy(d, jj).start()
+    def give(g, d):
+        def step(jj, carry):
+            forward(d, theirs + jj, part_send.at[g, jj])
+            part_copy(g, jj).start()
             return carry
 
-        def take(i, carry):
-            d, jj = member(g, i)
-            forward(d, mine + jj, part_mine)
-            part_copy(d, jj).wait_recv()
-            total = part_mine[...] + part_got[d, jj]
-            for side in range(2):
-
-                @pl.when(jnp.logical_and(d == 2 * side, has_row[side]))
-                def _(side=side):
-                    vis_send[side, jj] = total.astype(BF16)
-                    vis_copy(side, 1 - side, jj).start()
-
-            @pl.when(d == 1)
-            def _():
-                vis_own[jj] = total
-
+        lax.fori_loop(0, half_slots, step, 0)
+
+    def take(g, d, after):
+        def step(jj, carry):
+            forward(d, mine + jj, totals.at[g, jj])
+            part_copy(g, jj).wait_recv()
+            after(jj)
             return carry
 
-        lax.fori_loop(0, 2, give, 0)
-        lax.fori_loop(0, 2, take, 0)
-        return carry
-
-    lax.fori_loop(0, half_slots + 1, forward_group, 0)
+        lax.fori_loop(0, half_slots, step, 0)
+
+    def give_far(jj):
+        for k in range(slots_uv):
+            raw_send[jj, k] = (totals[0, jj, k] + part_got[0, jj, k]).astype(BF16)
+            raw_copy(to_giving, jj, k).start()
+
+    def keep(g):
+        def add(jj):
+            totals[g, jj] = totals[g, jj] + part_got[g, jj]
+
+        return add
+
+    @pl.when(has_far)
+    def _():
+        give(0, d_far)
+        take(0, d_far, give_far)
+
+    give(1, d_mate)
+    take(1, d_mate, keep(1))
+    give(2, 1)
+    take(2, 1, keep(2))
+
+    for jj in range(half_slots):
+        for k in range(slots_uv):
+
+            @pl.when(has_fed)
+            def _(jj=jj, k=k):
+                raw_copy(to_fed, jj, k).wait_recv()
+
+            sum_send[jj, k] = (totals[1, jj, k] + raw_got[jj, k].astype(F32)).astype(BF16)
+            sum_copy(jj, k).start()
 
     weight_copy().wait_recv()
-
-    def adjoint_mine(d, jj):
-        adjoint(d, mine + jj, scaled_own.at[d, jj])
-
-    def adjoint_theirs(d, jj):
-        par_copy(d, jj).wait_recv()
-        adjoint(d, theirs + jj, scaled_par.at[d, jj])
-
-    def own_step(jj, carry):
+    for jj in range(half_slots):
         from_odd, slot, live = pointing(1, mine + jj)
         used = meta_all[1, from_odd, slot, 3 + 2 * slots_uv]
         here = from_odd == core
-        for side in range(2):
-
-            @pl.when(has_row[side])
-            def _(side=side):
-                vis_copy(1 - side, side, jj).wait_recv()
-
         for k in range(slots_uv):
             weight = jnp.where(here, weight_ref[slot, k], weight_got[slot, k]).astype(F32)
             weight = weight * jnp.where(k < used, 1.0, 0.0).astype(F32)
-            total = vis_own[jj, k] + vis_got[0, jj, k].astype(F32) + vis_got[1, jj, k].astype(F32)
-            scaled_own[1, jj, k] = (total * wide(weight, 2 * block)).astype(BF16)
-        for side in range(2):
-
-            @pl.when(has_row[side])
-            def _(side=side):
-                scaled_copy(side, 1 - side, jj).start()
+            sum_copy(jj, k).wait_recv()
+            total = totals[2, jj, k] + sum_got[jj, k].astype(F32)
+            scaled_own[2, jj, k] = (total * wide(weight, 2 * block)).astype(BF16)
+            scaled_copy(jj, k).start()
+        par_copy(2, jj).start()
+
+    def adjoint_group(g, d):
+        def step_mine(jj, carry):
+            adjoint(d, mine + jj, scaled_own.at[g, jj])
+            return carry
+
+        def step_theirs(jj, carry):
+            par_copy(g, jj).wait_recv()
+            adjoint(d, theirs + jj, scaled_par.at[g, jj])
+            return carry
+
+        return step_mine, step_theirs
+
+    for step in adjoint_group(2, 1):
+        lax.fori_loop(0, half_slots, step, 0)
+
+    for jj in range(half_slots):
+        for k in range(slots_uv):
+            scaled_copy(jj, k).wait_recv()
+
+            @pl.when(has_fed)
+            def _(jj=jj, k=k):
+                onward_copy(to_fed, jj, k).start()
 
         par_copy(1, jj).start()
-        adjoint_mine(1, jj)
-        adjoint_theirs(1, jj)
-        return carry
-
-    lax.fori_loop(0, half_slots, own_step, 0)
-
-    def other_step(jj, carry):
-        for side in range(2):
-
-            @pl.when(has_row[side])
-            def _(side=side):
-                scaled_copy(1 - side, side, jj).wait_recv()
-                par_copy(2 * side, jj).start()
-
-        for side in range(2):
-
-            @pl.when(has_row[side])
-            def _(side=side):
-                adjoint_mine(2 * side, jj)
-
-        for side in range(2):
-
-            @pl.when(has_row[side])
-            def _(side=side):
-                adjoint_theirs(2 * side, jj)
-
-        return carry
-
-    lax.fori_loop(0, half_slots, other_step, 0)
+
+    for step in adjoint_group(1, d_mate):
+        lax.fori_loop(0, half_slots, step, 0)
+
+    @pl.when(has_far)
+    def _():
+        step_mine, step_theirs = adjoint_group(0, d_far)
+
+        def step(jj, carry):
+            for k in range(slots_uv):
+                onward_copy(to_giving, jj, k).wait_recv()
+            par_copy(0, jj).start()
+            return step_mine(jj, carry)
+
+        lax.fori_loop(0, half_slots, step, 0)
+        lax.fori_loop(0, half_slots, step_theirs, 0)
 
     @pl.when(has_beyond)
     def _():
@@ -463,15 +487,25 @@
         def _(side=side):
             for copy in meta_send(side):
                 copy.wait_send()
-            for jj in range(half_slots):
-                vis_copy(side, 1 - side, jj).wait_send()
-                scaled_copy(side, 1 - side, jj).wait_send()
-                par_copy(2 * side, jj).wait_send()
 
     for jj in range(half_slots):
-        par_copy(1, jj).wait_send()
-        for d in range(3):
-            part_copy(d, jj).wait_send()
+        for g in (1, 2):
+            part_copy(g, jj).wait_send()
+            par_copy(g, jj).wait_send()
+        for k in range(slots_uv):
+            sum_copy(jj, k).wait_send()
+            scaled_copy(jj, k).wait_send()
+
+            @pl.when(has_fed)
+            def _(jj=jj, k=k):
+                onward_copy(to_fed, jj, k).wait_send()
+
+        @pl.when(has_far)
+        def _(jj=jj):
+            part_copy(0, jj).wait_send()
+            par_copy(0, jj).wait_send()
+            for k in range(slots_uv):
+                raw_copy(to_giving, jj, k).wait_send()
 
     last_inner().wait()
 
@@ -498,7 +532,7 @@
     slots, slots_uv, block = uv_weight.shape[2], uv_weight.shape[3], uv_weight.shape[4]
     half_slots = slots // 2
     depth = 2 * slots_uv * block
-    cosines, sines = seed_tables(length, FINE)
+    seeds = seed_tables(length, FINE)
     count = point_count.reshape(1, 1)
     offset = jnp.transpose(point_offset, (0, 1, 3, 2)).reshape(2, slots)
     width = beam_width.astype(I32).reshape(1, slots)
@@ -516,7 +550,7 @@
         kernel,
         out_shape=(jax.ShapeDtypeStruct((size, size), F32), jax.ShapeDtypeStruct((size, size), BF16)),
         in_specs=[pl.BlockSpec(memory_space=pltpu.SMEM)] * 5
-        + [pl.BlockSpec(memory_space=pl.ANY)] * 4,
+        + [pl.BlockSpec(memory_space=pl.ANY)] * 3,
         out_specs=(vmem, vmem),
         scratch_shapes=[
             pltpu.SMEM(meta_shape, I32),
@@ -527,8 +561,7 @@
             tile,
             pltpu.VMEM(weight.shape, BF16),
             pltpu.VMEM(weight.shape, BF16),
-            pltpu.VMEM(cosines.shape, F32),
-            pltpu.VMEM(sines.shape, F32),
+            pltpu.VMEM(seeds.shape, F32),
             pltpu.VMEM((length // block, 2, block, size), BF16),
             pltpu.VMEM((length // block, 2, size, block), BF16),
             pltpu.VMEM((length // block, 2, block, size), BF16),
@@ -541,30 +574,33 @@
             pltpu.VMEM((2, 8, size), F32),
             pltpu.VMEM((size, 128), F32),
             pltpu.VMEM((3, half_slots) + patch, F32),
-            pltpu.VMEM(patch, F32),
             pltpu.VMEM((3, half_slots) + patch, F32),
-            pltpu.VMEM((half_slots,) + patch, F32),
-            pltpu.VMEM((2, half_slots) + patch, BF16),
-            pltpu.VMEM((2, half_slots) + patch, BF16),
+            pltpu.VMEM((3, half_slots) + patch, F32),
+            pltpu.VMEM((half_slots,) + patch, BF16),
+            pltpu.VMEM((half_slots,) + patch, BF16),
+            pltpu.VMEM((half_slots,) + patch, BF16),
+            pltpu.VMEM((half_slots,) + patch, BF16),
             pltpu.VMEM((3, half_slots) + patch, BF16),
             pltpu.VMEM((3, half_slots) + patch, BF16),
             plane,
             plane,
             tile,
-            dma((4,)),
+            dma((3,)),
             dma((2, 5)),
             dma((2, 2)),
             dma((2, 1)),
             dma((2, 3, half_slots)),
-            dma((2, 2, half_slots)),
-            dma((2, 2, half_slots)),
+            dma((2, half_slots, slots_uv)),
+            dma((2, half_slots, slots_uv)),
+            dma((2, half_slots, slots_uv)),
+            dma((2, half_slots, slots_uv)),
             dma((2, 3, half_slots)),
             dma((2, 2)),
         ],
         compiler_params=pltpu.CompilerParams(
-            vmem_limit_bytes=30 * 1024 * 1024, collective_id=0, has_side_effects=True
+            vmem_limit_bytes=int(56 * 1024 * 1024), collective_id=0, has_side_effects=True
         ),
-    )(count, offset, width, bins, used, cosines, sines, sky, weight)
+    )(count, offset, width, bins, used, seeds, sky, weight)
     return pl.pallas_call(
         add_kernel,
         out_shape=jax.ShapeDtypeStruct((size, size), F32),

time: 57.7 us -> 57.6 us (level)
  local copies, waits for them, and re-layouts: 5.2 us -> 2.91 us
  Pallas kernels: 51.5 us -> 53.3 us
    unnamed x16 -> x6, local copies, waits for them, and re-layouts: 5.2 us -> 2.91 us
    pallas_call x1, Pallas kernels: 50.5 us -> 52.2 us  [shards(): pl.pallas_call(kernel, out_shape=(jax.ShapeDtypeStruct((size, size), F32)...]
where the time goes in v3:
time: 57.6 us; the launch traced here: 57.4 us
  Pallas kernels  53.3 us (93%)
  local copies, waits for them, and re-layouts  2.91 us (5%)
  between operations  0.68 us (1%)
    pallas_call x1, Pallas kernels, shards(): pl.pallas_call(kernel, out_shape=(jax.ShapeDtypeStruct((size, size), F32)...  52.2 us
    unnamed x6, local copies, waits for them, and re-layouts  2.91 us

profile of v3, /device:TPU:13, one launch (start us, length us, event | category | flops | bytes accessed | tf_op | source)
XLA Modules:
  0.0 57.4 jit_solution(14203520960755112520)
XLA Ops:
  0.7 0.0 copy-start.2
  0.7 0.6 %copy-done.2 = bf16[1,1,4]{2,1,0:T(2,128)(2,1)S(1)} copy-done((bf16[1,1,4]{2,1,0:T(2,128)(2,1)S(1)}, bf16[1,1,4]{2,1,0:T(2,128)(2,1)}, u32[]{:S(2)}) %copy-start.2) | copy-done | bytes 32
  1.3 0.5 bitcast_convert_fusion.width_in
  1.8 52.2 %shard_map.82 = (f32[512,512]{1,0:T(8,128)}, bf16[512,512]{1,0:T(8,128)(2,1)}) custom-call(s32[1,1]{1,0:T(1,128)S(6)} %copy.9.count_in, s32[2,4]{1,0:T(2,128)} %bitcast.13, s32[1,4]{1,0:T(1,128)} %bitcast_convert_fusion.width_in, s32[2,2,4]{2,1,0:T(2,128)} %bitcast.12, s32[1,4]{1,0:T(1,128)} %bitcast.14, f32[2,64,1024]{2,1,0:T(8,128)} %constant.2.clone.seeds_in, ...), custom_call_target="tpu_custom_call" | custom-call | tf_op jit(solution)/shard_map/pallas_call | solution.py:549
  54.1 0.0 copy-start
  54.1 1.2 %copy-done = f32[512,512]{1,0:T(8,128)S(1)} copy-done((f32[512,512]{1,0:T(8,128)S(1)}, f32[512,512]{1,0:T(8,128)}, u32[]{:S(2)}) %copy-start) | copy-done | bytes 1048600
  55.3 0.0 copy-start.1
  55.3 1.0 %copy-done.1 = bf16[512,512]{1,0:T(8,128)(2,1)S(1)} copy-done((bf16[512,512]{1,0:T(8,128)(2,1)S(1)}, bf16[512,512]{1,0:T(8,128)(2,1)}, u32[]{:S(2)}) %copy-start.1) | copy-done | bytes 524312
  56.3 1.0 %shard_map.83 = f32[512,512]{1,0:T(8,128)} custom-call(f32[512,512]{1,0:T(8,128)S(1)} %copy-done, bf16[512,512]{1,0:T(8,128)(2,1)S(1)} %copy-done.1), custom_call_target="tpu_custom_call" | custom-call | flops 262144 | bytes 2621440 | tf_op jit(solution)/shard_map/pallas_call | solution.py:604
Async XLA Ops:
  0.7 0.7 %copy-start.2 = (bf16[1,1,4]{2,1,0:T(2,128)(2,1)S(1)}, bf16[1,1,4]{2,1,0:T(2,128)(2,1)}, u32[]{:S(2)}) copy-start(bf16[1,1,4]{2,1,0:T(2,128)(2,1)} %param.11) | copy-start | bytes 28
  54.1 1.2 %copy-start = (f32[512,512]{1,0:T(8,128)S(1)}, f32[512,512]{1,0:T(8,128)}, u32[]{:S(2)}) copy-start(f32[512,512]{1,0:T(8,128)} %get-tuple-element.7.inner_ref) | copy-start | bytes 3145732
  55.3 1.0 %copy-start.1 = (bf16[512,512]{1,0:T(8,128)(2,1)S(1)}, bf16[512,512]{1,0:T(8,128)(2,1)}, u32[]{:S(2)}) copy-start(bf16[512,512]{1,0:T(8,128)(2,1)} %get-tuple-element.8.edge_ref) | copy-start | bytes 1572868

commit v4 on v3

--- a/solution.py
+++ b/solution.py
@@ -36,7 +36,7 @@
     inner_got, edge_got,
     meta_ref, meta_got, meta_all, sky_ref, outer_ref, inner_ref, weight_ref, weight_got,
     seeds_ref, row_tab, flip_tab, col_tab,
-    rows_ref, flip_ref, cols_ref, beamed_ref, first_ref, spread_ref, gx_ref, gy_ref,
+    beamed_ref, first_ref, spread_ref, gx_ref, gy_ref,
     part_send, part_got, totals, raw_send, raw_got, sum_send, sum_got,
     scaled_own, scaled_par, acc_outer, acc_inner, edge_send,
     local_sems, meta_sems, sky_sems, weight_sems, part_sems, raw_sems, sum_sems, scaled_sems,
@@ -170,10 +170,6 @@
                 meta_ref[s, 3 + 2 * k + which] = bins_in[k, which, s]
         meta_ref[s, 3 + 2 * slots_uv] = used_in[0, s]
 
-    @pl.when(jnp.logical_not(has_fed))
-    def _():
-        raw_got[...] = jnp.zeros_like(raw_got)
-
     @pl.when(jnp.logical_not(has_beyond))
     def _():
         outer_ref[...] = jnp.zeros_like(outer_ref)
@@ -182,12 +178,13 @@
     acc_outer[...] = jnp.zeros_like(acc_outer)
     acc_inner[...] = jnp.zeros_like(acc_inner)
 
-    local[0].wait()
-    pl.semaphore_wait(
-        barrier,
-        1 + has_beyond.astype(I32) + 2 * has_up.astype(I32) + 2 * has_down.astype(I32)
-        + has_far.astype(I32) + has_fed.astype(I32),
-    )
+    with jax.named_scope("barrier"):
+        local[0].wait()
+        pl.semaphore_wait(
+            barrier,
+            1 + has_beyond.astype(I32) + 2 * has_up.astype(I32) + 2 * has_down.astype(I32)
+            + has_far.astype(I32) + has_fed.astype(I32),
+        )
 
     @pl.when(has_beyond)
     def _():
@@ -214,11 +211,12 @@
             lanes = pl.ds(half, size)
             c, s = seeds_ref[0, pl.ds(FINE + j, 1), lanes], seeds_ref[1, pl.ds(FINE + j, 1), lanes]
             fc, fs = seeds_ref[0, :FINE, lanes], seeds_ref[1, :FINE, lanes]
-            tab[blk, 0, at, :] = (fc * c - fs * s).astype(BF16)
-            tab[blk, 1, at, :] = (fs * c + fc * s).astype(BF16)
+            tab[blk, at, :] = (fc * c - fs * s).astype(BF16)
+            tab[blk, pl.ds(pl.multiple_of(block + (j % per_block) * FINE, FINE), FINE), :] = (fs * c + fc * s).astype(BF16)
         return carry
 
-    lax.fori_loop(0, length // FINE, table, 0)
+    with jax.named_scope("tables"):
+        lax.fori_loop(0, length // FINE, table, 0)
 
     def flipped(j, carry):
         row = (ty % 2) * (size // FINE) + j
@@ -227,27 +225,29 @@
         at = pl.ds(pl.multiple_of(j * FINE, FINE), FINE)
         cos, sin = (fc * c - fs * s).astype(BF16), (fs * c + fc * s).astype(BF16)
         for blk in range(length // block):
-            flip_tab[blk, 0, at, :] = cos[:, blk * block : (blk + 1) * block]
-            flip_tab[blk, 1, at, :] = sin[:, blk * block : (blk + 1) * block]
+            flip_tab[blk, at, :block] = cos[:, blk * block : (blk + 1) * block]
+            flip_tab[blk, at, block:] = sin[:, blk * block : (blk + 1) * block]
         return carry
 
-    lax.fori_loop(0, size // FINE, flipped, 0)
-
-    meta_partner().wait()
-    for side in range(2):
-
-        @pl.when(has_row[side])
-        def _(side=side):
-            for copy in meta_take(side):
-                copy.wait_recv()
-
-        @pl.when(jnp.logical_not(has_row[side]))
-        def _(side=side):
-            for slot in (1 + side, 3 + side):
-                meta_got[slot][slots, 0] = 0
-                for s in range(slots):
-                    for f in range(FIELDS):
-                        meta_got[slot][s, f] = 0
+    with jax.named_scope("flips"):
+        lax.fori_loop(0, size // FINE, flipped, 0)
+
+    with jax.named_scope("meta"):
+        meta_partner().wait()
+        for side in range(2):
+
+            @pl.when(has_row[side])
+            def _(side=side):
+                for copy in meta_take(side):
+                    copy.wait_recv()
+
+            @pl.when(jnp.logical_not(has_row[side]))
+            def _(side=side):
+                for slot in (1 + side, 3 + side):
+                    meta_got[slot][slots, 0] = 0
+                    for s in range(slots):
+                        for f in range(FIELDS):
+                            meta_got[slot][s, f] = 0
 
     sources = ((meta_got[1], meta_got[3]), (meta_ref, meta_got[0]), (meta_got[2], meta_got[4]))
     even_here = core == 0
@@ -289,43 +289,45 @@
             value = jnp.exp(-(away * away) * wide(decay, shape[1]))
         return jnp.where(inside, value, jnp.zeros(shape, F32))
 
-    def beams(d, from_odd, slot, live):
+    def beams(i, carry):
+        d, j = i // slots, i % slots
+        from_odd, slot, live = pointing(d, j)
         oy, ox = meta_all[d, from_odd, slot, 0], meta_all[d, from_odd, slot, 1]
         width = jnp.full((8, 128), meta_all[d, from_odd, slot, 2], I32).astype(F32)
         decay = 1.0 / (2.0 * width * width)
-        gy_ref[...] = gaussian((size, 128), 0, (1 - d) * size - oy, decay, live)
+        gy_ref[d, j] = gaussian((size, 128), 0, (1 - d) * size - oy, decay, live)
         outer_at, inner_at = 3 * core - 1, 1 - core
-        gx_ref[0] = gaussian((8, size), 1, (outer_at - from_odd) * size - ox, decay, live)
-        gx_ref[1] = gaussian((8, size), 1, (inner_at - from_odd) * size - ox, decay, live)
-
-    def column_tables(d, from_odd, slot):
-        for k in range(slots_uv):
-            at = bins(d, from_odd, slot, k, 1)
-            cols_ref[(2 * k) * block : (2 * k + 1) * block, :] = col_tab[at, 0]
-            cols_ref[(2 * k + 1) * block : (2 * k + 2) * block, :] = col_tab[at, 1]
+        gx_ref[d, j, 0] = gaussian((8, size), 1, (outer_at - from_odd) * size - ox, decay, live)
+        gx_ref[d, j, 1] = gaussian((8, size), 1, (inner_at - from_odd) * size - ox, decay, live)
+        return carry
+
+    with jax.named_scope("beams"):
+        lax.fori_loop(0, 3 * slots, beams, 0)
+
+    def column_table(d, from_odd, slot, k):
+        return col_tab[bins(d, from_odd, slot, k, 1)]
 
     def forward(d, j, result_ref):
         from_odd, slot, live = pointing(d, j)
-        beams(d, from_odd, slot, live)
-        column_tables(d, from_odd, slot)
-        for k in range(slots_uv):
-            at = bins(d, from_odd, slot, k, 0)
-            rows_ref[(2 * k) * block : (2 * k + 1) * block, :] = row_tab[at, 0]
-            rows_ref[(2 * k + 1) * block : (2 * k + 2) * block, :] = row_tab[at, 1]
+        rows = jnp.concatenate(
+            [row_tab[bins(d, from_odd, slot, k, 0)] for k in range(slots_uv)], axis=0
+        )
+        gy = wide(gy_ref[d, j], CHUNK)
         for at in range(0, size, CHUNK):
             cols = slice(at, at + CHUNK)
-            value = gx_ref[0, 0:1, cols] * outer_ref[:, cols].astype(F32)
-            value = value + gx_ref[1, 0:1, cols] * inner_ref[:, cols].astype(F32)
-            beamed_ref[:, cols] = (wide(gy_ref[...], CHUNK) * value).astype(BF16)
+            value = gx_ref[d, j, 0, 0:1, cols] * outer_ref[:, cols].astype(F32)
+            value = value + gx_ref[d, j, 1, 0:1, cols] * inner_ref[:, cols].astype(F32)
+            beamed_ref[:, cols] = (gy * value).astype(BF16)
         for at in range(0, size, CHUNK):
             cols = slice(at, at + CHUNK)
             first_ref[:, cols] = jnp.dot(
-                rows_ref[...], beamed_ref[:, cols], preferred_element_type=F32
+                rows, beamed_ref[:, cols], preferred_element_type=F32
             ).astype(BF16)
         for k in range(slots_uv):
-            rows = slice(2 * k * block, (2 * k + 2) * block)
             both = lax.dot_general(
-                first_ref[rows, :], cols_ref[rows, :], (((1,), (1,)), ((), ())),
+                first_ref[2 * k * block : (2 * k + 2) * block, :],
+                column_table(d, from_odd, slot, k),
+                (((1,), (1,)), ((), ())),
                 preferred_element_type=F32,
             )
             result_ref[k, :, :block] = both[:block, :block] - both[block:, block:]
@@ -333,36 +335,33 @@
 
     def adjoint(d, j, scaled_ref):
         from_odd, slot, live = pointing(d, j)
-        beams(d, from_odd, slot, live)
-        column_tables(d, from_odd, slot)
+        rows = jnp.concatenate(
+            [flip_tab[bins(d, from_odd, slot, k, 0)] for k in range(slots_uv)], axis=1
+        )
+        gy = wide(gy_ref[d, j], CHUNK)
         for k in range(slots_uv):
-            at = bins(d, from_odd, slot, k, 0)
-            flip_ref[:, (2 * k) * block : (2 * k + 1) * block] = flip_tab[at, 0]
-            flip_ref[:, (2 * k + 1) * block : (2 * k + 2) * block] = flip_tab[at, 1]
-        for k in range(slots_uv):
-            rows = slice(2 * k * block, (2 * k + 2) * block)
             value = scaled_ref[k]
             real, turned = value[:, :block], value[:, block:]
             square = jnp.concatenate(
                 [value, jnp.concatenate([turned, -real], axis=1)], axis=0
             )
-            spread_ref[rows, :] = jnp.dot(
-                square, cols_ref[rows, :], preferred_element_type=F32
+            spread_ref[2 * k * block : (2 * k + 2) * block, :] = jnp.dot(
+                square, column_table(d, from_odd, slot, k), preferred_element_type=F32
             ).astype(BF16)
         for at in range(0, size, CHUNK):
             cols = slice(at, at + CHUNK)
-            back = jnp.dot(flip_ref[...], spread_ref[:, cols], preferred_element_type=F32)
-            back = wide(gy_ref[...], CHUNK) * back
-            acc_outer[:, cols] += gx_ref[0, 0:1, cols] * back
-            acc_inner[:, cols] += gx_ref[1, 0:1, cols] * back
+            back = gy * jnp.dot(rows, spread_ref[:, cols], preferred_element_type=F32)
+            acc_outer[:, cols] += gx_ref[d, j, 0, 0:1, cols] * back
+            acc_inner[:, cols] += gx_ref[d, j, 1, 0:1, cols] * back
 
     mine, theirs = half_slots * core, half_slots * (1 - core)
 
-    @pl.when(has_beyond)
-    def _():
-        sky_beyond().wait_recv()
-
-    sky_partner().wait_recv()
+    with jax.named_scope("sky"):
+        @pl.when(has_beyond)
+        def _():
+            sky_beyond().wait_recv()
+
+        sky_partner().wait_recv()
 
     def give(g, d):
         def step(jj, carry):
@@ -370,7 +369,8 @@
             part_copy(g, jj).start()
             return carry
 
-        lax.fori_loop(0, half_slots, step, 0)
+        with jax.named_scope(f"give{g}"):
+            lax.fori_loop(0, half_slots, step, 0)
 
     def take(g, d, after):
         def step(jj, carry):
@@ -379,7 +379,8 @@
             after(jj)
             return carry
 
-        lax.fori_loop(0, half_slots, step, 0)
+        with jax.named_scope(f"take{g}"):
+            lax.fori_loop(0, half_slots, step, 0)
 
     def give_far(jj):
         for k in range(slots_uv):
@@ -397,34 +398,49 @@
         give(0, d_far)
         take(0, d_far, give_far)
 
+    def pass_one(jj, k, fed_too):
+        value = totals[1, jj, k]
+        if fed_too:
+            value = value + raw_got[jj, k].astype(F32)
+        sum_send[jj, k] = value.astype(BF16)
+        sum_copy(jj, k).start()
+
+    def give_mate(jj):
+        totals[1, jj] = totals[1, jj] + part_got[1, jj]
+
+        @pl.when(jnp.logical_not(has_fed))
+        def _():
+            for k in range(slots_uv):
+                pass_one(jj, k, False)
+
     give(1, d_mate)
-    take(1, d_mate, keep(1))
+    take(1, d_mate, give_mate)
     give(2, 1)
     take(2, 1, keep(2))
 
-    for jj in range(half_slots):
-        for k in range(slots_uv):
-
-            @pl.when(has_fed)
-            def _(jj=jj, k=k):
-                raw_copy(to_fed, jj, k).wait_recv()
-
-            sum_send[jj, k] = (totals[1, jj, k] + raw_got[jj, k].astype(F32)).astype(BF16)
-            sum_copy(jj, k).start()
-
-    weight_copy().wait_recv()
-    for jj in range(half_slots):
-        from_odd, slot, live = pointing(1, mine + jj)
-        used = meta_all[1, from_odd, slot, 3 + 2 * slots_uv]
-        here = from_odd == core
-        for k in range(slots_uv):
-            weight = jnp.where(here, weight_ref[slot, k], weight_got[slot, k]).astype(F32)
-            weight = weight * jnp.where(k < used, 1.0, 0.0).astype(F32)
-            sum_copy(jj, k).wait_recv()
-            total = totals[2, jj, k] + sum_got[jj, k].astype(F32)
-            scaled_own[2, jj, k] = (total * wide(weight, 2 * block)).astype(BF16)
-            scaled_copy(jj, k).start()
-        par_copy(2, jj).start()
+    with jax.named_scope("pass_sums"):
+
+        @pl.when(has_fed)
+        def _():
+            for jj in range(half_slots):
+                for k in range(slots_uv):
+                    raw_copy(to_fed, jj, k).wait_recv()
+                    pass_one(jj, k, True)
+
+    with jax.named_scope("scale"):
+        weight_copy().wait_recv()
+        for jj in range(half_slots):
+            from_odd, slot, live = pointing(1, mine + jj)
+            used = meta_all[1, from_odd, slot, 3 + 2 * slots_uv]
+            here = from_odd == core
+            for k in range(slots_uv):
+                weight = jnp.where(here, weight_ref[slot, k], weight_got[slot, k]).astype(F32)
+                weight = weight * jnp.where(k < used, 1.0, 0.0).astype(F32)
+                sum_copy(jj, k).wait_recv()
+                total = totals[2, jj, k] + sum_got[jj, k].astype(F32)
+                scaled_own[2, jj, k] = (total * wide(weight, 2 * block)).astype(BF16)
+                scaled_copy(jj, k).start()
+            par_copy(2, jj).start()
 
     def adjoint_group(g, d):
         def step_mine(jj, carry):
@@ -438,34 +454,38 @@
 
         return step_mine, step_theirs
 
-    for step in adjoint_group(2, 1):
-        lax.fori_loop(0, half_slots, step, 0)
-
-    for jj in range(half_slots):
-        for k in range(slots_uv):
-            scaled_copy(jj, k).wait_recv()
-
-            @pl.when(has_fed)
-            def _(jj=jj, k=k):
-                onward_copy(to_fed, jj, k).start()
-
-        par_copy(1, jj).start()
-
-    for step in adjoint_group(1, d_mate):
-        lax.fori_loop(0, half_slots, step, 0)
-
-    @pl.when(has_far)
-    def _():
-        step_mine, step_theirs = adjoint_group(0, d_far)
-
-        def step(jj, carry):
+    with jax.named_scope("adj_own"):
+        for step in adjoint_group(2, 1):
+            lax.fori_loop(0, half_slots, step, 0)
+
+    with jax.named_scope("pass_scaled"):
+        for jj in range(half_slots):
             for k in range(slots_uv):
-                onward_copy(to_giving, jj, k).wait_recv()
-            par_copy(0, jj).start()
-            return step_mine(jj, carry)
-
-        lax.fori_loop(0, half_slots, step, 0)
-        lax.fori_loop(0, half_slots, step_theirs, 0)
+                scaled_copy(jj, k).wait_recv()
+
+                @pl.when(has_fed)
+                def _(jj=jj, k=k):
+                    onward_copy(to_fed, jj, k).start()
+
+            par_copy(1, jj).start()
+
+    with jax.named_scope("adj_mate"):
+        for step in adjoint_group(1, d_mate):
+            lax.fori_loop(0, half_slots, step, 0)
+
+    with jax.named_scope("adj_far"):
+        @pl.when(has_far)
+        def _():
+            step_mine, step_theirs = adjoint_group(0, d_far)
+
+            def step(jj, carry):
+                for k in range(slots_uv):
+                    onward_copy(to_giving, jj, k).wait_recv()
+                par_copy(0, jj).start()
+                return step_mine(jj, carry)
+
+            lax.fori_loop(0, half_slots, step, 0)
+            lax.fori_loop(0, half_slots, step_theirs, 0)
 
     @pl.when(has_beyond)
     def _():
@@ -507,11 +527,12 @@
             for k in range(slots_uv):
                 raw_copy(to_giving, jj, k).wait_send()
 
-    last_inner().wait()
-
-    @pl.when(has_beyond)
-    def _():
-        last_edge().wait()
+    with jax.named_scope("last"):
+        last_inner().wait()
+
+        @pl.when(has_beyond)
+        def _():
+            last_edge().wait()
 
 
 def add_kernel(inner_ref, edge_ref, out_hbm, out_ref, sems):
@@ -562,17 +583,14 @@
             pltpu.VMEM(weight.shape, BF16),
             pltpu.VMEM(weight.shape, BF16),
             pltpu.VMEM(seeds.shape, F32),
-            pltpu.VMEM((length // block, 2, block, size), BF16),
-            pltpu.VMEM((length // block, 2, size, block), BF16),
-            pltpu.VMEM((length // block, 2, block, size), BF16),
-            pltpu.VMEM((depth, size), BF16),
-            pltpu.VMEM((size, depth), BF16),
-            pltpu.VMEM((depth, size), BF16),
+            pltpu.VMEM((length // block, 2 * block, size), BF16),
+            pltpu.VMEM((length // block, size, 2 * block), BF16),
+            pltpu.VMEM((length // block, 2 * block, size), BF16),
             tile,
             pltpu.VMEM((depth, size), BF16),
             pltpu.VMEM((depth, size), BF16),
-            pltpu.VMEM((2, 8, size), F32),
-            pltpu.VMEM((size, 128), F32),
+            pltpu.VMEM((3, slots, 2, 8, size), F32),
+            pltpu.VMEM((3, slots, size, 128), F32),
             pltpu.VMEM((3, half_slots) + patch, F32),
             pltpu.VMEM((3, half_slots) + patch, F32),
             pltpu.VMEM((3, half_slots) + patch, F32),

time: 57.6 us -> 51.9 us (0.901)
  Pallas kernels: 53.3 us -> 47.5 us
    pallas_call x1, Pallas kernels: 52.2 us -> 46.5 us  [shards(): pl.pallas_call(kernel, out_shape=(jax.ShapeDtypeStruct((size, size), F32)...]
where the time goes in v4:
time: 51.9 us; the launch traced here: 51.6 us
  Pallas kernels  47.5 us (92%)
  local copies, waits for them, and re-layouts  2.91 us (6%)
  between operations  0.68 us (1%)
    pallas_call x1, Pallas kernels, shards(): pl.pallas_call(kernel, out_shape=(jax.ShapeDtypeStruct((size, size), F32)...  46.5 us
    unnamed x6, local copies, waits for them, and re-layouts  2.91 us

profile of v4, /device:TPU:13, one launch (start us, length us, event | category | flops | bytes accessed | tf_op | source)
XLA Modules:
  0.0 51.6 jit_solution(11579108723480406873)
XLA Ops:
  0.7 0.0 copy-start.2
  0.7 0.6 %copy-done.2 = bf16[1,1,4]{2,1,0:T(2,128)(2,1)S(1)} copy-done((bf16[1,1,4]{2,1,0:T(2,128)(2,1)S(1)}, bf16[1,1,4]{2,1,0:T(2,128)(2,1)}, u32[]{:S(2)}) %copy-start.2) | copy-done | bytes 32
  1.3 0.5 bitcast_convert_fusion.width_in
  1.8 46.5 %shard_map.82 = (f32[512,512]{1,0:T(8,128)}, bf16[512,512]{1,0:T(8,128)(2,1)}) custom-call(s32[1,1]{1,0:T(1,128)S(6)} %copy.9.count_in, s32[2,4]{1,0:T(2,128)} %bitcast.13, s32[1,4]{1,0:T(1,128)} %bitcast_convert_fusion.width_in, s32[2,2,4]{2,1,0:T(2,128)} %bitcast.12, s32[1,4]{1,0:T(1,128)} %bitcast.14, f32[2,64,1024]{2,1,0:T(8,128)} %constant.2.clone.seeds_in, ...), custom_call_target="tpu_custom_call" | custom-call | tf_op jit(solution)/shard_map/pallas_call | solution.py:570
  48.3 0.0 copy-start
  48.3 1.2 %copy-done = f32[512,512]{1,0:T(8,128)S(1)} copy-done((f32[512,512]{1,0:T(8,128)S(1)}, f32[512,512]{1,0:T(8,128)}, u32[]{:S(2)}) %copy-start) | copy-done | bytes 1048600
  49.6 0.0 copy-start.1
  49.6 1.0 %copy-done.1 = bf16[512,512]{1,0:T(8,128)(2,1)S(1)} copy-done((bf16[512,512]{1,0:T(8,128)(2,1)S(1)}, bf16[512,512]{1,0:T(8,128)(2,1)}, u32[]{:S(2)}) %copy-start.1) | copy-done | bytes 524312
  50.6 1.0 %shard_map.83 = f32[512,512]{1,0:T(8,128)} custom-call(f32[512,512]{1,0:T(8,128)S(1)} %copy-done, bf16[512,512]{1,0:T(8,128)(2,1)S(1)} %copy-done.1), custom_call_target="tpu_custom_call" | custom-call | flops 262144 | bytes 2621440 | tf_op jit(solution)/shard_map/pallas_call | solution.py:622
Async XLA Ops:
  0.7 0.7 %copy-start.2 = (bf16[1,1,4]{2,1,0:T(2,128)(2,1)S(1)}, bf16[1,1,4]{2,1,0:T(2,128)(2,1)}, u32[]{:S(2)}) copy-start(bf16[1,1,4]{2,1,0:T(2,128)(2,1)} %param.11) | copy-start | bytes 28
  48.3 1.2 %copy-start = (f32[512,512]{1,0:T(8,128)S(1)}, f32[512,512]{1,0:T(8,128)}, u32[]{:S(2)}) copy-start(f32[512,512]{1,0:T(8,128)} %get-tuple-element.7.inner_ref) | copy-start | bytes 3145732
  49.6 1.0 %copy-start.1 = (bf16[512,512]{1,0:T(8,128)(2,1)S(1)}, bf16[512,512]{1,0:T(8,128)(2,1)}, u32[]{:S(2)}) copy-start(bf16[512,512]{1,0:T(8,128)(2,1)} %get-tuple-element.8.edge_ref) | copy-start | bytes 1572868

commit v5 on v4

--- a/solution.py
+++ b/solution.py
@@ -37,8 +37,8 @@
     meta_ref, meta_got, meta_all, sky_ref, outer_ref, inner_ref, weight_ref, weight_got,
     seeds_ref, row_tab, flip_tab, col_tab,
     beamed_ref, first_ref, spread_ref, gx_ref, gy_ref,
-    part_send, part_got, totals, raw_send, raw_got, sum_send, sum_got,
-    scaled_own, scaled_par, acc_outer, acc_inner, edge_send,
+    early, part_send, part_got, totals, raw_send, raw_got, sum_send, sum_got,
+    scaled_own, scaled_par, acc_outer, acc_inner, edge_send, inner_send,
     local_sems, meta_sems, sky_sems, weight_sems, part_sems, raw_sems, sum_sems, scaled_sems,
     onward_sems, par_sems, last_sems,
 ):
@@ -103,8 +103,9 @@
     def sky_partner():
         return remote(sky_ref, inner_ref, sky_sems, (0,), to_partner)
 
-    def sky_beyond():
-        return remote(sky_ref, outer_ref, sky_sems, (1,), to_beyond)
+    def sky_beyond(part):
+        cols = slice(part * CHUNK, (part + 1) * CHUNK)
+        return remote(sky_ref.at[:, cols], outer_ref.at[:, cols], sky_sems, (1 + part,), to_beyond)
 
     def weight_copy():
         return remote(weight_ref, weight_got, weight_sems, (0,), to_partner)
@@ -135,7 +136,10 @@
         return remote(edge_send, edge_got, last_sems, (0,), to_beyond)
 
     def last_inner():
-        return remote(acc_inner, inner_got, last_sems, (1,), to_partner)
+        return remote(inner_send, inner_got, last_sems, (1,), to_partner)
+
+    def no_edge():
+        return pltpu.make_async_copy(edge_send, edge_got, local_sems.at[len(local)])
 
     barrier = pltpu.get_barrier_semaphore()
     pl.semaphore_signal(barrier, inc=1, device_id=to_partner, device_id_type=MESH)
@@ -160,11 +164,13 @@
     for copy in local:
         copy.start()
 
+    lane = lax.broadcasted_iota(I32, (1, slots), 1)
+    widths = width_in[...].astype(F32)
     meta_ref[slots, 0] = count_in[0, 0]
     for s in range(slots):
         meta_ref[s, 0] = offset_in[0, s]
         meta_ref[s, 1] = offset_in[1, s]
-        meta_ref[s, 2] = width_in[0, s]
+        meta_ref[s, 2] = jnp.sum(jnp.where(lane == s, widths, 0.0)).astype(I32)
         for k in range(slots_uv):
             for which in range(2):
                 meta_ref[s, 3 + 2 * k + which] = bins_in[k, which, s]
@@ -173,10 +179,7 @@
     @pl.when(jnp.logical_not(has_beyond))
     def _():
         outer_ref[...] = jnp.zeros_like(outer_ref)
-        edge_got[...] = jnp.zeros_like(edge_got)
-
-    acc_outer[...] = jnp.zeros_like(acc_outer)
-    acc_inner[...] = jnp.zeros_like(acc_inner)
+        edge_send[...] = jnp.zeros_like(edge_send)
 
     with jax.named_scope("barrier"):
         local[0].wait()
@@ -188,7 +191,8 @@
 
     @pl.when(has_beyond)
     def _():
-        sky_beyond().start()
+        for part in range(size // CHUNK):
+            sky_beyond(part).start()
 
     sky_partner().start()
     meta_partner().start()
@@ -201,7 +205,9 @@
 
     for copy in local[1:]:
         copy.wait()
-    weight_copy().start()
+
+    acc_outer[...] = jnp.zeros_like(acc_outer)
+    acc_inner[...] = jnp.zeros_like(acc_inner)
 
     per_block = block // FINE
 
@@ -307,31 +313,36 @@
     def column_table(d, from_odd, slot, k):
         return col_tab[bins(d, from_odd, slot, k, 1)]
 
-    def forward(d, j, result_ref):
+    def forward(d, j, result_ref, parts, before_ref=None):
         from_odd, slot, live = pointing(d, j)
         rows = jnp.concatenate(
             [row_tab[bins(d, from_odd, slot, k, 0)] for k in range(slots_uv)], axis=0
         )
         gy = wide(gy_ref[d, j], CHUNK)
-        for at in range(0, size, CHUNK):
-            cols = slice(at, at + CHUNK)
+        for part in parts:
+            cols = slice(part * CHUNK, (part + 1) * CHUNK)
             value = gx_ref[d, j, 0, 0:1, cols] * outer_ref[:, cols].astype(F32)
             value = value + gx_ref[d, j, 1, 0:1, cols] * inner_ref[:, cols].astype(F32)
             beamed_ref[:, cols] = (gy * value).astype(BF16)
-        for at in range(0, size, CHUNK):
-            cols = slice(at, at + CHUNK)
+        for part in parts:
+            cols = slice(part * CHUNK, (part + 1) * CHUNK)
             first_ref[:, cols] = jnp.dot(
                 rows, beamed_ref[:, cols], preferred_element_type=F32
             ).astype(BF16)
+        cols = slice(parts[0] * CHUNK, (parts[-1] + 1) * CHUNK)
         for k in range(slots_uv):
             both = lax.dot_general(
-                first_ref[2 * k * block : (2 * k + 2) * block, :],
-                column_table(d, from_odd, slot, k),
+                first_ref[2 * k * block : (2 * k + 2) * block, cols],
+                col_tab[bins(d, from_odd, slot, k, 1), :, cols],
                 (((1,), (1,)), ((), ())),
                 preferred_element_type=F32,
             )
-            result_ref[k, :, :block] = both[:block, :block] - both[block:, block:]
-            result_ref[k, :, block:] = both[:block, block:] + both[block:, :block]
+            real = both[:block, :block] - both[block:, block:]
+            turned = both[:block, block:] + both[block:, :block]
+            if before_ref is not None:
+                real, turned = real + before_ref[k, :, :block], turned + before_ref[k, :, block:]
+            result_ref[k, :, :block] = real
+            result_ref[k, :, block:] = turned
 
     def adjoint(d, j, scaled_ref):
         from_odd, slot, live = pointing(d, j)
@@ -356,16 +367,47 @@
 
     mine, theirs = half_slots * core, half_slots * (1 - core)
 
-    with jax.named_scope("sky"):
+    parts = size // CHUNK
+
+    def ahead(g, d):
+        def step(j, carry):
+            forward(d, j, early.at[g, j], range(parts - 1))
+            return carry
+
+        with jax.named_scope(f"ahead{g}"):
+            lax.fori_loop(0, slots, step, 0)
+
+    with jax.named_scope("sky0"):
+        sky_partner().wait_recv()
+
         @pl.when(has_beyond)
         def _():
-            sky_beyond().wait_recv()
-
-        sky_partner().wait_recv()
+            for part in range(parts - 1):
+                sky_beyond(part).wait_recv()
+
+    @pl.when(has_far)
+    def _():
+        ahead(0, d_far)
+
+    ahead(1, d_mate)
+
+    with jax.named_scope("sky1"):
+
+        @pl.when(has_beyond)
+        def _():
+            sky_beyond(parts - 1).wait_recv()
+
+    weight_copy().start()
+
+    def complete(g, d, j, result_ref):
+        if g == 2:
+            forward(d, j, result_ref, range(parts))
+        else:
+            forward(d, j, result_ref, range(parts - 1, parts), early.at[g, j])
 
     def give(g, d):
         def step(jj, carry):
-            forward(d, theirs + jj, part_send.at[g, jj])
+            complete(g, d, theirs + jj, part_send.at[g, jj])
             part_copy(g, jj).start()
             return carry
 
@@ -374,7 +416,7 @@
 
     def take(g, d, after):
         def step(jj, carry):
-            forward(d, mine + jj, totals.at[g, jj])
+            complete(g, d, mine + jj, totals.at[g, jj])
             part_copy(g, jj).wait_recv()
             after(jj)
             return carry
@@ -427,79 +469,89 @@
                     raw_copy(to_fed, jj, k).wait_recv()
                     pass_one(jj, k, True)
 
-    with jax.named_scope("scale"):
-        weight_copy().wait_recv()
-        for jj in range(half_slots):
-            from_odd, slot, live = pointing(1, mine + jj)
-            used = meta_all[1, from_odd, slot, 3 + 2 * slots_uv]
-            here = from_odd == core
-            for k in range(slots_uv):
-                weight = jnp.where(here, weight_ref[slot, k], weight_got[slot, k]).astype(F32)
-                weight = weight * jnp.where(k < used, 1.0, 0.0).astype(F32)
-                sum_copy(jj, k).wait_recv()
-                total = totals[2, jj, k] + sum_got[jj, k].astype(F32)
-                scaled_own[2, jj, k] = (total * wide(weight, 2 * block)).astype(BF16)
-                scaled_copy(jj, k).start()
-            par_copy(2, jj).start()
-
-    def adjoint_group(g, d):
-        def step_mine(jj, carry):
-            adjoint(d, mine + jj, scaled_own.at[g, jj])
-            return carry
-
-        def step_theirs(jj, carry):
+    def adjoint_mine(g, d, jj):
+        adjoint(d, mine + jj, scaled_own.at[g, jj])
+
+    def adjoint_theirs(g, d):
+        def step(jj, carry):
             par_copy(g, jj).wait_recv()
             adjoint(d, theirs + jj, scaled_par.at[g, jj])
             return carry
 
-        return step_mine, step_theirs
-
-    with jax.named_scope("adj_own"):
-        for step in adjoint_group(2, 1):
+        with jax.named_scope(f"theirs{g}"):
             lax.fori_loop(0, half_slots, step, 0)
 
-    with jax.named_scope("pass_scaled"):
-        for jj in range(half_slots):
-            for k in range(slots_uv):
-                scaled_copy(jj, k).wait_recv()
-
-                @pl.when(has_fed)
-                def _(jj=jj, k=k):
-                    onward_copy(to_fed, jj, k).start()
-
-            par_copy(1, jj).start()
-
-    with jax.named_scope("adj_mate"):
-        for step in adjoint_group(1, d_mate):
-            lax.fori_loop(0, half_slots, step, 0)
-
-    with jax.named_scope("adj_far"):
-        @pl.when(has_far)
-        def _():
-            step_mine, step_theirs = adjoint_group(0, d_far)
-
-            def step(jj, carry):
-                for k in range(slots_uv):
-                    onward_copy(to_giving, jj, k).wait_recv()
-                par_copy(0, jj).start()
-                return step_mine(jj, carry)
-
-            lax.fori_loop(0, half_slots, step, 0)
-            lax.fori_loop(0, half_slots, step_theirs, 0)
+    weight_copy().wait_recv()
+
+    def scale_step(jj, carry):
+        from_odd, slot, live = pointing(1, mine + jj)
+        used = meta_all[1, from_odd, slot, 3 + 2 * slots_uv]
+        here = from_odd == core
+        for k in range(slots_uv):
+            weight = jnp.where(here, weight_ref[slot, k], weight_got[slot, k]).astype(F32)
+            weight = weight * jnp.where(k < used, 1.0, 0.0).astype(F32)
+            sum_copy(jj, k).wait_recv()
+            total = totals[2, jj, k] + sum_got[jj, k].astype(F32)
+            scaled_own[2, jj, k] = (total * wide(weight, 2 * block)).astype(BF16)
+            scaled_copy(jj, k).start()
+        par_copy(2, jj).start()
+        adjoint_mine(2, 1, jj)
+        return carry
+
+    with jax.named_scope("scale"):
+        lax.fori_loop(0, half_slots, scale_step, 0)
+
+    adjoint_theirs(2, 1)
+
+    def mate_step(jj, carry):
+        for k in range(slots_uv):
+            scaled_copy(jj, k).wait_recv()
+
+            @pl.when(has_fed)
+            def _():
+                onward_copy(to_fed, jj, k).start()
+
+        par_copy(1, jj).start()
+        adjoint_mine(1, d_mate, jj)
+        return carry
+
+    with jax.named_scope("mate"):
+        lax.fori_loop(0, half_slots, mate_step, 0)
+
+    adjoint_theirs(1, d_mate)
+
+    def far_step(jj, carry):
+        for k in range(slots_uv):
+            onward_copy(to_giving, jj, k).wait_recv()
+        par_copy(0, jj).start()
+        adjoint_mine(0, d_far, jj)
+        return carry
+
+    @pl.when(has_far)
+    def _():
+        with jax.named_scope("far"):
+            lax.fori_loop(0, half_slots, far_step, 0)
+        adjoint_theirs(0, d_far)
 
     @pl.when(has_beyond)
     def _():
         edge_send[...] = acc_outer[...].astype(BF16)
         last_edge().start()
 
+    inner_send[...] = acc_inner[...].astype(BF16)
     last_inner().start()
+
+    @pl.when(jnp.logical_not(has_beyond))
+    def _():
+        no_edge().start()
 
     sky_partner().wait_send()
     weight_copy().wait_send()
 
     @pl.when(has_beyond)
     def _():
-        sky_beyond().wait_send()
+        for part in range(size // CHUNK):
+            sky_beyond(part).wait_send()
 
     for side in range(2):
 
@@ -534,17 +586,32 @@
         def _():
             last_edge().wait()
 
-
-def add_kernel(inner_ref, edge_ref, out_hbm, out_ref, sems):
+        @pl.when(jnp.logical_not(has_beyond))
+        def _():
+            no_edge().wait()
+
+
+def add_kernel(inner_hbm, edge_hbm, out_hbm, inner_ref, edge_ref, out_ref, sems):
     band = out_ref.shape[0] // BANDS
-    copies = []
-    for i in range(BANDS):
-        rows = slice(i * band, (i + 1) * band)
-        out_ref[rows, :] = inner_ref[rows, :] + edge_ref[rows, :].astype(F32)
-        copies.append(pltpu.make_async_copy(out_ref.at[rows], out_hbm.at[rows], sems.at[i]))
-        copies[-1].start()
-    for copy in copies:
-        copy.wait()
+    bands = [slice(i * band, (i + 1) * band) for i in range(BANDS)]
+    moves = [
+        [
+            pltpu.make_async_copy(inner_hbm.at[rows], inner_ref.at[rows], sems.at[0, i]),
+            pltpu.make_async_copy(edge_hbm.at[rows], edge_ref.at[rows], sems.at[1, i]),
+            pltpu.make_async_copy(out_ref.at[rows], out_hbm.at[rows], sems.at[2, i]),
+        ]
+        for i, rows in enumerate(bands)
+    ]
+    for inner, edge, out in moves:
+        inner.start()
+        edge.start()
+    for rows, (inner, edge, out) in zip(bands, moves):
+        inner.wait()
+        edge.wait()
+        out_ref[rows, :] = inner_ref[rows, :].astype(F32) + edge_ref[rows, :].astype(F32)
+        out.start()
+    for inner, edge, out in moves:
+        out.wait()
 
 
 def shards(sky, point_count, point_offset, beam_width, uv_bins, uv_count, uv_weight):
@@ -556,7 +623,7 @@
     seeds = seed_tables(length, FINE)
     count = point_count.reshape(1, 1)
     offset = jnp.transpose(point_offset, (0, 1, 3, 2)).reshape(2, slots)
-    width = beam_width.astype(I32).reshape(1, slots)
+    width = beam_width.reshape(1, slots)
     bins = jnp.transpose(uv_bins, (0, 1, 3, 4, 2)).reshape(slots_uv, 2, slots)
     used = uv_count.reshape(1, slots)
     weight = uv_weight.reshape(slots, slots_uv, block, block)
@@ -566,13 +633,12 @@
     tile = pltpu.VMEM((size, size), BF16)
     plane = pltpu.VMEM((size, size), F32)
     patch = (slots_uv, block, 2 * block)
-    vmem = pl.BlockSpec(memory_space=pltpu.VMEM)
+    smem, anywhere = pl.BlockSpec(memory_space=pltpu.SMEM), pl.BlockSpec(memory_space=pl.ANY)
     inner, edge = pl.pallas_call(
         kernel,
-        out_shape=(jax.ShapeDtypeStruct((size, size), F32), jax.ShapeDtypeStruct((size, size), BF16)),
-        in_specs=[pl.BlockSpec(memory_space=pltpu.SMEM)] * 5
-        + [pl.BlockSpec(memory_space=pl.ANY)] * 3,
-        out_specs=(vmem, vmem),
+        out_shape=(jax.ShapeDtypeStruct((size, size), BF16),) * 2,
+        in_specs=[smem, smem, pl.BlockSpec(memory_space=pltpu.VMEM), smem, smem] + [anywhere] * 3,
+        out_specs=(anywhere, anywhere),
         scratch_shapes=[
             pltpu.SMEM(meta_shape, I32),
             tuple([pltpu.SMEM(meta_shape, I32)] * 5),
@@ -591,6 +657,7 @@
             pltpu.VMEM((depth, size), BF16),
             pltpu.VMEM((3, slots, 2, 8, size), F32),
             pltpu.VMEM((3, slots, size, 128), F32),
+            pltpu.VMEM((2, slots) + patch, F32),
             pltpu.VMEM((3, half_slots) + patch, F32),
             pltpu.VMEM((3, half_slots) + patch, F32),
             pltpu.VMEM((3, half_slots) + patch, F32),
@@ -603,9 +670,10 @@
             plane,
             plane,
             tile,
-            dma((3,)),
+            tile,
+            dma((4,)),
             dma((2, 5)),
-            dma((2, 2)),
+            dma((2, 1 + size // CHUNK)),
             dma((2, 1)),
             dma((2, 3, half_slots)),
             dma((2, half_slots, slots_uv)),
@@ -622,10 +690,10 @@
     return pl.pallas_call(
         add_kernel,
         out_shape=jax.ShapeDtypeStruct((size, size), F32),
-        in_specs=[vmem, vmem],
-        out_specs=pl.BlockSpec(memory_space=pl.ANY),
-        scratch_shapes=[plane, dma((BANDS,))],
-        compiler_params=pltpu.CompilerParams(vmem_limit_bytes=8 * 1024 * 1024),
+        in_specs=[anywhere, anywhere],
+        out_specs=anywhere,
+        scratch_shapes=[tile, tile, plane, dma((3, BANDS))],
+        compiler_params=pltpu.CompilerParams(vmem_limit_bytes=56 * 1024 * 1024),
         cost_estimate=pl.CostEstimate(flops=size * size, bytes_accessed=10 * size * size, transcendentals=0),
     )(inner, edge)
 

time: 51.9 us -> 48.8 us (0.940)
  local copies, waits for them, and re-layouts: 2.91 us -> 0 us
    unnamed x6 -> x0, local copies, waits for them, and re-layouts: 2.91 us -> none
    pallas_call x1, Pallas kernels: 1.02 us -> 2.12 us  [shards(): pl.pallas_call(add_kernel, out_shape=jax.ShapeDtypeStruct((size, size), F...]
    pallas_call x1, Pallas kernels: 46.5 us -> 45.7 us  [shards(): pl.pallas_call(kernel, out_shape=(jax.ShapeDtypeStruct((size, size), BF16...]
where the time goes in v5:
time: 48.8 us; the launch traced here: 48.5 us
  Pallas kernels  47.8 us (98%)
  between operations  0.66 us (1%)
    pallas_call x1, Pallas kernels, shards(): pl.pallas_call(kernel, out_shape=(jax.ShapeDtypeStruct((size, size), BF16...  45.7 us
    pallas_call x1, Pallas kernels, shards(): pl.pallas_call(add_kernel, out_shape=jax.ShapeDtypeStruct((size, size), F...  2.12 us

profile of v5, /device:TPU:13, one launch (start us, length us, event | category | flops | bytes accessed | tf_op | source)
XLA Modules:
  0.0 48.5 jit_solution(9129089253647175082)
XLA Ops:
  0.7 45.7 %shard_map.82 = (bf16[512,512]{1,0:T(8,128)(2,1)}, bf16[512,512]{1,0:T(8,128)(2,1)}) custom-call(s32[1,1]{1,0:T(1,128)S(6)} %copy.9.count_in, s32[2,4]{1,0:T(2,128)} %bitcast.11, bf16[1,4]{1,0:T(2,128)(2,1)} %bitcast.12, s32[2,2,4]{2,1,0:T(2,128)} %bitcast.10, s32[1,4]{1,0:T(1,128)} %bitcast.13, f32[2,64,1024]{2,1,0:T(8,128)} %constant.2.clone.seeds_in, ...), custom_call_target="tpu_custom_call" | custom-call | tf_op jit(solution)/shard_map/pallas_call | solution.py:637
  46.4 2.1 %shard_map.83 = f32[512,512]{1,0:T(8,128)} custom-call(bf16[512,512]{1,0:T(8,128)(2,1)} %get-tuple-element.7.inner_hbm, bf16[512,512]{1,0:T(8,128)(2,1)} %get-tuple-element.8.edge_hbm), custom_call_target="tpu_custom_call" | custom-call | flops 262144 | bytes 2621440 | tf_op jit(solution)/shard_map/pallas_call | solution.py:690

commit v6 on v5

--- a/solution.py
+++ b/solution.py
@@ -36,8 +36,8 @@
     inner_got, edge_got,
     meta_ref, meta_got, meta_all, sky_ref, outer_ref, inner_ref, weight_ref, weight_got,
     seeds_ref, row_tab, flip_tab, col_tab,
-    beamed_ref, first_ref, spread_ref, gx_ref, gy_ref,
-    early, part_send, part_got, totals, raw_send, raw_got, sum_send, sum_got,
+    beamed, first, spread, gx_ref, gy_ref,
+    part_send, part_got, totals, raw_send, raw_got, sum_send, sum_got,
     scaled_own, scaled_par, acc_outer, acc_inner, edge_send, inner_send,
     local_sems, meta_sems, sky_sems, weight_sems, part_sems, raw_sems, sum_sems, scaled_sems,
     onward_sems, par_sems, last_sems,
@@ -103,9 +103,8 @@
     def sky_partner():
         return remote(sky_ref, inner_ref, sky_sems, (0,), to_partner)
 
-    def sky_beyond(part):
-        cols = slice(part * CHUNK, (part + 1) * CHUNK)
-        return remote(sky_ref.at[:, cols], outer_ref.at[:, cols], sky_sems, (1 + part,), to_beyond)
+    def sky_beyond():
+        return remote(sky_ref, outer_ref, sky_sems, (1,), to_beyond)
 
     def weight_copy():
         return remote(weight_ref, weight_got, weight_sems, (0,), to_partner)
@@ -129,8 +128,10 @@
             scaled_own.at[1, jj, k], scaled_own.at[0, jj, k], onward_sems, (jj, k), target
         )
 
-    def par_copy(g, jj):
-        return remote(scaled_own.at[g, jj], scaled_par.at[g, jj], par_sems, (g, jj), to_partner)
+    def par_copy(g, jj, k):
+        return remote(
+            scaled_own.at[g, jj, k], scaled_par.at[g, jj, k], par_sems, (g, jj, k), to_partner
+        )
 
     def last_edge():
         return remote(edge_send, edge_got, last_sems, (0,), to_beyond)
@@ -191,8 +192,7 @@
 
     @pl.when(has_beyond)
     def _():
-        for part in range(size // CHUNK):
-            sky_beyond(part).start()
+        sky_beyond().start()
 
     sky_partner().start()
     meta_partner().start()
@@ -313,38 +313,37 @@
     def column_table(d, from_odd, slot, k):
         return col_tab[bins(d, from_odd, slot, k, 1)]
 
-    def forward(d, j, result_ref, parts, before_ref=None):
+    def prepare(d, j, beamed_ref):
+        gy = wide(gy_ref[d, j], CHUNK)
+        for at in range(0, size, CHUNK):
+            cols = slice(at, at + CHUNK)
+            value = gx_ref[d, j, 0, 0:1, cols] * outer_ref[:, cols].astype(F32)
+            value = value + gx_ref[d, j, 1, 0:1, cols] * inner_ref[:, cols].astype(F32)
+            beamed_ref[:, cols] = (gy * value).astype(BF16)
+
+    def multiply(d, j, beamed_ref, first_ref, result_ref):
         from_odd, slot, live = pointing(d, j)
         rows = jnp.concatenate(
             [row_tab[bins(d, from_odd, slot, k, 0)] for k in range(slots_uv)], axis=0
         )
-        gy = wide(gy_ref[d, j], CHUNK)
-        for part in parts:
-            cols = slice(part * CHUNK, (part + 1) * CHUNK)
-            value = gx_ref[d, j, 0, 0:1, cols] * outer_ref[:, cols].astype(F32)
-            value = value + gx_ref[d, j, 1, 0:1, cols] * inner_ref[:, cols].astype(F32)
-            beamed_ref[:, cols] = (gy * value).astype(BF16)
-        for part in parts:
-            cols = slice(part * CHUNK, (part + 1) * CHUNK)
+        for at in range(0, size, CHUNK):
+            cols = slice(at, at + CHUNK)
             first_ref[:, cols] = jnp.dot(
                 rows, beamed_ref[:, cols], preferred_element_type=F32
             ).astype(BF16)
-        cols = slice(parts[0] * CHUNK, (parts[-1] + 1) * CHUNK)
         for k in range(slots_uv):
             both = lax.dot_general(
-                first_ref[2 * k * block : (2 * k + 2) * block, cols],
-                col_tab[bins(d, from_odd, slot, k, 1), :, cols],
+                first_ref[2 * k * block : (2 * k + 2) * block, :],
+                col_tab[bins(d, from_odd, slot, k, 1)],
                 (((1,), (1,)), ((), ())),
                 preferred_element_type=F32,
             )
             real = both[:block, :block] - both[block:, block:]
             turned = both[:block, block:] + both[block:, :block]
-            if before_ref is not None:
-                real, turned = real + before_ref[k, :, :block], turned + before_ref[k, :, block:]
-            result_ref[k, :, :block] = real
-            result_ref[k, :, block:] = turned
-
-    def adjoint(d, j, scaled_ref):
+            result_ref[k, :, :block] = real.astype(result_ref.dtype)
+            result_ref[k, :, block:] = turned.astype(result_ref.dtype)
+
+    def adjoint(d, j, scaled_ref, spread_ref):
         from_odd, slot, live = pointing(d, j)
         rows = jnp.concatenate(
             [flip_tab[bins(d, from_odd, slot, k, 0)] for k in range(slots_uv)], axis=1
@@ -367,98 +366,58 @@
 
     mine, theirs = half_slots * core, half_slots * (1 - core)
 
-    parts = size // CHUNK
-
-    def ahead(g, d):
-        def step(j, carry):
-            forward(d, j, early.at[g, j], range(parts - 1))
-            return carry
-
-        with jax.named_scope(f"ahead{g}"):
-            lax.fori_loop(0, slots, step, 0)
-
-    with jax.named_scope("sky0"):
+    with jax.named_scope("sky"):
         sky_partner().wait_recv()
 
         @pl.when(has_beyond)
         def _():
-            for part in range(parts - 1):
-                sky_beyond(part).wait_recv()
-
-    @pl.when(has_far)
-    def _():
-        ahead(0, d_far)
-
-    ahead(1, d_mate)
-
-    with jax.named_scope("sky1"):
-
-        @pl.when(has_beyond)
-        def _():
-            sky_beyond(parts - 1).wait_recv()
+            sky_beyond().wait_recv()
 
     weight_copy().start()
 
-    def complete(g, d, j, result_ref):
-        if g == 2:
-            forward(d, j, result_ref, range(parts))
-        else:
-            forward(d, j, result_ref, range(parts - 1, parts), early.at[g, j])
-
-    def give(g, d):
-        def step(jj, carry):
-            complete(g, d, theirs + jj, part_send.at[g, jj])
-            part_copy(g, jj).start()
-            return carry
-
-        with jax.named_scope(f"give{g}"):
-            lax.fori_loop(0, half_slots, step, 0)
-
-    def take(g, d, after):
-        def step(jj, carry):
-            complete(g, d, mine + jj, totals.at[g, jj])
-            part_copy(g, jj).wait_recv()
-            after(jj)
-            return carry
-
-        with jax.named_scope(f"take{g}"):
-            lax.fori_loop(0, half_slots, step, 0)
-
-    def give_far(jj):
-        for k in range(slots_uv):
-            raw_send[jj, k] = (totals[0, jj, k] + part_got[0, jj, k]).astype(BF16)
-            raw_copy(to_giving, jj, k).start()
-
-    def keep(g):
-        def add(jj):
-            totals[g, jj] = totals[g, jj] + part_got[g, jj]
-
-        return add
-
-    @pl.when(has_far)
-    def _():
-        give(0, d_far)
-        take(0, d_far, give_far)
-
-    def pass_one(jj, k, fed_too):
-        value = totals[1, jj, k]
-        if fed_too:
-            value = value + raw_got[jj, k].astype(F32)
+    def pass_sum(jj, k, value):
         sum_send[jj, k] = value.astype(BF16)
         sum_copy(jj, k).start()
 
-    def give_mate(jj):
-        totals[1, jj] = totals[1, jj] + part_got[1, jj]
-
-        @pl.when(jnp.logical_not(has_fed))
-        def _():
+    def row_of(g):
+        own = g // 2
+        return 2 * (odd_row * (1 - g) + (1 - odd_row) * g) * (1 - own) + own
+
+    order = [(theirs, jj) for jj in range(half_slots)] + [(mine, jj) for jj in range(half_slots)]
+
+    def forward_group(g, carry):
+        d, d_next = row_of(g), row_of(g + 1)
+        for i, (base, jj) in enumerate(order):
+            result = part_send.at[g, jj] if i < half_slots else totals.at[g, jj]
+            multiply(d, base + jj, beamed[i % 2], first[i % 2], result)
+            if i < half_slots:
+                part_copy(g, jj).start()
+            if i + 1 < len(order):
+                prepare(d, order[i + 1][0] + order[i + 1][1], beamed[(i + 1) % 2])
+            else:
+                prepare(d_next, theirs, beamed[(i + 1) % 2])
+        for jj in range(half_slots):
+            part_copy(g, jj).wait_recv()
             for k in range(slots_uv):
-                pass_one(jj, k, False)
-
-    give(1, d_mate)
-    take(1, d_mate, give_mate)
-    give(2, 1)
-    take(2, 1, keep(2))
+                totals[g, jj, k] = totals[g, jj, k] + part_got[g, jj, k].astype(F32)
+
+            @pl.when(g == 0)
+            def _(jj=jj):
+                for k in range(slots_uv):
+                    raw_send[jj, k] = totals[0, jj, k].astype(BF16)
+                    raw_copy(to_giving, jj, k).start()
+
+            @pl.when(jnp.logical_and(g == 1, jnp.logical_not(has_fed)))
+            def _(jj=jj):
+                for k in range(slots_uv):
+                    pass_sum(jj, k, totals[1, jj, k])
+
+        return carry
+
+    g_first = 1 - has_far.astype(I32)
+    with jax.named_scope("forward"):
+        prepare(row_of(g_first), theirs, beamed[0])
+        lax.fori_loop(g_first, 3, forward_group, 0)
 
     with jax.named_scope("pass_sums"):
 
@@ -467,19 +426,18 @@
             for jj in range(half_slots):
                 for k in range(slots_uv):
                     raw_copy(to_fed, jj, k).wait_recv()
-                    pass_one(jj, k, True)
+                    pass_sum(jj, k, totals[1, jj, k] + raw_got[jj, k].astype(F32))
 
     def adjoint_mine(g, d, jj):
-        adjoint(d, mine + jj, scaled_own.at[g, jj])
+        adjoint(d, mine + jj, scaled_own.at[g, jj], spread[0])
 
     def adjoint_theirs(g, d):
-        def step(jj, carry):
-            par_copy(g, jj).wait_recv()
-            adjoint(d, theirs + jj, scaled_par.at[g, jj])
-            return carry
-
         with jax.named_scope(f"theirs{g}"):
-            lax.fori_loop(0, half_slots, step, 0)
+            for jj in range(half_slots):
+                for k in range(slots_uv):
+                    par_copy(g, jj, k).wait_recv()
+            for jj in range(half_slots):
+                adjoint(d, theirs + jj, scaled_par.at[g, jj], spread[jj % 2])
 
     weight_copy().wait_recv()
 
@@ -493,8 +451,8 @@
             sum_copy(jj, k).wait_recv()
             total = totals[2, jj, k] + sum_got[jj, k].astype(F32)
             scaled_own[2, jj, k] = (total * wide(weight, 2 * block)).astype(BF16)
+            par_copy(2, jj, k).start()
             scaled_copy(jj, k).start()
-        par_copy(2, jj).start()
         adjoint_mine(2, 1, jj)
         return carry
 
@@ -506,12 +464,12 @@
     def mate_step(jj, carry):
         for k in range(slots_uv):
             scaled_copy(jj, k).wait_recv()
+            par_copy(1, jj, k).start()
 
             @pl.when(has_fed)
-            def _():
+            def _(k=k):
                 onward_copy(to_fed, jj, k).start()
 
-        par_copy(1, jj).start()
         adjoint_mine(1, d_mate, jj)
         return carry
 
@@ -523,7 +481,7 @@
     def far_step(jj, carry):
         for k in range(slots_uv):
             onward_copy(to_giving, jj, k).wait_recv()
-        par_copy(0, jj).start()
+            par_copy(0, jj, k).start()
         adjoint_mine(0, d_far, jj)
         return carry
 
@@ -550,8 +508,7 @@
 
     @pl.when(has_beyond)
     def _():
-        for part in range(size // CHUNK):
-            sky_beyond(part).wait_send()
+        sky_beyond().wait_send()
 
     for side in range(2):
 
@@ -563,7 +520,8 @@
     for jj in range(half_slots):
         for g in (1, 2):
             part_copy(g, jj).wait_send()
-            par_copy(g, jj).wait_send()
+            for k in range(slots_uv):
+                par_copy(g, jj, k).wait_send()
         for k in range(slots_uv):
             sum_copy(jj, k).wait_send()
             scaled_copy(jj, k).wait_send()
@@ -575,8 +533,8 @@
         @pl.when(has_far)
         def _(jj=jj):
             part_copy(0, jj).wait_send()
-            par_copy(0, jj).wait_send()
             for k in range(slots_uv):
+                par_copy(0, jj, k).wait_send()
                 raw_copy(to_giving, jj, k).wait_send()
 
     with jax.named_scope("last"):
@@ -652,14 +610,13 @@
             pltpu.VMEM((length // block, 2 * block, size), BF16),
             pltpu.VMEM((length // block, size, 2 * block), BF16),
             pltpu.VMEM((length // block, 2 * block, size), BF16),
-            tile,
-            pltpu.VMEM((depth, size), BF16),
-            pltpu.VMEM((depth, size), BF16),
+            (tile, tile),
+            (pltpu.VMEM((depth, size), BF16),) * 2,
+            (pltpu.VMEM((depth, size), BF16),) * 2,
             pltpu.VMEM((3, slots, 2, 8, size), F32),
             pltpu.VMEM((3, slots, size, 128), F32),
-            pltpu.VMEM((2, slots) + patch, F32),
-            pltpu.VMEM((3, half_slots) + patch, F32),
-            pltpu.VMEM((3, half_slots) + patch, F32),
+            pltpu.VMEM((3, half_slots) + patch, BF16),
+            pltpu.VMEM((3, half_slots) + patch, BF16),
             pltpu.VMEM((3, half_slots) + patch, F32),
             pltpu.VMEM((half_slots,) + patch, BF16),
             pltpu.VMEM((half_slots,) + patch, BF16),
@@ -673,14 +630,14 @@
             tile,
             dma((4,)),
             dma((2, 5)),
-            dma((2, 1 + size // CHUNK)),
+            dma((2, 2)),
             dma((2, 1)),
             dma((2, 3, half_slots)),
             dma((2, half_slots, slots_uv)),
             dma((2, half_slots, slots_uv)),
             dma((2, half_slots, slots_uv)),
             dma((2, half_slots, slots_uv)),
-            dma((2, 3, half_slots)),
+            dma((2, 3, half_slots, slots_uv)),
             dma((2, 2)),
         ],
         compiler_params=pltpu.CompilerParams(

time: 48.8 us -> 49 us (level)
  no operation moved by 1% of the time
where the time goes in v6:
time: 49 us; the launch traced here: 48.7 us
  Pallas kernels  48.1 us (98%)
  between operations  0.66 us (1%)
    pallas_call x1, Pallas kernels, shards(): pl.pallas_call(kernel, out_shape=(jax.ShapeDtypeStruct((size, size), BF16...  46 us
    pallas_call x1, Pallas kernels, shards(): pl.pallas_call(add_kernel, out_shape=jax.ShapeDtypeStruct((size, size), F...  2.12 us

profile of v6, /device:TPU:13, one launch (start us, length us, event | category | flops | bytes accessed | tf_op | source)
XLA Modules:
  0.0 48.7 jit_solution(13829014632958973176)
XLA Ops:
  0.7 46.0 %shard_map.82 = (bf16[512,512]{1,0:T(8,128)(2,1)}, bf16[512,512]{1,0:T(8,128)(2,1)}) custom-call(s32[1,1]{1,0:T(1,128)S(6)} %copy.9.count_in, s32[2,4]{1,0:T(2,128)} %bitcast.11, bf16[1,4]{1,0:T(2,128)(2,1)} %bitcast.12, s32[2,2,4]{2,1,0:T(2,128)} %bitcast.10, s32[1,4]{1,0:T(1,128)} %bitcast.13, f32[2,64,1024]{2,1,0:T(8,128)} %constant.2.clone.seeds_in, ...), custom_call_target="tpu_custom_call" | custom-call | tf_op jit(solution)/shard_map/pallas_call | solution.py:595
  46.6 2.1 %shard_map.83 = f32[512,512]{1,0:T(8,128)} custom-call(bf16[512,512]{1,0:T(8,128)(2,1)} %get-tuple-element.7.inner_hbm, bf16[512,512]{1,0:T(8,128)(2,1)} %get-tuple-element.8.edge_hbm), custom_call_target="tpu_custom_call" | custom-call | flops 262144 | bytes 2621440 | tf_op jit(solution)/shard_map/pallas_call | solution.py:647

commit v7 on v6

--- a/solution.py
+++ b/solution.py
@@ -383,41 +383,42 @@
         own = g // 2
         return 2 * (odd_row * (1 - g) + (1 - odd_row) * g) * (1 - own) + own
 
-    order = [(theirs, jj) for jj in range(half_slots)] + [(mine, jj) for jj in range(half_slots)]
-
-    def forward_group(g, carry):
-        d, d_next = row_of(g), row_of(g + 1)
-        for i, (base, jj) in enumerate(order):
-            result = part_send.at[g, jj] if i < half_slots else totals.at[g, jj]
-            multiply(d, base + jj, beamed[i % 2], first[i % 2], result)
-            if i < half_slots:
-                part_copy(g, jj).start()
-            if i + 1 < len(order):
-                prepare(d, order[i + 1][0] + order[i + 1][1], beamed[(i + 1) % 2])
-            else:
-                prepare(d_next, theirs, beamed[(i + 1) % 2])
-        for jj in range(half_slots):
-            part_copy(g, jj).wait_recv()
+    def settle(g, jj):
+        part_copy(g, jj).wait_recv()
+        for k in range(slots_uv):
+            totals[g, jj, k] = totals[g, jj, k] + part_got[g, jj, k].astype(F32)
+
+        @pl.when(g == 0)
+        def _():
             for k in range(slots_uv):
-                totals[g, jj, k] = totals[g, jj, k] + part_got[g, jj, k].astype(F32)
-
-            @pl.when(g == 0)
-            def _(jj=jj):
-                for k in range(slots_uv):
-                    raw_send[jj, k] = totals[0, jj, k].astype(BF16)
-                    raw_copy(to_giving, jj, k).start()
-
-            @pl.when(jnp.logical_and(g == 1, jnp.logical_not(has_fed)))
-            def _(jj=jj):
-                for k in range(slots_uv):
-                    pass_sum(jj, k, totals[1, jj, k])
-
-        return carry
-
-    g_first = 1 - has_far.astype(I32)
+                raw_send[jj, k] = totals[0, jj, k].astype(BF16)
+                raw_copy(to_giving, jj, k).start()
+
+        @pl.when(jnp.logical_and(g == 1, jnp.logical_not(has_fed)))
+        def _():
+            for k in range(slots_uv):
+                pass_sum(jj, k, totals[1, jj, k])
+
+    far = has_far.astype(I32)
+
+    def forward_units(s, carry):
+        own = s // half_slots
+        units = (
+            (2 * own + (1 - own) * (1 - far), (1 - own) * far * s),
+            (2 * own + (1 - own), own + (1 - own) * (far * s + 1 - far)),
+        )
+        for i, (g, jj) in enumerate(units):
+            prepare(row_of(g), theirs + jj, beamed[i])
+            multiply(row_of(g), theirs + jj, beamed[i], first[i], part_send.at[g, jj])
+            part_copy(g, jj).start()
+        for i, (g, jj) in enumerate(units):
+            prepare(row_of(g), mine + jj, beamed[i])
+            multiply(row_of(g), mine + jj, beamed[i], first[i], totals.at[g, jj])
+            settle(g, jj)
+        return carry
+
     with jax.named_scope("forward"):
-        prepare(row_of(g_first), theirs, beamed[0])
-        lax.fori_loop(g_first, 3, forward_group, 0)
+        lax.fori_loop(1 - far, half_slots + 1, forward_units, 0)
 
     with jax.named_scope("pass_sums"):
 

time: 49 us -> 48 us (0.980)
  Pallas kernels: 48.1 us -> 47.2 us
    pallas_call x1, Pallas kernels: 46 us -> 45.1 us  [shards(): pl.pallas_call(kernel, out_shape=(jax.ShapeDtypeStruct((size, size), BF16...]
where the time goes in v7:
time: 48 us; the launch traced here: 47.9 us
  Pallas kernels  47.2 us (98%)
  between operations  0.66 us (1%)
    pallas_call x1, Pallas kernels, shards(): pl.pallas_call(kernel, out_shape=(jax.ShapeDtypeStruct((size, size), BF16...  45.1 us
    pallas_call x1, Pallas kernels, shards(): pl.pallas_call(add_kernel, out_shape=jax.ShapeDtypeStruct((size, size), F...  2.12 us

profile of v7, /device:TPU:13, one launch (start us, length us, event | category | flops | bytes accessed | tf_op | source)
XLA Modules:
  0.0 47.9 jit_solution(16926899093492282387)
XLA Ops:
  0.7 45.1 %shard_map.82 = (bf16[512,512]{1,0:T(8,128)(2,1)}, bf16[512,512]{1,0:T(8,128)(2,1)}) custom-call(s32[1,1]{1,0:T(1,128)S(6)} %copy.9.count_in, s32[2,4]{1,0:T(2,128)} %bitcast.11, bf16[1,4]{1,0:T(2,128)(2,1)} %bitcast.12, s32[2,2,4]{2,1,0:T(2,128)} %bitcast.10, s32[1,4]{1,0:T(1,128)} %bitcast.13, f32[2,64,1024]{2,1,0:T(8,128)} %constant.2.clone.seeds_in, ...), custom_call_target="tpu_custom_call" | custom-call | tf_op jit(solution)/shard_map/pallas_call | solution.py:596
  45.7 2.1 %shard_map.83 = f32[512,512]{1,0:T(8,128)} custom-call(bf16[512,512]{1,0:T(8,128)(2,1)} %get-tuple-element.7.inner_hbm, bf16[512,512]{1,0:T(8,128)(2,1)} %get-tuple-element.8.edge_hbm), custom_call_target="tpu_custom_call" | custom-call | flops 262144 | bytes 2621440 | tf_op jit(solution)/shard_map/pallas_call | solution.py:648

commit v8 on v7

--- a/solution.py
+++ b/solution.py
@@ -36,11 +36,11 @@
     inner_got, edge_got,
     meta_ref, meta_got, meta_all, sky_ref, outer_ref, inner_ref, weight_ref, weight_got,
     seeds_ref, row_tab, flip_tab, col_tab,
-    beamed, first, spread, gx_ref, gy_ref,
-    part_send, part_got, totals, raw_send, raw_got, sum_send, sum_got,
-    scaled_own, scaled_par, acc_outer, acc_inner, edge_send, inner_send,
-    local_sems, meta_sems, sky_sems, weight_sems, part_sems, raw_sems, sum_sems, scaled_sems,
-    onward_sems, par_sems, last_sems,
+    beamed, first, spread, gx_ref, gy_ref, gx_half, gy_half,
+    part_send, part_got, totals, raw_send, raw_got, own_send, own_got,
+    sum_send, sum_got, back_send, back_got, weights, scaled_own, scaled_par, acc_outer, acc_inner, edge_send, inner_send,
+    local_sems, meta_sems, sky_sems, weight_sems, part_sems, raw_sems, own_sems, sum_sems,
+    back_sems, par_sems, last_sems,
 ):
     size = sky_ref.shape[0]
     length = 2 * size
@@ -66,6 +66,7 @@
     has_far = jnp.logical_and(giving >= 0, giving < ny)
     has_fed = jnp.logical_and(fed >= 0, fed < ny)
     to_mate, to_giving, to_fed = {"ty": ty + 1 - 2 * odd_row}, {"ty": giving}, {"ty": fed}
+    to_far = {"ty": ty - 1 + 2 * odd_row}
 
     local = [
         pltpu.make_async_copy(source, target, local_sems.at[i])
@@ -115,18 +116,20 @@
     def raw_copy(target, jj, k):
         return remote(raw_send.at[jj, k], raw_got.at[jj, k], raw_sems, (jj, k), target)
 
+    def own_copy(jj, k):
+        return remote(own_send.at[jj, k], own_got.at[jj, k], own_sems, (jj, k), to_mate)
+
     def sum_copy(jj, k):
         return remote(sum_send.at[jj, k], sum_got.at[jj, k], sum_sems, (jj, k), to_mate)
 
-    def scaled_copy(jj, k):
-        return remote(
-            scaled_own.at[2, jj, k], scaled_own.at[1, jj, k], scaled_sems, (jj, k), to_mate
-        )
-
-    def onward_copy(target, jj, k):
-        return remote(
-            scaled_own.at[1, jj, k], scaled_own.at[0, jj, k], onward_sems, (jj, k), target
-        )
+    def back_copy(target, jj, k):
+        return remote(back_send.at[jj, k], back_got.at[jj, k], back_sems, (jj, k), target)
+
+    def weights_mate():
+        return remote(weights.at[2], weights.at[1], weight_sems, (1,), to_mate)
+
+    def weights_far():
+        return remote(weights.at[2], weights.at[0], weight_sems, (2,), to_far)
 
     def par_copy(g, jj, k):
         return remote(
@@ -205,6 +208,7 @@
 
     for copy in local[1:]:
         copy.wait()
+    weight_copy().start()
 
     acc_outer[...] = jnp.zeros_like(acc_outer)
     acc_inner[...] = jnp.zeros_like(acc_inner)
@@ -301,11 +305,31 @@
         oy, ox = meta_all[d, from_odd, slot, 0], meta_all[d, from_odd, slot, 1]
         width = jnp.full((8, 128), meta_all[d, from_odd, slot, 2], I32).astype(F32)
         decay = 1.0 / (2.0 * width * width)
-        gy_ref[d, j] = gaussian((size, 128), 0, (1 - d) * size - oy, decay, live)
+        gy = gaussian((size, 128), 0, (1 - d) * size - oy, decay, live)
+        gy_ref[d, j] = gy
+        gy_half[d, j] = gy.astype(BF16)
         outer_at, inner_at = 3 * core - 1, 1 - core
-        gx_ref[d, j, 0] = gaussian((8, size), 1, (outer_at - from_odd) * size - ox, decay, live)
-        gx_ref[d, j, 1] = gaussian((8, size), 1, (inner_at - from_odd) * size - ox, decay, live)
+        for i, tile_at in enumerate((outer_at, inner_at)):
+            gx = gaussian((8, size), 1, (tile_at - from_odd) * size - ox, decay, live)
+            gx_ref[d, j, i] = gx
+            gx_half[d, j, i] = jnp.concatenate([gx, gx], axis=0).astype(BF16)
         return carry
+
+    with jax.named_scope("weights"):
+        weight_copy().wait_recv()
+        for jj in range(half_slots):
+            from_odd, slot, live = pointing(1, half_slots * core + jj)
+            used = meta_all[1, from_odd, slot, 3 + 2 * slots_uv]
+            for k in range(slots_uv):
+                weight = jnp.where(from_odd == core, weight_ref[slot, k], weight_got[slot, k])
+                weight = weight.astype(F32) * jnp.where(k < used, 1.0, 0.0).astype(F32)
+                weights[2, jj, k] = weight.astype(BF16)
+
+        weights_mate().start()
+
+        @pl.when(has_far)
+        def _():
+            weights_far().start()
 
     with jax.named_scope("beams"):
         lax.fori_loop(0, 3 * slots, beams, 0)
@@ -314,12 +338,12 @@
         return col_tab[bins(d, from_odd, slot, k, 1)]
 
     def prepare(d, j, beamed_ref):
-        gy = wide(gy_ref[d, j], CHUNK)
+        gy = wide(gy_half[d, j], CHUNK)
         for at in range(0, size, CHUNK):
             cols = slice(at, at + CHUNK)
-            value = gx_ref[d, j, 0, 0:1, cols] * outer_ref[:, cols].astype(F32)
-            value = value + gx_ref[d, j, 1, 0:1, cols] * inner_ref[:, cols].astype(F32)
-            beamed_ref[:, cols] = (gy * value).astype(BF16)
+            gx = [jnp.concatenate([gx_half[d, j, i, :, cols]] * (size // 16), axis=0) for i in range(2)]
+            value = gx[0] * outer_ref[:, cols] + gx[1] * inner_ref[:, cols]
+            beamed_ref[:, cols] = gy * value
 
     def multiply(d, j, beamed_ref, first_ref, result_ref):
         from_odd, slot, live = pointing(d, j)
@@ -373,8 +397,6 @@
         def _():
             sky_beyond().wait_recv()
 
-    weight_copy().start()
-
     def pass_sum(jj, k, value):
         sum_send[jj, k] = value.astype(BF16)
         sum_copy(jj, k).start()
@@ -394,6 +416,12 @@
                 raw_send[jj, k] = totals[0, jj, k].astype(BF16)
                 raw_copy(to_giving, jj, k).start()
 
+        @pl.when(g == 2)
+        def _():
+            for k in range(slots_uv):
+                own_send[jj, k] = totals[2, jj, k].astype(BF16)
+                own_copy(jj, k).start()
+
         @pl.when(jnp.logical_and(g == 1, jnp.logical_not(has_fed)))
         def _():
             for k in range(slots_uv):
@@ -402,10 +430,11 @@
     far = has_far.astype(I32)
 
     def forward_units(s, carry):
-        own = s // half_slots
+        end = s // half_slots
+        slot = s * (1 - end)
         units = (
-            (2 * own + (1 - own) * (1 - far), (1 - own) * far * s),
-            (2 * own + (1 - own), own + (1 - own) * (far * s + 1 - far)),
+            (2 * (1 - end) * (1 - far) + end, slot),
+            ((1 - end) * (1 + far) + end, slot + end),
         )
         for i, (g, jj) in enumerate(units):
             prepare(row_of(g), theirs + jj, beamed[i])
@@ -418,79 +447,72 @@
         return carry
 
     with jax.named_scope("forward"):
-        lax.fori_loop(1 - far, half_slots + 1, forward_units, 0)
-
-    with jax.named_scope("pass_sums"):
-
-        @pl.when(has_fed)
-        def _():
-            for jj in range(half_slots):
-                for k in range(slots_uv):
-                    raw_copy(to_fed, jj, k).wait_recv()
-                    pass_sum(jj, k, totals[1, jj, k] + raw_got[jj, k].astype(F32))
-
-    def adjoint_mine(g, d, jj):
-        adjoint(d, mine + jj, scaled_own.at[g, jj], spread[0])
-
-    def adjoint_theirs(g, d):
+        lax.fori_loop(0, half_slots + far, forward_units, 0)
+
+    def scale(g, jj, k, total):
+        weight = weights[g, jj, k].astype(F32)
+        scaled_own[g, jj, k] = (total * wide(weight, 2 * block)).astype(BF16)
+        par_copy(g, jj, k).start()
+
+    def adjoint_mine(g, jj):
+        adjoint(row_of(g), mine + jj, scaled_own.at[g, jj], spread[0])
+
+    def adjoint_theirs(g):
         with jax.named_scope(f"theirs{g}"):
             for jj in range(half_slots):
                 for k in range(slots_uv):
                     par_copy(g, jj, k).wait_recv()
             for jj in range(half_slots):
-                adjoint(d, theirs + jj, scaled_par.at[g, jj], spread[jj % 2])
-
-    weight_copy().wait_recv()
-
-    def scale_step(jj, carry):
-        from_odd, slot, live = pointing(1, mine + jj)
-        used = meta_all[1, from_odd, slot, 3 + 2 * slots_uv]
-        here = from_odd == core
-        for k in range(slots_uv):
-            weight = jnp.where(here, weight_ref[slot, k], weight_got[slot, k]).astype(F32)
-            weight = weight * jnp.where(k < used, 1.0, 0.0).astype(F32)
-            sum_copy(jj, k).wait_recv()
-            total = totals[2, jj, k] + sum_got[jj, k].astype(F32)
-            scaled_own[2, jj, k] = (total * wide(weight, 2 * block)).astype(BF16)
-            par_copy(2, jj, k).start()
-            scaled_copy(jj, k).start()
-        adjoint_mine(2, 1, jj)
-        return carry
-
-    with jax.named_scope("scale"):
-        lax.fori_loop(0, half_slots, scale_step, 0)
-
-    adjoint_theirs(2, 1)
-
-    def mate_step(jj, carry):
-        for k in range(slots_uv):
-            scaled_copy(jj, k).wait_recv()
-            par_copy(1, jj, k).start()
-
-            @pl.when(has_fed)
-            def _(k=k):
-                onward_copy(to_fed, jj, k).start()
-
-        adjoint_mine(1, d_mate, jj)
-        return carry
+                adjoint(row_of(g), theirs + jj, scaled_par.at[g, jj], spread[jj % 2])
 
     with jax.named_scope("mate"):
-        lax.fori_loop(0, half_slots, mate_step, 0)
-
-    adjoint_theirs(1, d_mate)
+        weights_mate().wait_recv()
+        for jj in range(half_slots):
+            for k in range(slots_uv):
+                own_copy(jj, k).wait_recv()
+                both = totals[1, jj, k] + own_got[jj, k].astype(F32)
+
+                @pl.when(has_fed)
+                def _(jj=jj, k=k, both=both):
+                    back_send[jj, k] = both.astype(BF16)
+                    back_copy(to_fed, jj, k).start()
+                    raw_copy(to_fed, jj, k).wait_recv()
+                    far_part = raw_got[jj, k].astype(F32)
+                    pass_sum(jj, k, totals[1, jj, k] + far_part)
+                    totals[1, jj, k] = totals[1, jj, k] + far_part
+
+                scale(1, jj, k, totals[1, jj, k] + own_got[jj, k].astype(F32))
+
+        for jj in range(half_slots):
+            adjoint_mine(1, jj)
+
+    adjoint_theirs(1)
 
     def far_step(jj, carry):
         for k in range(slots_uv):
-            onward_copy(to_giving, jj, k).wait_recv()
-            par_copy(0, jj, k).start()
-        adjoint_mine(0, d_far, jj)
+            back_copy(to_giving, jj, k).wait_recv()
+            scale(0, jj, k, totals[0, jj, k] + back_got[jj, k].astype(F32))
+        adjoint_mine(0, jj)
         return carry
 
     @pl.when(has_far)
     def _():
+        weights_far().wait_recv()
         with jax.named_scope("far"):
             lax.fori_loop(0, half_slots, far_step, 0)
-        adjoint_theirs(0, d_far)
+        adjoint_theirs(0)
+
+    def own_step(jj, carry):
+        for k in range(slots_uv):
+            sum_copy(jj, k).wait_recv()
+            scale(2, jj, k, totals[2, jj, k] + sum_got[jj, k].astype(F32))
+        adjoint_mine(2, jj)
+        return carry
+
+    with jax.named_scope("own"):
+        lax.fori_loop(0, half_slots, own_step, 0)
+
+    adjoint_theirs(2)
 
     @pl.when(has_beyond)
     def _():
@@ -524,12 +546,12 @@
             for k in range(slots_uv):
                 par_copy(g, jj, k).wait_send()
         for k in range(slots_uv):
+            own_copy(jj, k).wait_send()
             sum_copy(jj, k).wait_send()
-            scaled_copy(jj, k).wait_send()
 
             @pl.when(has_fed)
             def _(jj=jj, k=k):
-                onward_copy(to_fed, jj, k).wait_send()
+                back_copy(to_fed, jj, k).wait_send()
 
         @pl.when(has_far)
         def _(jj=jj):
@@ -537,6 +559,12 @@
             for k in range(slots_uv):
                 par_copy(0, jj, k).wait_send()
                 raw_copy(to_giving, jj, k).wait_send()
+
+    weights_mate().wait_send()
+
+    @pl.when(has_far)
+    def _():
+        weights_far().wait_send()
 
     with jax.named_scope("last"):
         last_inner().wait()
@@ -616,13 +644,13 @@
             (pltpu.VMEM((depth, size), BF16),) * 2,
             pltpu.VMEM((3, slots, 2, 8, size), F32),
             pltpu.VMEM((3, slots, size, 128), F32),
+            pltpu.VMEM((3, slots, 2, 16, size), BF16),
+            pltpu.VMEM((3, slots, size, 128), BF16),
             pltpu.VMEM((3, half_slots) + patch, BF16),
             pltpu.VMEM((3, half_slots) + patch, BF16),
             pltpu.VMEM((3, half_slots) + patch, F32),
-            pltpu.VMEM((half_slots,) + patch, BF16),
-            pltpu.VMEM((half_slots,) + patch, BF16),
-            pltpu.VMEM((half_slots,) + patch, BF16),
-            pltpu.VMEM((half_slots,) + patch, BF16),
+            *[pltpu.VMEM((half_slots,) + patch, BF16)] * 8,
+            pltpu.VMEM((3, half_slots, slots_uv, block, block), BF16),
             pltpu.VMEM((3, half_slots) + patch, BF16),
             pltpu.VMEM((3, half_slots) + patch, BF16),
             plane,
@@ -632,7 +660,7 @@
             dma((4,)),
             dma((2, 5)),
             dma((2, 2)),
-            dma((2, 1)),
+            dma((2, 3)),
             dma((2, 3, half_slots)),
             dma((2, half_slots, slots_uv)),
             dma((2, half_slots, slots_uv)),

time: 48 us -> 42.8 us (0.89)
  Pallas kernels: 47.2 us -> 41.9 us
    pallas_call x1, Pallas kernels: 45.1 us -> 39.8 us  [shards(): pl.pallas_call(kernel, out_shape=(jax.ShapeDtypeStruct((size, size), BF16...]
where the time goes in v8:
time: 42.8 us; the launch traced here: 42.6 us
  Pallas kernels  41.9 us (98%)
  between operations  0.66 us (2%)
    pallas_call x1, Pallas kernels, shards(): pl.pallas_call(kernel, out_shape=(jax.ShapeDtypeStruct((size, size), BF16...  39.8 us
    pallas_call x1, Pallas kernels, shards(): pl.pallas_call(add_kernel, out_shape=jax.ShapeDtypeStruct((size, size), F...  2.12 us

profile of v8, /device:TPU:13, one launch (start us, length us, event | category | flops | bytes accessed | tf_op | source)
XLA Modules:
  0.0 42.6 jit_solution(12463979416018284203)
XLA Ops:
  0.7 39.8 %shard_map.82 = (bf16[512,512]{1,0:T(8,128)(2,1)}, bf16[512,512]{1,0:T(8,128)(2,1)}) custom-call(s32[1,1]{1,0:T(1,128)S(6)} %copy.9.count_in, s32[2,4]{1,0:T(2,128)} %bitcast.11, bf16[1,4]{1,0:T(2,128)(2,1)} %bitcast.12, s32[2,2,4]{2,1,0:T(2,128)} %bitcast.10, s32[1,4]{1,0:T(1,128)} %bitcast.13, f32[2,64,1024]{2,1,0:T(8,128)} %constant.2.clone.seeds_in, ...), custom_call_target="tpu_custom_call" | custom-call | tf_op jit(solution)/shard_map/pallas_call | solution.py:624
  40.4 2.1 %shard_map.83 = f32[512,512]{1,0:T(8,128)} custom-call(bf16[512,512]{1,0:T(8,128)(2,1)} %get-tuple-element.7.inner_hbm, bf16[512,512]{1,0:T(8,128)(2,1)} %get-tuple-element.8.edge_hbm), custom_call_target="tpu_custom_call" | custom-call | flops 262144 | bytes 2621440 | tf_op jit(solution)/shard_map/pallas_call | solution.py:676

commit v9 on v8

--- a/solution.py
+++ b/solution.py
@@ -15,6 +15,7 @@
 FINE = 32
 CHUNK = 256
 BANDS = 4
+EDGES = 2
 FIELDS = 8
 MESH = pl.DeviceIdType.MESH
 
@@ -136,11 +137,12 @@
             scaled_own.at[g, jj, k], scaled_par.at[g, jj, k], par_sems, (g, jj, k), to_partner
         )
 
-    def last_edge():
-        return remote(edge_send, edge_got, last_sems, (0,), to_beyond)
+    def last_edge(band):
+        rows = slice(band * size // EDGES, (band + 1) * size // EDGES)
+        return remote(edge_send.at[rows], edge_got.at[rows], last_sems, (1 + band,), to_beyond)
 
     def last_inner():
-        return remote(inner_send, inner_got, last_sems, (1,), to_partner)
+        return remote(inner_send, inner_got, last_sems, (0,), to_partner)
 
     def no_edge():
         return pltpu.make_async_copy(edge_send, edge_got, local_sems.at[len(local)])
@@ -367,12 +369,8 @@
             result_ref[k, :, :block] = real.astype(result_ref.dtype)
             result_ref[k, :, block:] = turned.astype(result_ref.dtype)
 
-    def adjoint(d, j, scaled_ref, spread_ref):
+    def spread_out(d, j, scaled_ref, spread_ref):
         from_odd, slot, live = pointing(d, j)
-        rows = jnp.concatenate(
-            [flip_tab[bins(d, from_odd, slot, k, 0)] for k in range(slots_uv)], axis=1
-        )
-        gy = wide(gy_ref[d, j], CHUNK)
         for k in range(slots_uv):
             value = scaled_ref[k]
             real, turned = value[:, :block], value[:, block:]
@@ -380,13 +378,24 @@
                 [value, jnp.concatenate([turned, -real], axis=1)], axis=0
             )
             spread_ref[2 * k * block : (2 * k + 2) * block, :] = jnp.dot(
-                square, column_table(d, from_odd, slot, k), preferred_element_type=F32
+                square, col_tab[bins(d, from_odd, slot, k, 1)], preferred_element_type=F32
             ).astype(BF16)
+
+    def bring_back(d, j, spread_ref, start, stop):
+        from_odd, slot, live = pointing(d, j)
+        rows = jnp.concatenate(
+            [flip_tab[bins(d, from_odd, slot, k, 0), start:stop] for k in range(slots_uv)], axis=1
+        )
+        gy = wide(gy_ref[d, j, start:stop], CHUNK)
         for at in range(0, size, CHUNK):
             cols = slice(at, at + CHUNK)
             back = gy * jnp.dot(rows, spread_ref[:, cols], preferred_element_type=F32)
-            acc_outer[:, cols] += gx_ref[d, j, 0, 0:1, cols] * back
-            acc_inner[:, cols] += gx_ref[d, j, 1, 0:1, cols] * back
+            acc_outer[start:stop, cols] += gx_ref[d, j, 0, 0:1, cols] * back
+            acc_inner[start:stop, cols] += gx_ref[d, j, 1, 0:1, cols] * back
+
+    def adjoint(d, j, scaled_ref, spread_ref):
+        spread_out(d, j, scaled_ref, spread_ref)
+        bring_back(d, j, spread_ref, 0, size)
 
     mine, theirs = half_slots * core, half_slots * (1 - core)
 
@@ -500,7 +509,6 @@
         weights_far().wait_recv()
         with jax.named_scope("far"):
             lax.fori_loop(0, half_slots, far_step, 0)
-        adjoint_theirs(0)
 
     def own_step(jj, carry):
         for k in range(slots_uv):
@@ -512,12 +520,24 @@
     with jax.named_scope("own"):
         lax.fori_loop(0, half_slots, own_step, 0)
 
-    adjoint_theirs(2)
-
-    @pl.when(has_beyond)
+    @pl.when(has_far)
     def _():
-        edge_send[...] = acc_outer[...].astype(BF16)
-        last_edge().start()
+        adjoint_theirs(0)
+
+    with jax.named_scope("theirs2"):
+        for jj in range(half_slots):
+            for k in range(slots_uv):
+                par_copy(2, jj, k).wait_recv()
+            spread_out(1, theirs + jj, scaled_par.at[2, jj], spread[jj % 2])
+        for band in range(EDGES):
+            start, stop = band * size // EDGES, (band + 1) * size // EDGES
+            for jj in range(half_slots):
+                bring_back(1, theirs + jj, spread[jj % 2], start, stop)
+
+            @pl.when(has_beyond)
+            def _(band=band, start=start, stop=stop):
+                edge_send[start:stop] = acc_outer[start:stop].astype(BF16)
+                last_edge(band).start()
 
     inner_send[...] = acc_inner[...].astype(BF16)
     last_inner().start()
@@ -571,7 +591,8 @@
 
         @pl.when(has_beyond)
         def _():
-            last_edge().wait()
+            for band in range(EDGES):
+                last_edge(band).wait()
 
         @pl.when(jnp.logical_not(has_beyond))
         def _():
@@ -667,7 +688,7 @@
             dma((2, half_slots, slots_uv)),
             dma((2, half_slots, slots_uv)),
             dma((2, 3, half_slots, slots_uv)),
-            dma((2, 2)),
+            dma((2, 1 + EDGES)),
         ],
         compiler_params=pltpu.CompilerParams(
             vmem_limit_bytes=int(56 * 1024 * 1024), collective_id=0, has_side_effects=True

time: 42.8 us -> 42.4 us (level)
  Pallas kernels: 41.9 us -> 41.2 us
    pallas_call x1, Pallas kernels: 39.8 us -> 39.1 us  [shards(): pl.pallas_call(kernel, out_shape=(jax.ShapeDtypeStruct((size, size), BF16...]
where the time goes in v9:
time: 42.4 us; the launch traced here: 41.8 us
  Pallas kernels  41.2 us (97%)
  between operations  0.66 us (2%)
    pallas_call x1, Pallas kernels, shards(): pl.pallas_call(kernel, out_shape=(jax.ShapeDtypeStruct((size, size), BF16...  39.1 us
    pallas_call x1, Pallas kernels, shards(): pl.pallas_call(add_kernel, out_shape=jax.ShapeDtypeStruct((size, size), F...  2.12 us

profile of v9, /device:TPU:13, one launch (start us, length us, event | category | flops | bytes accessed | tf_op | source)
XLA Modules:
  0.0 41.8 jit_solution(1235617890145357495)
XLA Ops:
  0.7 39.1 %shard_map.82 = (bf16[512,512]{1,0:T(8,128)(2,1)}, bf16[512,512]{1,0:T(8,128)(2,1)}) custom-call(s32[1,1]{1,0:T(1,128)S(6)} %copy.9.count_in, s32[2,4]{1,0:T(2,128)} %bitcast.11, bf16[1,4]{1,0:T(2,128)(2,1)} %bitcast.12, s32[2,2,4]{2,1,0:T(2,128)} %bitcast.10, s32[1,4]{1,0:T(1,128)} %bitcast.13, f32[2,64,1024]{2,1,0:T(8,128)} %constant.2.clone.seeds_in, ...), custom_call_target="tpu_custom_call" | custom-call | tf_op jit(solution)/shard_map/pallas_call | solution.py:645
  39.7 2.1 %shard_map.83 = f32[512,512]{1,0:T(8,128)} custom-call(bf16[512,512]{1,0:T(8,128)(2,1)} %get-tuple-element.7.inner_hbm, bf16[512,512]{1,0:T(8,128)(2,1)} %get-tuple-element.8.edge_hbm), custom_call_target="tpu_custom_call" | custom-call | flops 262144 | bytes 2621440 | tf_op jit(solution)/shard_map/pallas_call | solution.py:697

commit v10 on v9

--- a/solution.py
+++ b/solution.py
@@ -36,7 +36,7 @@
     count_in, offset_in, width_in, bins_in, used_in, seeds_in, sky_in, weight_in,
     inner_got, edge_got,
     meta_ref, meta_got, meta_all, sky_ref, outer_ref, inner_ref, weight_ref, weight_got,
-    seeds_ref, row_tab, flip_tab, col_tab,
+    seeds_ref, row_tab, flip_tab, col_tab, turn_tab,
     beamed, first, spread, gx_ref, gy_ref, gx_half, gy_half,
     part_send, part_got, totals, raw_send, raw_got, own_send, own_got,
     sum_send, sum_got, back_send, back_got, weights, scaled_own, scaled_par, acc_outer, acc_inner, edge_send, inner_send,
@@ -231,14 +231,15 @@
         lax.fori_loop(0, length // FINE, table, 0)
 
     def flipped(j, carry):
-        row = (ty % 2) * (size // FINE) + j
-        c, s = seeds_ref[0, pl.ds(FINE + row, 1), :], seeds_ref[1, pl.ds(FINE + row, 1), :]
-        fc, fs = seeds_ref[0, :FINE, :], seeds_ref[1, :FINE, :]
         at = pl.ds(pl.multiple_of(j * FINE, FINE), FINE)
-        cos, sin = (fc * c - fs * s).astype(BF16), (fs * c + fc * s).astype(BF16)
-        for blk in range(length // block):
-            flip_tab[blk, at, :block] = cos[:, blk * block : (blk + 1) * block]
-            flip_tab[blk, at, block:] = sin[:, blk * block : (blk + 1) * block]
+        for tab, parity in ((flip_tab, odd_row), (turn_tab, 1 - core)):
+            row = parity * (size // FINE) + j
+            c, s = seeds_ref[0, pl.ds(FINE + row, 1), :], seeds_ref[1, pl.ds(FINE + row, 1), :]
+            fc, fs = seeds_ref[0, :FINE, :], seeds_ref[1, :FINE, :]
+            cos, sin = (fc * c - fs * s).astype(BF16), (fs * c + fc * s).astype(BF16)
+            for blk in range(length // block):
+                tab[blk, at, :block] = cos[:, blk * block : (blk + 1) * block]
+                tab[blk, at, block:] = sin[:, blk * block : (blk + 1) * block]
         return carry
 
     with jax.named_scope("flips"):
@@ -347,7 +348,7 @@
             value = gx[0] * outer_ref[:, cols] + gx[1] * inner_ref[:, cols]
             beamed_ref[:, cols] = gy * value
 
-    def multiply(d, j, beamed_ref, first_ref, result_ref):
+    def transform_rows(d, j, beamed_ref, first_ref):
         from_odd, slot, live = pointing(d, j)
         rows = jnp.concatenate(
             [row_tab[bins(d, from_odd, slot, k, 0)] for k in range(slots_uv)], axis=0
@@ -357,11 +358,13 @@
             first_ref[:, cols] = jnp.dot(
                 rows, beamed_ref[:, cols], preferred_element_type=F32
             ).astype(BF16)
-        for k in range(slots_uv):
-            both = lax.dot_general(
+
+    def transform_columns(d, j, first_ref, result_ref):
+        from_odd, slot, live = pointing(d, j)
+        for k in range(slots_uv):
+            both = jnp.dot(
                 first_ref[2 * k * block : (2 * k + 2) * block, :],
-                col_tab[bins(d, from_odd, slot, k, 1)],
-                (((1,), (1,)), ((), ())),
+                turn_tab[bins(d, from_odd, slot, k, 1)],
                 preferred_element_type=F32,
             )
             real = both[:block, :block] - both[block:, block:]
@@ -393,10 +396,6 @@
             acc_outer[start:stop, cols] += gx_ref[d, j, 0, 0:1, cols] * back
             acc_inner[start:stop, cols] += gx_ref[d, j, 1, 0:1, cols] * back
 
-    def adjoint(d, j, scaled_ref, spread_ref):
-        spread_out(d, j, scaled_ref, spread_ref)
-        bring_back(d, j, spread_ref, 0, size)
-
     mine, theirs = half_slots * core, half_slots * (1 - core)
 
     with jax.named_scope("sky"):
@@ -445,14 +444,19 @@
             (2 * (1 - end) * (1 - far) + end, slot),
             ((1 - end) * (1 + far) + end, slot + end),
         )
-        for i, (g, jj) in enumerate(units):
-            prepare(row_of(g), theirs + jj, beamed[i])
-            multiply(row_of(g), theirs + jj, beamed[i], first[i], part_send.at[g, jj])
-            part_copy(g, jj).start()
-        for i, (g, jj) in enumerate(units):
-            prepare(row_of(g), mine + jj, beamed[i])
-            multiply(row_of(g), mine + jj, beamed[i], first[i], totals.at[g, jj])
-            settle(g, jj)
+        for base in (theirs, mine):
+            for i, (g, jj) in enumerate(units):
+                prepare(row_of(g), base + jj, beamed[i])
+            for i, (g, jj) in enumerate(units):
+                transform_rows(row_of(g), base + jj, beamed[i], first[i])
+            for i, (g, jj) in enumerate(units):
+                result = part_send.at[g, jj] if base is theirs else totals.at[g, jj]
+                transform_columns(row_of(g), base + jj, first[i], result)
+            for g, jj in units:
+                if base is theirs:
+                    part_copy(g, jj).start()
+                else:
+                    settle(g, jj)
         return carry
 
     with jax.named_scope("forward"):
@@ -463,76 +467,87 @@
         scaled_own[g, jj, k] = (total * wide(weight, 2 * block)).astype(BF16)
         par_copy(g, jj, k).start()
 
-    def adjoint_mine(g, jj):
-        adjoint(row_of(g), mine + jj, scaled_own.at[g, jj], spread[0])
+    def adjoint_all(g, base, scaled_ref):
+        for jj in range(half_slots):
+            spread_out(row_of(g), base + jj, scaled_ref.at[g, jj], spread[jj])
+        for jj in range(half_slots):
+            bring_back(row_of(g), base + jj, spread[jj], 0, size)
+
+    def adjoint_one(g, base, jj, scaled_ref):
+        spread_out(row_of(g), base + jj, scaled_ref.at[g, jj], spread[0])
+        bring_back(row_of(g), base + jj, spread[0], 0, size)
 
     def adjoint_theirs(g):
         with jax.named_scope(f"theirs{g}"):
             for jj in range(half_slots):
                 for k in range(slots_uv):
                     par_copy(g, jj, k).wait_recv()
-            for jj in range(half_slots):
-                adjoint(row_of(g), theirs + jj, scaled_par.at[g, jj], spread[jj % 2])
+            adjoint_all(g, theirs, scaled_par)
+
+    def mate_slot(jj, carry):
+        for k in range(slots_uv):
+            own_copy(jj, k).wait_recv()
+            own_part = own_got[jj, k].astype(F32)
+
+            @pl.when(has_fed)
+            def _(k=k):
+                back_send[jj, k] = (totals[1, jj, k] + own_got[jj, k].astype(F32)).astype(BF16)
+                back_copy(to_fed, jj, k).start()
+                raw_copy(to_fed, jj, k).wait_recv()
+                both = totals[1, jj, k] + raw_got[jj, k].astype(F32)
+                pass_sum(jj, k, both)
+                totals[1, jj, k] = both
+
+            scale(1, jj, k, totals[1, jj, k] + own_part)
+        adjoint_one(1, mine, jj, scaled_own)
+        return carry
 
     with jax.named_scope("mate"):
         weights_mate().wait_recv()
-        for jj in range(half_slots):
-            for k in range(slots_uv):
-                own_copy(jj, k).wait_recv()
-                both = totals[1, jj, k] + own_got[jj, k].astype(F32)
-
-                @pl.when(has_fed)
-                def _(jj=jj, k=k, both=both):
-                    back_send[jj, k] = both.astype(BF16)
-                    back_copy(to_fed, jj, k).start()
-                    raw_copy(to_fed, jj, k).wait_recv()
-                    far_part = raw_got[jj, k].astype(F32)
-                    pass_sum(jj, k, totals[1, jj, k] + far_part)
-                    totals[1, jj, k] = totals[1, jj, k] + far_part
-
-                scale(1, jj, k, totals[1, jj, k] + own_got[jj, k].astype(F32))
-
-        for jj in range(half_slots):
-            adjoint_mine(1, jj)
+        lax.fori_loop(0, half_slots, mate_slot, 0)
 
     adjoint_theirs(1)
 
-    def far_step(jj, carry):
+    def far_slot(jj, carry):
         for k in range(slots_uv):
             back_copy(to_giving, jj, k).wait_recv()
             scale(0, jj, k, totals[0, jj, k] + back_got[jj, k].astype(F32))
-        adjoint_mine(0, jj)
+        adjoint_one(0, mine, jj, scaled_own)
         return carry
 
     @pl.when(has_far)
     def _():
-        weights_far().wait_recv()
         with jax.named_scope("far"):
-            lax.fori_loop(0, half_slots, far_step, 0)
-
-    def own_step(jj, carry):
-        for k in range(slots_uv):
-            sum_copy(jj, k).wait_recv()
-            scale(2, jj, k, totals[2, jj, k] + sum_got[jj, k].astype(F32))
-        adjoint_mine(2, jj)
-        return carry
-
-    with jax.named_scope("own"):
-        lax.fori_loop(0, half_slots, own_step, 0)
+            weights_far().wait_recv()
+            lax.fori_loop(0, half_slots, far_slot, 0)
+
+    def own_slot(jj):
+        with jax.named_scope(f"own{jj}"):
+            for k in range(slots_uv):
+                sum_copy(jj, k).wait_recv()
+                scale(2, jj, k, totals[2, jj, k] + sum_got[jj, k].astype(F32))
+            adjoint_one(2, mine, jj, scaled_own)
+
+    own_slot(0)
 
     @pl.when(has_far)
     def _():
         adjoint_theirs(0)
 
-    with jax.named_scope("theirs2"):
-        for jj in range(half_slots):
-            for k in range(slots_uv):
-                par_copy(2, jj, k).wait_recv()
-            spread_out(1, theirs + jj, scaled_par.at[2, jj], spread[jj % 2])
+    for jj in range(half_slots - 1):
+        for k in range(slots_uv):
+            par_copy(2, jj, k).wait_recv()
+        adjoint_one(2, theirs, jj, scaled_par)
+        own_slot(jj + 1)
+
+    with jax.named_scope("final"):
+        jj = half_slots - 1
+        for k in range(slots_uv):
+            par_copy(2, jj, k).wait_recv()
+        spread_out(1, theirs + jj, scaled_par.at[2, jj], spread[0])
         for band in range(EDGES):
             start, stop = band * size // EDGES, (band + 1) * size // EDGES
-            for jj in range(half_slots):
-                bring_back(1, theirs + jj, spread[jj % 2], start, stop)
+            bring_back(1, theirs + jj, spread[0], start, stop)
 
             @pl.when(has_beyond)
             def _(band=band, start=start, stop=stop):
@@ -660,9 +675,10 @@
             pltpu.VMEM((length // block, 2 * block, size), BF16),
             pltpu.VMEM((length // block, size, 2 * block), BF16),
             pltpu.VMEM((length // block, 2 * block, size), BF16),
+            pltpu.VMEM((length // block, size, 2 * block), BF16),
             (tile, tile),
             (pltpu.VMEM((depth, size), BF16),) * 2,
-            (pltpu.VMEM((depth, size), BF16),) * 2,
+            (pltpu.VMEM((depth, size), BF16),) * half_slots,
             pltpu.VMEM((3, slots, 2, 8, size), F32),
             pltpu.VMEM((3, slots, size, 128), F32),
             pltpu.VMEM((3, slots, 2, 16, size), BF16),

time: 42.4 us -> 41.9 us (0.988)
  no operation moved by 1% of the time
where the time goes in v10:
time: 41.9 us; the launch traced here: 41.7 us
  Pallas kernels  41.1 us (98%)
  between operations  0.66 us (2%)
    pallas_call x1, Pallas kernels, shards(): pl.pallas_call(kernel, out_shape=(jax.ShapeDtypeStruct((size, size), BF16...  38.9 us
    pallas_call x1, Pallas kernels, shards(): pl.pallas_call(add_kernel, out_shape=jax.ShapeDtypeStruct((size, size), F...  2.12 us

profile of v10, /device:TPU:13, one launch (start us, length us, event | category | flops | bytes accessed | tf_op | source)
XLA Modules:
  0.0 41.7 jit_solution(7152428638797999084)
XLA Ops:
  0.7 38.9 %shard_map.82 = (bf16[512,512]{1,0:T(8,128)(2,1)}, bf16[512,512]{1,0:T(8,128)(2,1)}) custom-call(s32[1,1]{1,0:T(1,128)S(6)} %copy.9.count_in, s32[2,4]{1,0:T(2,128)} %bitcast.11, bf16[1,4]{1,0:T(2,128)(2,1)} %bitcast.12, s32[2,2,4]{2,1,0:T(2,128)} %bitcast.10, s32[1,4]{1,0:T(1,128)} %bitcast.13, f32[2,64,1024]{2,1,0:T(8,128)} %constant.2.clone.seeds_in, ...), custom_call_target="tpu_custom_call" | custom-call | tf_op jit(solution)/shard_map/pallas_call | solution.py:660
  39.6 2.1 %shard_map.83 = f32[512,512]{1,0:T(8,128)} custom-call(bf16[512,512]{1,0:T(8,128)(2,1)} %get-tuple-element.7.inner_hbm, bf16[512,512]{1,0:T(8,128)(2,1)} %get-tuple-element.8.edge_hbm), custom_call_target="tpu_custom_call" | custom-call | flops 262144 | bytes 2621440 | tf_op jit(solution)/shard_map/pallas_call | solution.py:713

commit v11 on v10

--- a/solution.py
+++ b/solution.py
@@ -33,8 +33,9 @@
 
 
 def kernel(
-    count_in, offset_in, width_in, bins_in, used_in, seeds_in, sky_in, weight_in,
+    count_hbm, offset_hbm, width_hbm, bins_hbm, used_hbm, seeds_in, sky_in, weight_in,
     inner_got, edge_got,
+    count_in, offset_in, width_in, bins_in, used_in,
     meta_ref, meta_got, meta_all, sky_ref, outer_ref, inner_ref, weight_ref, weight_got,
     seeds_ref, row_tab, flip_tab, col_tab, turn_tab,
     beamed, first, spread, gx_ref, gy_ref, gx_half, gy_half,
@@ -74,6 +75,11 @@
         for i, (source, target) in enumerate(
             (
                 (sky_in, sky_ref),
+                (count_hbm, count_in),
+                (offset_hbm, offset_in),
+                (width_hbm, width_in),
+                (bins_hbm, bins_in),
+                (used_hbm, used_in),
                 (seeds_in, seeds_ref),
                 (weight_in, weight_ref),
             )
@@ -170,6 +176,9 @@
     for copy in local:
         copy.start()
 
+    for copy in local[1:6]:
+        copy.wait()
+
     lane = lax.broadcasted_iota(I32, (1, slots), 1)
     widths = width_in[...].astype(F32)
     meta_ref[slots, 0] = count_in[0, 0]
@@ -208,7 +217,7 @@
             for copy in meta_send(side):
                 copy.start()
 
-    for copy in local[1:]:
+    for copy in local[6:]:
         copy.wait()
     weight_copy().start()
 
@@ -656,13 +665,18 @@
     tile = pltpu.VMEM((size, size), BF16)
     plane = pltpu.VMEM((size, size), F32)
     patch = (slots_uv, block, 2 * block)
-    smem, anywhere = pl.BlockSpec(memory_space=pltpu.SMEM), pl.BlockSpec(memory_space=pl.ANY)
+    anywhere = pl.BlockSpec(memory_space=pl.ANY)
     inner, edge = pl.pallas_call(
         kernel,
         out_shape=(jax.ShapeDtypeStruct((size, size), BF16),) * 2,
-        in_specs=[smem, smem, pl.BlockSpec(memory_space=pltpu.VMEM), smem, smem] + [anywhere] * 3,
+        in_specs=[anywhere] * 8,
         out_specs=(anywhere, anywhere),
         scratch_shapes=[
+            pltpu.SMEM(count.shape, I32),
+            pltpu.SMEM(offset.shape, I32),
+            pltpu.VMEM(width.shape, BF16),
+            pltpu.SMEM(bins.shape, I32),
+            pltpu.SMEM(used.shape, I32),
             pltpu.SMEM(meta_shape, I32),
             tuple([pltpu.SMEM(meta_shape, I32)] * 5),
             pltpu.SMEM((3, 2) + meta_shape, I32),
@@ -694,7 +708,7 @@
             plane,
             tile,
             tile,
-            dma((4,)),
+            dma((9,)),
             dma((2, 5)),
             dma((2, 2)),
             dma((2, 3)),

time: 41.9 us -> 41.1 us (0.981)
  Pallas kernels: 41.1 us -> 40.3 us
    pallas_call x1, Pallas kernels: 38.9 us -> 38.2 us  [shards(): pl.pallas_call(kernel, out_shape=(jax.ShapeDtypeStruct((size, size), BF16...]
where the time goes in v11:
time: 41.1 us; the launch traced here: 41 us
  Pallas kernels  40.3 us (98%)
  between operations  0.66 us (2%)
    pallas_call x1, Pallas kernels, shards(): pl.pallas_call(kernel, out_shape=(jax.ShapeDtypeStruct((size, size), BF16...  38.2 us
    pallas_call x1, Pallas kernels, shards(): pl.pallas_call(add_kernel, out_shape=jax.ShapeDtypeStruct((size, size), F...  2.12 us

profile of v11, /device:TPU:13, one launch (start us, length us, event | category | flops | bytes accessed | tf_op | source)
XLA Modules:
  0.0 41.0 jit_solution(12006676462814146406)
XLA Ops:
  0.7 38.2 %shard_map.82 = (bf16[512,512]{1,0:T(8,128)(2,1)}, bf16[512,512]{1,0:T(8,128)(2,1)}) custom-call(s32[1,1]{1,0:T(1,128)S(6)} %copy.9.count_hbm, s32[2,4]{1,0:T(2,128)} %bitcast.11, bf16[1,4]{1,0:T(2,128)(2,1)} %bitcast.12, s32[2,2,4]{2,1,0:T(2,128)} %bitcast.10, s32[1,4]{1,0:T(1,128)} %bitcast.13, f32[2,64,1024]{2,1,0:T(8,128)} %constant.2.clone.seeds_in, ...), custom_call_target="tpu_custom_call" | custom-call | tf_op jit(solution)/shard_map/pallas_call | solution.py:669
  38.8 2.1 %shard_map.83 = f32[512,512]{1,0:T(8,128)} custom-call(bf16[512,512]{1,0:T(8,128)(2,1)} %get-tuple-element.7.inner_hbm, bf16[512,512]{1,0:T(8,128)(2,1)} %get-tuple-element.8.edge_hbm), custom_call_target="tpu_custom_call" | custom-call | flops 262144 | bytes 2621440 | tf_op jit(solution)/shard_map/pallas_call | solution.py:727

commit v12 on v11

--- a/solution.py
+++ b/solution.py
@@ -13,7 +13,7 @@
 BF16 = jnp.bfloat16
 I32 = jnp.int32
 FINE = 32
-CHUNK = 256
+CHUNK = 512
 BANDS = 4
 EDGES = 2
 FIELDS = 8
@@ -543,11 +543,22 @@
     def _():
         adjoint_theirs(0)
 
-    for jj in range(half_slots - 1):
+    def own_theirs(jj):
         for k in range(slots_uv):
             par_copy(2, jj, k).wait_recv()
         adjoint_one(2, theirs, jj, scaled_par)
+
+    for jj in range(half_slots - 1):
+
+        @pl.when(jnp.logical_not(has_far))
+        def _(jj=jj):
+            own_theirs(jj)
+
         own_slot(jj + 1)
+
+        @pl.when(has_far)
+        def _(jj=jj):
+            own_theirs(jj)
 
     with jax.named_scope("final"):
         jj = half_slots - 1

time: 41.1 us -> 41 us (level)
    pallas_call x1, Pallas kernels: 38.2 us -> 37.8 us  [shards(): pl.pallas_call(kernel, out_shape=(jax.ShapeDtypeStruct((size, size), BF16...]
where the time goes in v12:
time: 41 us; the launch traced here: 40.5 us
  Pallas kernels  39.9 us (97%)
  between operations  0.66 us (2%)
    pallas_call x1, Pallas kernels, shards(): pl.pallas_call(kernel, out_shape=(jax.ShapeDtypeStruct((size, size), BF16...  37.8 us
    pallas_call x1, Pallas kernels, shards(): pl.pallas_call(add_kernel, out_shape=jax.ShapeDtypeStruct((size, size), F...  2.12 us

profile of v12, /device:TPU:13, one launch (start us, length us, event | category | flops | bytes accessed | tf_op | source)
XLA Modules:
  0.0 40.5 jit_solution(1427582950481953029)
XLA Ops:
  0.7 37.8 %shard_map.82 = (bf16[512,512]{1,0:T(8,128)(2,1)}, bf16[512,512]{1,0:T(8,128)(2,1)}) custom-call(s32[1,1]{1,0:T(1,128)S(6)} %copy.9.count_hbm, s32[2,4]{1,0:T(2,128)} %bitcast.11, bf16[1,4]{1,0:T(2,128)(2,1)} %bitcast.12, s32[2,2,4]{2,1,0:T(2,128)} %bitcast.10, s32[1,4]{1,0:T(1,128)} %bitcast.13, f32[2,64,1024]{2,1,0:T(8,128)} %constant.2.clone.seeds_in, ...), custom_call_target="tpu_custom_call" | custom-call | tf_op jit(solution)/shard_map/pallas_call | solution.py:680
  38.4 2.1 %shard_map.83 = f32[512,512]{1,0:T(8,128)} custom-call(bf16[512,512]{1,0:T(8,128)(2,1)} %get-tuple-element.7.inner_hbm, bf16[512,512]{1,0:T(8,128)(2,1)} %get-tuple-element.8.edge_hbm), custom_call_target="tpu_custom_call" | custom-call | flops 262144 | bytes 2621440 | tf_op jit(solution)/shard_map/pallas_call | solution.py:738

commit v13 on v12

--- a/solution.py
+++ b/solution.py
@@ -515,8 +515,6 @@
         weights_mate().wait_recv()
         lax.fori_loop(0, half_slots, mate_slot, 0)
 
-    adjoint_theirs(1)
-
     def far_slot(jj, carry):
         for k in range(slots_uv):
             back_copy(to_giving, jj, k).wait_recv()
@@ -526,9 +524,21 @@
 
     @pl.when(has_far)
     def _():
-        with jax.named_scope("far"):
-            weights_far().wait_recv()
-            lax.fori_loop(0, half_slots, far_slot, 0)
+        weights_far().wait_recv()
+
+    def mate_theirs(jj, carry):
+        for k in range(slots_uv):
+            par_copy(1, jj, k).wait_recv()
+        adjoint_one(1, theirs, jj, scaled_par)
+
+        @pl.when(has_far)
+        def _():
+            far_slot(jj, 0)
+
+        return carry
+
+    with jax.named_scope("far"):
+        lax.fori_loop(0, half_slots, mate_theirs, 0)
 
     def own_slot(jj):
         with jax.named_scope(f"own{jj}"):

time: 41 us -> 41 us (level)
  no operation moved by 1% of the time
where the time goes in v13:
time: 41 us; the launch traced here: 40.7 us
  Pallas kernels  40.1 us (98%)
  between operations  0.66 us (2%)
    pallas_call x1, Pallas kernels, shards(): pl.pallas_call(kernel, out_shape=(jax.ShapeDtypeStruct((size, size), BF16...  38 us
    pallas_call x1, Pallas kernels, shards(): pl.pallas_call(add_kernel, out_shape=jax.ShapeDtypeStruct((size, size), F...  2.12 us

profile of v13, /device:TPU:13, one launch (start us, length us, event | category | flops | bytes accessed | tf_op | source)
XLA Modules:
  0.0 40.7 jit_solution(9284272544686973667)
XLA Ops:
  0.7 38.0 %shard_map.82 = (bf16[512,512]{1,0:T(8,128)(2,1)}, bf16[512,512]{1,0:T(8,128)(2,1)}) custom-call(s32[1,1]{1,0:T(1,128)S(6)} %copy.9.count_hbm, s32[2,4]{1,0:T(2,128)} %bitcast.11, bf16[1,4]{1,0:T(2,128)(2,1)} %bitcast.12, s32[2,2,4]{2,1,0:T(2,128)} %bitcast.10, s32[1,4]{1,0:T(1,128)} %bitcast.13, f32[2,64,1024]{2,1,0:T(8,128)} %constant.2.clone.seeds_in, ...), custom_call_target="tpu_custom_call" | custom-call | tf_op jit(solution)/shard_map/pallas_call | solution.py:690
  38.6 2.1 %shard_map.83 = f32[512,512]{1,0:T(8,128)} custom-call(bf16[512,512]{1,0:T(8,128)(2,1)} %get-tuple-element.7.inner_hbm, bf16[512,512]{1,0:T(8,128)(2,1)} %get-tuple-element.8.edge_hbm), custom_call_target="tpu_custom_call" | custom-call | flops 262144 | bytes 2621440 | tf_op jit(solution)/shard_map/pallas_call | solution.py:748

commit v14 on v12

--- a/solution.py
+++ b/solution.py
@@ -15,7 +15,7 @@
 FINE = 32
 CHUNK = 512
 BANDS = 4
-EDGES = 2
+EDGES = 4
 FIELDS = 8
 MESH = pl.DeviceIdType.MESH
 

time: 41 us -> 41 us (level)
  no operation moved by 1% of the time
where the time goes in v14:
time: 41 us; the launch traced here: 40.5 us
  Pallas kernels  39.9 us (97%)
  between operations  0.66 us (2%)
    pallas_call x1, Pallas kernels, shards(): pl.pallas_call(kernel, out_shape=(jax.ShapeDtypeStruct((size, size), BF16...  37.7 us
    pallas_call x1, Pallas kernels, shards(): pl.pallas_call(add_kernel, out_shape=jax.ShapeDtypeStruct((size, size), F...  2.12 us

profile of v14, /device:TPU:13, one launch (start us, length us, event | category | flops | bytes accessed | tf_op | source)
XLA Modules:
  0.0 40.5 jit_solution(171962935429746787)
XLA Ops:
  0.7 37.7 %shard_map.82 = (bf16[512,512]{1,0:T(8,128)(2,1)}, bf16[512,512]{1,0:T(8,128)(2,1)}) custom-call(s32[1,1]{1,0:T(1,128)S(6)} %copy.9.count_hbm, s32[2,4]{1,0:T(2,128)} %bitcast.11, bf16[1,4]{1,0:T(2,128)(2,1)} %bitcast.12, s32[2,2,4]{2,1,0:T(2,128)} %bitcast.10, s32[1,4]{1,0:T(1,128)} %bitcast.13, f32[2,64,1024]{2,1,0:T(8,128)} %constant.2.clone.seeds_in, ...), custom_call_target="tpu_custom_call" | custom-call | tf_op jit(solution)/shard_map/pallas_call | solution.py:680
  38.4 2.1 %shard_map.83 = f32[512,512]{1,0:T(8,128)} custom-call(bf16[512,512]{1,0:T(8,128)(2,1)} %get-tuple-element.7.inner_hbm, bf16[512,512]{1,0:T(8,128)(2,1)} %get-tuple-element.8.edge_hbm), custom_call_target="tpu_custom_call" | custom-call | flops 262144 | bytes 2621440 | tf_op jit(solution)/shard_map/pallas_call | solution.py:738
